TPU v7x, 32 devices: a whole 2x2x4 slice. The times are simulated.
32 devices in a mesh: dp: 16 (over z, y, x), tensor: 2 (over core).
Axes of the slice: x: 2, y: 2, z: 4, core: 2. Of those that a mesh axis runs over, the one named last changes fastest.
Arguments:
- stream_in: bfloat16 [16384, 1024], P(('dp', 'tensor'))
- grad_out: bfloat16 [16384, 1024], P(('dp', 'tensor')), may hold values from -6 to 6
- clip_lengths: int32 [16], P('dp'), may hold values from 512 to 1024, as said below
- first_up: bfloat16 [1024, 4096], P('dp', 'tensor'), may hold values from -0.1875 to 0.1875
- first_down: bfloat16 [4096, 1024], P('tensor', 'dp'), may hold values from -0.1875 to 0.1875
- attn_proj: bfloat16 [3, 1024, 1024], P(None, 'dp', 'tensor'), may hold values from -0.1875 to 0.1875
- attn_out: bfloat16 [1024, 1024], P('tensor', 'dp'), may hold values from -1.5 to 1.5
- rel_table: bfloat16 [73, 64], replicated, may hold values from -6 to 6
- glu_weight: bfloat16 [2, 1024, 1024], P(None, 'dp', 'tensor'), may hold values from -0.1875 to 0.1875
- conv_taps: float32 [31, 1024], replicated, may hold values from -1.8 to 1.8
- conv_out: bfloat16 [1024, 1024], P('tensor', 'dp'), may hold values from -0.375 to 0.375
- second_up: bfloat16 [1024, 4096], P('dp', 'tensor'), may hold values from -0.1875 to 0.1875
- second_down: bfloat16 [4096, 1024], P('tensor', 'dp'), may hold values from -0.1875 to 0.1875
- norm_gains: float32 [6, 1024], replicated, may hold values from 0.1 to 1.9
- norm_shifts: float32 [6, 1024], replicated, may hold values from -1.8 to 1.8
Outputs:
- output: bfloat16 [16384, 1024], P(('dp', 'tensor'))
- grad_in: float32 [16384, 1024], P(('dp', 'tensor'))
- grad_first_up: float32 [1024, 4096], P('dp', 'tensor')
- grad_first_down: float32 [4096, 1024], P('tensor', 'dp')
- grad_attn_proj: float32 [3, 1024, 1024], P(None, 'dp', 'tensor')
- grad_attn_out: float32 [1024, 1024], P('tensor', 'dp')
- grad_rel_table: float32 [73, 64], replicated
- grad_glu_weight: float32 [2, 1024, 1024], P(None, 'dp', 'tensor')
- grad_conv_taps: float32 [31, 1024], replicated
- grad_conv_out: float32 [1024, 1024], P('tensor', 'dp')
- grad_second_up: float32 [1024, 4096], P('dp', 'tensor')
- grad_second_down: float32 [4096, 1024], P('tensor', 'dp')
- grad_norm_gains: float32 [6, 1024], replicated
- grad_norm_shifts: float32 [6, 1024], replicated
- rms_values: float32 [5], replicated
Inputs may be any that keep to these rules, and one draw needn't show every extreme that they name: `clip_lengths`: keys at or past a clip's length are excluded; some clip is full in every draw.
All inputs are finite; a program needn't handle non-finite values.
Results may differ from a plain program's by a relative error of at most 0.025.
Values may be sent and summed in bfloat16 or wider, within the bound.
A program may use at most 256 MiB of HBM per device.

v0:
```python
import jax
import jax.numpy as jnp
from jax import lax
from jax.sharding import PartitionSpec as P

D = 1024
HEAD = 64
KERNEL = 31
LEFT = 64
RIGHT = 8
L = 1024
CLIPS = 1


EPSILON = 1e-05
MASKED = -1e30


def matmul(first_op, second_op):
    return jnp.dot(first_op, second_op, preferred_element_type=jnp.float32)


def matmul_tn(first_op, second_op):
    return lax.dot_general(
        first_op, second_op, (((0,), (0,)), ((), ())), preferred_element_type=jnp.float32
    )


def matmul_nt(first_op, second_op):
    return lax.dot_general(
        first_op, second_op, (((1,), (1,)), ((), ())), preferred_element_type=jnp.float32
    )


def norm_forward(stream, gain_row, shift_row):
    centered = stream - jnp.mean(stream, axis=-1, keepdims=True)
    inv_std = lax.rsqrt(jnp.mean(centered * centered, axis=-1, keepdims=True) + EPSILON)
    normed = centered * inv_std
    return (normed * gain_row + shift_row, normed, inv_std)


def norm_backward(grad_result, normed, inv_std, gain_row):
    grad_normed = grad_result * gain_row
    return inv_std * (
        grad_normed
        - jnp.mean(grad_normed, axis=-1, keepdims=True)
        - normed * jnp.mean(grad_normed * normed, axis=-1, keepdims=True)
    )


def ffn_forward(entered, weight_in, weight_out):
    before = matmul(entered, weight_in)
    active = jax.nn.silu(before).astype(jnp.bfloat16)
    return (matmul(active, weight_out), before)


def ffn_backward(entered, before, grad_low, weight_in, weight_out):
    active = jax.nn.silu(before).astype(jnp.bfloat16)
    sigma = jax.nn.sigmoid(before)
    grad_active = matmul_nt(grad_low, weight_out)
    grad_before = (grad_active * sigma * (1.0 + before * (1.0 - sigma))).astype(jnp.bfloat16)
    partial_value = matmul_nt(grad_before, weight_in)
    return (partial_value, matmul_tn(entered, grad_before), matmul_tn(active, grad_low))


def bucket_picks(first_row, block_rows, key_count):
    spots = lax.iota(jnp.int32, key_count + block_rows)
    return jnp.clip(spots - block_rows - first_row, -LEFT, RIGHT) + LEFT


def block_scores(query_blk, key_clip, rel_table, first_row, length):
    direct = jnp.einsum("bhd,khd->hbk", query_blk, key_clip, preferred_element_type=jnp.float32)
    toward = jnp.einsum("bhd,nd->hbn", query_blk, rel_table, preferred_element_type=jnp.float32)
    local_heads, block_rows, key_count = direct.shape
    width = key_count + block_rows
    spread = jnp.take(toward, bucket_picks(first_row, block_rows, key_count), axis=2)
    flat = spread.reshape(local_heads, block_rows * width)
    sliced = lax.slice_in_dim(flat, block_rows, block_rows + block_rows * (width - 1), axis=1)
    relative = sliced.reshape(local_heads, block_rows, width - 1)[:, :, :key_count]
    col_ids = lax.iota(jnp.int32, key_count)
    scores = (direct + relative) * HEAD ** (-0.5)
    return jnp.where((col_ids < length)[None, None, :], scores, MASKED)


def bucket_sums(grad_scores, first_row):
    local_heads, block_rows, key_count = grad_scores.shape
    width = key_count + block_rows
    padded = jnp.pad(grad_scores, ((0, 0), (0, 0), (0, width - 1 - key_count)))
    flat = jnp.pad(padded.reshape(local_heads, block_rows * (width - 1)), ((0, 0), (block_rows, 0)))
    spread = flat.reshape(local_heads, block_rows, width)
    picks = bucket_picks(first_row, block_rows, key_count)
    selector = (picks[:, None] == lax.iota(jnp.int32, LEFT + RIGHT + 1)[None, :]).astype(
        jnp.bfloat16
    )
    return jnp.einsum("hbw,wn->hbn", spread, selector, preferred_element_type=jnp.float32)


def attention_forward(entered, proj_full, out_full, rel_table, clip_lengths):
    group_rows = entered.shape[0]
    head_cols = proj_full.shape[2]
    local_heads = head_cols // HEAD
    block_rows = min(512, L)
    block_count = L // block_rows
    queries = matmul(entered, proj_full[0]).astype(jnp.bfloat16)
    key_rows = matmul(entered, proj_full[1]).astype(jnp.bfloat16)
    value_rows = matmul(entered, proj_full[2]).astype(jnp.bfloat16)

    def by_clip(array):
        return array.reshape(CLIPS, L, local_heads, HEAD)

    def one_clip(clip_item):
        query_clip, key_clip, value_clip, length = clip_item

        def one_block(blk_index):
            query_blk = lax.dynamic_slice_in_dim(query_clip, blk_index * block_rows, block_rows, 0)
            scores = block_scores(query_blk, key_clip, rel_table, blk_index * block_rows, length)
            row_peak = jnp.max(scores, axis=-1, keepdims=True)
            exponent = jnp.exp(scores - row_peak)
            row_total = jnp.sum(exponent, axis=-1, keepdims=True)
            attn_probs = (exponent / row_total).astype(jnp.bfloat16)
            attended = jnp.einsum(
                "hbk,khd->bhd", attn_probs, value_clip, preferred_element_type=jnp.float32
            )
            return (attended, (row_peak + jnp.log(row_total))[..., 0])

        return lax.map(one_block, jnp.arange(block_count, dtype=jnp.int32))

    attended, log_totals = lax.map(
        one_clip, (by_clip(queries), by_clip(key_rows), by_clip(value_rows), clip_lengths)
    )
    attended = attended.reshape(group_rows, head_cols).astype(jnp.bfloat16)
    return (matmul(attended, out_full), (queries, key_rows, value_rows, attended, log_totals))


def attention_backward(entered, saved, grad_low, proj_full, out_full, rel_table, clip_lengths):
    queries, key_rows, value_rows, attended, log_totals = saved
    group_rows, head_cols = queries.shape
    local_heads = head_cols // HEAD
    block_rows = min(512, L)
    block_count = L // block_rows
    score_scale = HEAD ** (-0.5)
    grad_attended = matmul_nt(grad_low, out_full).astype(jnp.bfloat16)
    grad_out_full = matmul_tn(attended, grad_low)
    table_wide = rel_table.astype(jnp.float32)

    def by_clip(array):
        return array.reshape(CLIPS, L, local_heads, HEAD)

    def one_clip(clip_item):
        query_clip, key_clip, value_clip, grad_clip, total_clip, length = clip_item

        def one_block(carried, blk_index):
            grad_keys, grad_values, grad_table = carried
            first_row = blk_index * block_rows
            query_blk = lax.dynamic_slice_in_dim(query_clip, first_row, block_rows, 0)
            grad_blk = lax.dynamic_slice_in_dim(grad_clip, first_row, block_rows, 0)
            scores = block_scores(query_blk, key_clip, rel_table, first_row, length)
            attn_probs = jnp.exp(scores - total_clip[blk_index][..., None])
            grad_probs = jnp.einsum(
                "bhd,khd->hbk", grad_blk, value_clip, preferred_element_type=jnp.float32
            )
            row_inner = jnp.sum(attn_probs * grad_probs, axis=-1, keepdims=True)
            grad_scores = (attn_probs * (grad_probs - row_inner)).astype(jnp.bfloat16)
            grad_toward = bucket_sums(grad_scores, first_row)
            grad_query = score_scale * (
                jnp.einsum(
                    "hbk,khd->bhd", grad_scores, key_clip, preferred_element_type=jnp.float32
                )
                + jnp.einsum(
                    "hbn,nd->bhd", grad_toward, table_wide, precision=lax.Precision.HIGHEST
                )
            )
            grad_keys = grad_keys + score_scale * jnp.einsum(
                "hbk,bhd->khd", grad_scores, query_blk, preferred_element_type=jnp.float32
            )
            grad_values = grad_values + jnp.einsum(
                "hbk,bhd->khd",
                attn_probs.astype(jnp.bfloat16),
                grad_blk,
                preferred_element_type=jnp.float32,
            )
            grad_table = grad_table + score_scale * jnp.einsum(
                "hbn,bhd->nd",
                grad_toward,
                query_blk.astype(jnp.float32),
                precision=lax.Precision.HIGHEST,
            )
            return ((grad_keys, grad_values, grad_table), grad_query)

        zero_rows = jnp.zeros((L, local_heads, HEAD), jnp.float32)
        initial = (zero_rows, zero_rows, jnp.zeros(rel_table.shape, jnp.float32))
        (grad_keys, grad_values, grad_table), grad_query = lax.scan(
            one_block, initial, jnp.arange(block_count, dtype=jnp.int32)
        )
        return (grad_query, grad_keys, grad_values, grad_table)

    grad_query, grad_keys, grad_values, grad_table = lax.map(
        one_clip,
        (
            by_clip(queries),
            by_clip(key_rows),
            by_clip(value_rows),
            by_clip(grad_attended),
            log_totals,
            clip_lengths,
        ),
    )
    low_query = grad_query.reshape(group_rows, head_cols).astype(jnp.bfloat16)
    low_keys = grad_keys.reshape(group_rows, head_cols).astype(jnp.bfloat16)
    low_values = grad_values.reshape(group_rows, head_cols).astype(jnp.bfloat16)
    grad_proj = jnp.stack(
        [
            matmul_tn(entered, low_query),
            matmul_tn(entered, low_keys),
            matmul_tn(entered, low_values),
        ]
    )
    partial_value = (
        matmul_nt(low_query, proj_full[0])
        + matmul_nt(low_keys, proj_full[1])
        + matmul_nt(low_values, proj_full[2])
    )
    return (partial_value, grad_proj, grad_out_full, jnp.sum(grad_table, axis=0))


def depthwise(signal, conv_taps):
    shaped = signal.reshape(CLIPS, L, signal.shape[-1])
    padded = jnp.pad(shaped, ((0, 0), (KERNEL - 1, 0), (0, 0)))
    result = jnp.zeros_like(shaped)
    for tap_index in range(KERNEL):
        result = result + conv_taps[tap_index] * padded[:, tap_index : tap_index + L]
    return result.reshape(signal.shape)


def depthwise_back(grad_conv, signal, conv_taps):
    grad_shaped = grad_conv.reshape(CLIPS, L, grad_conv.shape[-1])
    padded_signal = jnp.pad(signal.reshape(grad_shaped.shape), ((0, 0), (KERNEL - 1, 0), (0, 0)))
    padded_grad = jnp.pad(grad_shaped, ((0, 0), (0, KERNEL - 1), (0, 0)))
    grad_signal = jnp.zeros_like(grad_shaped)
    taps_rows = []
    for tap_index in range(KERNEL):
        shift_at = KERNEL - 1 - tap_index
        grad_signal = grad_signal + conv_taps[tap_index] * padded_grad[:, shift_at : shift_at + L]
        taps_rows.append(
            jnp.sum(grad_shaped * padded_signal[:, tap_index : tap_index + L], axis=(0, 1))
        )
    return (grad_signal.reshape(grad_conv.shape), jnp.stack(taps_rows))


def conv_forward(entered, glu_full, taps_local, gain_local, shift_local, out_full):
    glu_first = matmul(entered, glu_full[0])
    glu_second = matmul(entered, glu_full[1])
    gated = glu_first * jax.nn.sigmoid(glu_second)
    mixed_conv = depthwise(gated, taps_local)
    sum_plain, sum_square = lax.psum(
        (jnp.sum(mixed_conv, axis=-1), jnp.sum(mixed_conv * mixed_conv, axis=-1)), "tensor"
    )
    mean_val = sum_plain / D
    inv_std = lax.rsqrt(sum_square / D - mean_val * mean_val + EPSILON)[:, None]
    normed = (mixed_conv - mean_val[:, None]) * inv_std
    shaped = normed * gain_local + shift_local
    activated = jax.nn.silu(shaped).astype(jnp.bfloat16)
    return (
        matmul(activated, out_full),
        (glu_first, glu_second, normed, inv_std, shaped, activated),
    )


def conv_backward(entered, saved, grad_low, glu_full, taps_local, gain_local, out_full):
    glu_first, glu_second, normed, inv_std, shaped, activated = saved
    grad_act = matmul_nt(grad_low, out_full)
    grad_out_full = matmul_tn(activated, grad_low)
    sigma = jax.nn.sigmoid(shaped)
    grad_shaped = grad_act * sigma * (1.0 + shaped * (1.0 - sigma))
    gain_grad = jnp.sum(grad_shaped * normed, axis=0)
    shift_grad = jnp.sum(grad_shaped, axis=0)
    grad_normed = grad_shaped * gain_local
    sum_plain, sum_cross = lax.psum(
        (jnp.sum(grad_normed, axis=-1), jnp.sum(grad_normed * normed, axis=-1)), "tensor"
    )
    grad_conv = inv_std * (grad_normed - sum_plain[:, None] / D - normed * sum_cross[:, None] / D)
    sig_second = jax.nn.sigmoid(glu_second)
    grad_gated, taps_grad = depthwise_back(grad_conv, glu_first * sig_second, taps_local)
    grad_first = (grad_gated * sig_second).astype(jnp.bfloat16)
    grad_second = (grad_gated * glu_first * sig_second * (1.0 - sig_second)).astype(jnp.bfloat16)
    grad_glu = jnp.stack([matmul_tn(entered, grad_first), matmul_tn(entered, grad_second)])
    partial_value = matmul_nt(grad_first, glu_full[0]) + matmul_nt(grad_second, glu_full[1])
    return (partial_value, grad_glu, grad_out_full, taps_grad, gain_grad, shift_grad)


def on_device(
    stream_in,
    grad_out,
    clip_lengths,
    first_up,
    first_down,
    attn_proj,
    attn_out,
    rel_table,
    glu_weight,
    conv_taps,
    conv_out,
    second_up,
    second_down,
    norm_gains,
    norm_shifts,
):
    tensor_index = lax.axis_index("tensor")
    channels = D // lax.axis_size("tensor")
    gathered = (
        lax.all_gather(first_up, "dp", axis=0, tiled=True),
        lax.all_gather(first_down, "dp", axis=1, tiled=True),
        lax.all_gather(attn_proj, "dp", axis=1, tiled=True),
        lax.all_gather(attn_out, "dp", axis=1, tiled=True),
        lax.all_gather(glu_weight, "dp", axis=1, tiled=True),
        lax.all_gather(conv_out, "dp", axis=1, tiled=True),
        lax.all_gather(second_up, "dp", axis=0, tiled=True),
        lax.all_gather(second_down, "dp", axis=1, tiled=True),
    )
    up_one, down_one, proj_full, attn_full, glu_full, conv_full, up_two, down_two = gathered

    def enter_branch(stream, norm_row):
        result, normed, inv_std = norm_forward(stream, norm_gains[norm_row], norm_shifts[norm_row])
        lowered = result.astype(jnp.bfloat16)
        lowered = lax.all_gather(lowered, "tensor", axis=0, tiled=True)
        return (lowered, normed, inv_std)

    def leave_branch(partial_value):
        return lax.psum_scatter(partial_value, "tensor", scatter_dimension=0, tiled=True)

    def enter_back(grad_branch):
        lowered = grad_branch.astype(jnp.bfloat16)
        lowered = lax.all_gather(lowered, "tensor", axis=0, tiled=True)
        return lowered

    def leave_back(partial_value):
        return lax.psum_scatter(
            partial_value.astype(jnp.bfloat16), "tensor", scatter_dimension=0, tiled=True
        ).astype(jnp.float32)

    def record(branch):
        total_sq = jnp.sum(branch * branch)
        total_sq = lax.psum(total_sq, ("dp", "tensor"))
        return total_sq

    def norm_back(grad_result, normed, inv_std, norm_row):
        grad_input = norm_backward(grad_result, normed, inv_std, norm_gains[norm_row])
        return (grad_input, jnp.sum(grad_result * normed, axis=0), jnp.sum(grad_result, axis=0))

    def widen(vector, axis_at, full_shape):
        return lax.dynamic_update_slice_in_dim(
            jnp.zeros(full_shape, jnp.float32), vector, tensor_index * channels, axis_at
        )

    stream = stream_in.astype(jnp.float32)
    squares = []
    entered_a, normed_a, scale_a = enter_branch(stream, 0)
    partial_value, before_a = ffn_forward(entered_a, up_one, down_one)
    branch = leave_branch(partial_value)
    squares.append(record(branch))
    stream = stream + 0.5 * branch
    entered_b, normed_b, scale_b = enter_branch(stream, 1)
    partial_value, attn_saved = attention_forward(
        entered_b, proj_full, attn_full, rel_table, clip_lengths
    )
    branch = leave_branch(partial_value)
    squares.append(record(branch))
    stream = stream + branch
    entered_c, normed_c, scale_c = enter_branch(stream, 2)
    taps_local = lax.dynamic_slice_in_dim(conv_taps, tensor_index * channels, channels, 1)
    gain_local = lax.dynamic_slice_in_dim(norm_gains[3], tensor_index * channels, channels, 0)
    shift_local = lax.dynamic_slice_in_dim(norm_shifts[3], tensor_index * channels, channels, 0)
    partial_value, conv_saved = conv_forward(
        entered_c, glu_full, taps_local, gain_local, shift_local, conv_full
    )
    branch = leave_branch(partial_value)
    squares.append(record(branch))
    stream = stream + branch
    entered_d, normed_d, scale_d = enter_branch(stream, 4)
    partial_value, before_d = ffn_forward(entered_d, up_two, down_two)
    branch = leave_branch(partial_value)
    squares.append(record(branch))
    stream = stream + 0.5 * branch
    squares.append(record(stream))
    result, normed_e, scale_e = norm_forward(stream, norm_gains[5], norm_shifts[5])
    output = result.astype(jnp.bfloat16)
    grad_stream, gain_e, shift_e = norm_back(grad_out.astype(jnp.float32), normed_e, scale_e, 5)
    grad_low = enter_back(0.5 * grad_stream)
    partial_value, grad_up_two, grad_down_two = ffn_backward(
        entered_d, before_d, grad_low, up_two, down_two
    )
    grad_extra, gain_d, shift_d = norm_back(leave_back(partial_value), normed_d, scale_d, 4)
    grad_stream = grad_stream + grad_extra
    grad_low = enter_back(grad_stream)
    partial_value, grad_glu, grad_conv_out, taps_grad, gain_mid, shift_mid = conv_backward(
        entered_c, conv_saved, grad_low, glu_full, taps_local, gain_local, conv_full
    )
    grad_extra, gain_c, shift_c = norm_back(leave_back(partial_value), normed_c, scale_c, 2)
    grad_stream = grad_stream + grad_extra
    grad_low = enter_back(grad_stream)
    partial_value, grad_proj, grad_attn_out, table_grad = attention_backward(
        entered_b, attn_saved, grad_low, proj_full, attn_full, rel_table, clip_lengths
    )
    grad_extra, gain_b, shift_b = norm_back(leave_back(partial_value), normed_b, scale_b, 1)
    grad_stream = grad_stream + grad_extra
    grad_low = enter_back(0.5 * grad_stream)
    partial_value, grad_up_one, grad_down_one = ffn_backward(
        entered_a, before_a, grad_low, up_one, down_one
    )
    grad_extra, gain_a, shift_a = norm_back(leave_back(partial_value), normed_a, scale_a, 0)
    grad_stream = grad_stream + grad_extra
    weight_grads = (
        lax.psum_scatter(
            grad_up_one.astype(jnp.bfloat16), "dp", scatter_dimension=0, tiled=True
        ).astype(jnp.float32),
        lax.psum_scatter(
            grad_down_one.astype(jnp.bfloat16), "dp", scatter_dimension=1, tiled=True
        ).astype(jnp.float32),
        lax.psum_scatter(
            grad_proj.astype(jnp.bfloat16), "dp", scatter_dimension=1, tiled=True
        ).astype(jnp.float32),
        lax.psum_scatter(
            grad_attn_out.astype(jnp.bfloat16), "dp", scatter_dimension=1, tiled=True
        ).astype(jnp.float32),
        lax.psum_scatter(
            grad_glu.astype(jnp.bfloat16), "dp", scatter_dimension=1, tiled=True
        ).astype(jnp.float32),
        lax.psum_scatter(
            grad_conv_out.astype(jnp.bfloat16), "dp", scatter_dimension=1, tiled=True
        ).astype(jnp.float32),
        lax.psum_scatter(
            grad_up_two.astype(jnp.bfloat16), "dp", scatter_dimension=0, tiled=True
        ).astype(jnp.float32),
        lax.psum_scatter(
            grad_down_two.astype(jnp.bfloat16), "dp", scatter_dimension=1, tiled=True
        ).astype(jnp.float32),
    )
    gains_stack = jnp.stack([gain_a, gain_b, gain_c, widen(gain_mid, 0, (D,)), gain_d, gain_e])
    shifts_stack = jnp.stack(
        [shift_a, shift_b, shift_c, widen(shift_mid, 0, (D,)), shift_d, shift_e]
    )
    taps_wide = widen(taps_grad, 1, (KERNEL, D))
    gains_sum, shifts_sum, taps_sum, table_sum = lax.psum(
        (gains_stack, shifts_stack, taps_wide, table_grad), ("dp", "tensor")
    )
    square_sum = jnp.stack(squares)
    count_all = float(lax.axis_size("dp") * CLIPS * L * D)
    rms_values = jnp.sqrt(square_sum / count_all)
    return (
        output,
        grad_stream,
        weight_grads[0],
        weight_grads[1],
        weight_grads[2],
        weight_grads[3],
        table_sum,
        weight_grads[4],
        taps_sum,
        weight_grads[5],
        weight_grads[6],
        weight_grads[7],
        gains_sum,
        shifts_sum,
        rms_values,
    )


def solution(mesh):
    return jax.shard_map(
        on_device,
        mesh=mesh,
        in_specs=(
            P(("dp", "tensor"), None),
            P(("dp", "tensor"), None),
            P("dp"),
            P("dp", "tensor"),
            P("tensor", "dp"),
            P(None, "dp", "tensor"),
            P("tensor", "dp"),
            P(),
            P(None, "dp", "tensor"),
            P(),
            P("tensor", "dp"),
            P("dp", "tensor"),
            P("tensor", "dp"),
            P(),
            P(),
        ),
        out_specs=(
            P(("dp", "tensor"), None),
            P(("dp", "tensor"), None),
            P("dp", "tensor"),
            P("tensor", "dp"),
            P(None, "dp", "tensor"),
            P("tensor", "dp"),
            P(),
            P(None, "dp", "tensor"),
            P(),
            P("tensor", "dp"),
            P("dp", "tensor"),
            P("tensor", "dp"),
            P(),
            P(),
            P(),
        ),
        check_vma=False,
    )
```

profile of v0, /device:TPU:0, one launch (start us, length us, event | category | flops | bytes accessed | tf_op | source)
XLA Modules:
  0.0 2577.0 jit_solution(7572864464534047946)
XLA Ops:
  14.7 11.9 all-gather.17.cloned.1.call-done
  26.6 79.6 %all-gather.19.cloned.1.call-done = bf16[1024,2048]{1,0:T(8,128)(2,1)} async-done(((bf16[64,2048]{1,0:T(8,128)(2,1)}), bf16[1024,2048]{1,0:T(8,128)(2,1)}) %all-gather.19.cloned.1.call-update) | async-done | bytes 4194320 | tf_op jit(solution)/shard_map/all_gather | solution.py:311
  106.2 12.6 multiply_convert_fusion.4
  118.8 64.4 %all-gather.21.cloned.1.call-done = bf16[2048,1024]{0,1:T(8,128)(2,1)} async-done(((bf16[2048,64]{0,1:T(8,128)(2,1)}), bf16[2048,1024]{0,1:T(8,128)(2,1)}) %all-gather.21.cloned.1.call-update) | async-done | bytes 4194320 | tf_op jit(solution)/shard_map/all_gather | solution.py:312
  193.8 10.2 reduce-scatter.17.cloned.1.call-done
  210.6 65.1 %all-gather.25.cloned.1.call-done = bf16[3,1024,512]{2,1,0:T(8,128)(2,1)} async-done(((bf16[3,64,512]{2,1,0:T(8,128)(2,1)}), bf16[3,1024,512]{2,1,0:T(8,128)(2,1)}) %all-gather.25.cloned.1.call-update) | async-done | bytes 3145744 | tf_op jit(solution)/shard_map/all_gather | solution.py:313
  275.7 11.2 all-gather.23.cloned.1.call-done
  298.4 333.2 %while.55 = (s32[]{:T(128)}, bf16[2,512,8,64]{1,3,2,0:T(8,128)(2,1)}, f32[2,8,512]{2,1,0:T(8,128)}, s32[]{:T(128)}, s32[2]{0:T(128)S(1)}, /*index=5*/bf16[1024,8...) while((s32[]{:T(128)}, ...), condition=%wide.region_8.10_spmd, body=%wide.region_5.9_spmd.sunk | while | flops 1156080128 | bytes 440197600 | solution.py:126
  311.6 18.4 select_bitcast_fusion.4
  329.9 24.8 copy.53
  354.8 21.8 copy.54
  385.1 18.1 reshape.425
  403.2 39.1 %reshape.426 = f32[8,512,1535]{2,1,0:T(8,128)} reshape(f32[6287360]{0:T(1024)} %reshape.425) | data formatting | bytes 50298880 | tf_op jit(solution)/shard_map/while/body/eval_jaxpr/while/body/eval_jaxpr/reshape | solution.py:79
  474.2 18.3 select_bitcast_fusion.4
  492.6 24.8 copy.53
  517.4 21.8 copy.54
  547.7 18.1 reshape.425
  565.8 39.1 %reshape.426 = f32[8,512,1535]{2,1,0:T(8,128)} reshape(f32[6287360]{0:T(1024)} %reshape.425) | data formatting | bytes 50298880 | tf_op jit(solution)/shard_map/while/body/eval_jaxpr/while/body/eval_jaxpr/reshape | solution.py:79
  639.9 12.6 reduce-scatter.19.cloned.1.call-done
  661.5 55.3 %all-gather.31.cloned.1.call-done = bf16[2,1024,512]{2,1,0:T(8,128)(2,1)} async-done(((bf16[2,64,512]{2,1,0:T(8,128)(2,1)}), bf16[2,1024,512]{2,1,0:T(8,128)(2,1)}) %all-gather.31.cloned.1.call-update) | async-done | bytes 2097168 | tf_op jit(solution)/shard_map/all_gather | solution.py:315
  716.9 11.3 all-gather.29.cloned.1.call-done
  750.3 37.0 %all-gather.33.cloned.1.call-done = bf16[512,1024]{0,1:T(8,128)(2,1)} async-done(((bf16[512,64]{0,1:T(8,128)(2,1)}), bf16[512,1024]{0,1:T(8,128)(2,1)}) %all-gather.33.cloned.1.call-update) | async-done | bytes 1048592 | tf_op jit(solution)/shard_map/all_gather | solution.py:316
  809.9 72.8 %all-gather.37.cloned.1.call-done = bf16[1024,2048]{1,0:T(8,128)(2,1)} async-done(((bf16[64,2048]{1,0:T(8,128)(2,1)}), bf16[1024,2048]{1,0:T(8,128)(2,1)}) %all-gather.37.cloned.1.call-update) | async-done | bytes 4194320 | tf_op jit(solution)/shard_map/all_gather | solution.py:317
  882.7 11.2 all-gather.35.cloned.1.call-done
  893.9 12.5 multiply_convert_fusion.3
  906.4 66.9 %all-gather.39.cloned.1.call-done = bf16[2048,1024]{0,1:T(8,128)(2,1)} async-done(((bf16[2048,64]{0,1:T(8,128)(2,1)}), bf16[2048,1024]{0,1:T(8,128)(2,1)}) %all-gather.39.cloned.1.call-update) | async-done | bytes 4194320 | tf_op jit(solution)/shard_map/all_gather | solution.py:318
  983.3 10.8 reduce-scatter.23.cloned.1.call-done
  1003.7 11.5 all-gather.41.cloned.1.call-done
  1015.2 11.4 multiply_convert_fusion.2
  1034.4 11.0 reduce-scatter.25.cloned.1.call-done
  1053.5 12.0 all-gather.43.cloned.1.call-done
  1092.3 11.0 reduce-scatter.27.cloned.1.call-done
  1110.1 10.6 all-gather.45.cloned.1.call-done
  1125.9 547.7 %while.56 = (s32[]{:T(128)}, f32[1024,8,64]{0,2,1:T(8,128)}, f32[1024,8,64]{0,2,1:T(8,128)}, f32[73,64]{0,1:T(8,128)}, bf16[2,512,8,64]{1,3,2,0:T(8,128)(2,1)}, ...) while((s32[]{:T(128)}, f32[1024,8,64]{0,2,1:T(8,128)}, ...), condition=%wide.region_36.38_spmd.clone, body=%wide.region_34.37_spmd.clone.sunk | while | flops 4151987968 | bytes 650503936 | solution.py:192
  1151.1 18.3 select_bitcast_fusion.5
  1169.4 24.8 copy.57
  1194.3 21.8 copy.58
  1224.6 18.1 reshape.429
  1242.6 39.1 %reshape.430 = f32[8,512,1535]{2,1,0:T(8,128)} reshape(f32[6287360]{0:T(1024)} %reshape.429) | data formatting | bytes 50298880 | tf_op jit(solution)/shard_map/while/body/eval_jaxpr/while/body/eval_jaxpr/reshape | solution.py:79
  1281.7 17.5 multiply_reduce_fusion.45
  1299.3 11.4 multiply_convert_fusion.9
  1331.8 22.4 reshape.431
  1354.2 22.7 reshape.432
  1419.5 18.3 select_bitcast_fusion.5
  1437.9 24.8 copy.57
  1462.7 21.8 copy.58
  1493.0 18.1 reshape.429
  1511.1 39.1 %reshape.430 = f32[8,512,1535]{2,1,0:T(8,128)} reshape(f32[6287360]{0:T(1024)} %reshape.429) | data formatting | bytes 50298880 | tf_op jit(solution)/shard_map/while/body/eval_jaxpr/while/body/eval_jaxpr/reshape | solution.py:79
  1550.2 17.3 multiply_reduce_fusion.45
  1567.5 11.4 multiply_convert_fusion.9
  1602.3 22.6 reshape.431
  1624.9 22.7 reshape.432
  1686.7 11.0 reduce-scatter.29.cloned.1.call-done
  1745.8 11.4 multiply_convert_fusion.1
  1797.3 16.0 reduce-scatter.47.cloned.1.call-done
  1815.0 95.2 %reduce-scatter.45.cloned.1.call-done = bf16[64,2048]{1,0:T(8,128)(2,1)} async-done(((bf16[1024,2048]{1,0:T(8,128)(2,1)}), bf16[64,2048]{1,0:T(8,128)(2,1)}) %reduce-scatter.45.cloned.1.call-update) | async-done | bytes 262160 | tf_op jit(solution)/shard_map/reduce_scatter | solution.py:431
  1912.1 78.5 %reduce-scatter.43.cloned.1.call-done = bf16[512,64]{0,1:T(8,128)(2,1)} async-done(((bf16[512,1024]{0,1:T(8,128)(2,1)}), bf16[512,64]{0,1:T(8,128)(2,1)}) %reduce-scatter.43.cloned.1.call-update) | async-done | bytes 65552 | tf_op jit(solution)/shard_map/reduce_scatter | solution.py:428
  1992.1 78.7 %reduce-scatter.41.cloned.1.call-done = bf16[2,64,512]{2,1,0:T(8,128)(2,1)} async-done(((bf16[2,1024,512]{2,1,0:T(8,128)(2,1)}), bf16[2,64,512]{2,1,0:T(8,128)(2,1)}) %reduce-scatter.41.cloned.1.call-update) | async-done | bytes 131088 | tf_op jit(solution)/shard_map/reduce_scatter | solution.py:425
  2072.4 76.0 %reduce-scatter.39.cloned.1.call-done = bf16[512,64]{0,1:T(8,128)(2,1)} async-done(((bf16[512,1024]{0,1:T(8,128)(2,1)}), bf16[512,64]{0,1:T(8,128)(2,1)}) %reduce-scatter.39.cloned.1.call-update) | async-done | bytes 65552 | tf_op jit(solution)/shard_map/reduce_scatter | solution.py:422
  2149.9 81.8 %reduce-scatter.37.cloned.1.call-done = bf16[3,64,512]{2,1,0:T(8,128)(2,1)} async-done(((bf16[3,1024,512]{2,1,0:T(8,128)(2,1)}), bf16[3,64,512]{2,1,0:T(8,128)(2,1)}) %reduce-scatter.37.cloned.1.call-update) | async-done | bytes 196624 | tf_op jit(solution)/shard_map/reduce_scatter | solution.py:419
  2243.9 46.9 %all-reduce.11 = (f32[73,64]{0,1:T(8,128)}, f32[6,1024]{1,0:T(8,128)}, f32[6,1024]{1,0:T(8,128)}, f32[1]{0:T(128)}, f32[1]{0:T(128)}, /*index=5*/f32[1]{0:T(128)}, f32[1]{0:T(128)}, f32[1]{0:T(128)}) all-reduce(f32[73,64]{0,1:T(8,128)S(1)} %copy-done.44, ...), channel_id=1, replica_groups=mesh['dp'=16,'tensor'=2] {'dp','tensor'}, use_global_device_ids=true, to_apply=%region_47.49 | all-reduce | flops 16965 | bytes 135720 | tf_op jit(solution)/shard_map/psum | solution.py:443
  2297.9 43.2 %reduce-scatter.35.cloned.1.call-done = bf16[2048,64]{0,1:T(8,128)(2,1)} async-done(((bf16[2048,1024]{0,1:T(8,128)(2,1)}), bf16[2048,64]{0,1:T(8,128)(2,1)}) %reduce-scatter.35.cloned.1.call-update) | async-done | bytes 262160 | tf_op jit(solution)/shard_map/reduce_scatter | solution.py:416
  2342.9 95.4 %reduce-scatter.33.cloned.1.call-done = bf16[64,2048]{1,0:T(8,128)(2,1)} async-done(((bf16[1024,2048]{1,0:T(8,128)(2,1)}), bf16[64,2048]{1,0:T(8,128)(2,1)}) %reduce-scatter.33.cloned.1.call-update) | async-done | bytes 262160 | tf_op jit(solution)/shard_map/reduce_scatter | solution.py:413
  2440.0 128.2 %all-reduce.10.cloned.1.call-done = f32[31,1024]{1,0:T(8,128)} async-done(((f32[31,1024]{1,0:T(8,128)}), f32[31,1024]{1,0:T(8,128)}) %all-reduce.10.cloned.1.call-update) | async-done | bytes 126992 | tf_op jit(solution)/shard_map/psum | solution.py:443
  (495 shorter events, 525.0 us)
Async XLA Ops:
  7.2 19.4 all-gather.17.cloned.1.call-start
  11.1 196.1 %copy-start.57 = (f32[1,1024]{1,0:T(1,128)}, f32[1,1024]{1,0:T(1,128)S(1)}, u32[]{:S(2)}) copy-start(f32[1,1024]{1,0:T(1,128)S(1)} %get-tuple-element.599) | copy-start | bytes 12292
  13.2 93.0 %all-gather.19.cloned.1.call-start = ((), (), s32[]{:S(2)}) async-start(), calls=%async_computation.17 | async-start | bytes 4456448 | tf_op jit(solution)/shard_map/all_gather | solution.py:311
  13.9 169.3 %all-gather.21.cloned.1.call-start = ((), (), s32[]{:S(2)}) async-start(), calls=%async_computation.18 | async-start | bytes 4456448 | tf_op jit(solution)/shard_map/all_gather | solution.py:312
  14.6 189.3 %reduce-scatter.17.cloned.1.call-start = ((), (), s32[]{:S(2)}) async-start(), calls=%async_computation.19 | async-start | bytes 6291456 | tf_op jit(solution)/shard_map/reduce_scatter | solution.py:329
  193.1 82.6 %all-gather.25.cloned.1.call-start = ((), (), s32[]{:S(2)}) async-start(), calls=%async_computation.21 | async-start | bytes 3342336 | tf_op jit(solution)/shard_map/all_gather | solution.py:313
  193.7 93.2 %all-gather.23.cloned.1.call-start = ((), (), s32[]{:S(2)}) async-start(), calls=%async_computation.20 | async-start | bytes 3145728 | tf_op jit(solution)/shard_map/all_gather | solution.py:325
  209.5 424.7 %all-gather.27.cloned.1.call-start = ((), (), s32[]{:S(2)}) async-start(), calls=%async_computation.22 | async-start | bytes 1114112 | tf_op jit(solution)/shard_map/all_gather | solution.py:314
  210.3 442.2 %reduce-scatter.19.cloned.1.call-start = ((), (), s32[]{:S(2)}) async-start(), calls=%async_computation.23 | async-start | bytes 6291456 | tf_op jit(solution)/shard_map/reduce_scatter | solution.py:329
  639.1 13.4 copy-start.8
  639.1 77.8 %all-gather.31.cloned.1.call-start = ((), (), s32[]{:S(2)}) async-start(), calls=%async_computation.25 | async-start | bytes 2228224 | tf_op jit(solution)/shard_map/all_gather | solution.py:315
  639.8 88.4 %all-gather.29.cloned.1.call-start = ((), (), s32[]{:S(2)}) async-start(), calls=%async_computation.24 | async-start | bytes 3145728 | tf_op jit(solution)/shard_map/all_gather | solution.py:325
  658.1 129.2 %all-gather.33.cloned.1.call-start = ((), (), s32[]{:S(2)}) async-start(), calls=%async_computation.26 | async-start | bytes 1114112 | tf_op jit(solution)/shard_map/all_gather | solution.py:316
  658.8 144.3 %reduce-scatter.21.cloned.1.call-start = ((), (), s32[]{:S(2)}) async-start(), calls=%async_computation.27 | async-start | bytes 6291456 | tf_op jit(solution)/shard_map/reduce_scatter | solution.py:329
  734.4 340.3 %copy-start.1 = (f32[1024,512]{1,0:T(8,128)}, f32[1024,512]{1,0:T(8,128)S(1)}, u32[]{:S(2)}) copy-start(f32[1024,512]{1,0:T(8,128)S(1)} %get-tuple-element.612) | copy-start | bytes 6291460
  792.0 90.7 %all-gather.37.cloned.1.call-start = ((), (), s32[]{:S(2)}) async-start(), calls=%async_computation.29 | async-start | bytes 4456448 | tf_op jit(solution)/shard_map/all_gather | solution.py:317
  792.8 101.1 %all-gather.35.cloned.1.call-start = ((), (), s32[]{:S(2)}) async-start(), calls=%async_computation.28 | async-start | bytes 3145728 | tf_op jit(solution)/shard_map/all_gather | solution.py:325
  809.3 164.0 %all-gather.39.cloned.1.call-start = ((), (), s32[]{:S(2)}) async-start(), calls=%async_computation.30 | async-start | bytes 4456448 | tf_op jit(solution)/shard_map/all_gather | solution.py:318
  809.9 184.2 %reduce-scatter.23.cloned.1.call-start = ((), (), s32[]{:S(2)}) async-start(), calls=%async_computation.31 | async-start | bytes 6291456 | tf_op jit(solution)/shard_map/reduce_scatter | solution.py:329
  983.3 32.0 %all-gather.41.cloned.1.call-start = ((), (), s32[]{:S(2)}) async-start(), calls=%async_computation.32 | async-start | bytes 3145728 | tf_op jit(solution)/shard_map/all_gather | solution.py:333
  1003.2 42.2 %reduce-scatter.25.cloned.1.call-start = ((), (), s32[]{:S(2)}) async-start(), calls=%async_computation.33 | async-start | bytes 3145728 | tf_op jit(solution)/shard_map/reduce_scatter | solution.py:337
  1015.2 13.3 copy-start.89
  1034.3 14.7 copy-start.80
  1034.3 31.1 %all-gather.43.cloned.1.call-start = ((), (), s32[]{:S(2)}) async-start(), calls=%async_computation.34 | async-start | bytes 3145728 | tf_op jit(solution)/shard_map/all_gather | solution.py:333
  1053.5 49.9 %reduce-scatter.27.cloned.1.call-start = ((), (), s32[]{:S(2)}) async-start(), calls=%async_computation.35 | async-start | bytes 3145728 | tf_op jit(solution)/shard_map/reduce_scatter | solution.py:337
  1078.1 8.2 copy-start.3
  1092.2 11.1 copy-start.11
  1092.3 28.4 %all-gather.45.cloned.1.call-start = ((), (), s32[]{:S(2)}) async-start(), calls=%async_computation.36 | async-start | bytes 3145728 | tf_op jit(solution)/shard_map/all_gather | solution.py:333
  1108.7 589.1 %reduce-scatter.29.cloned.1.call-start = ((), (), s32[]{:S(2)}) async-start(), calls=%async_computation.37 | async-start | bytes 3145728 | tf_op jit(solution)/shard_map/reduce_scatter | solution.py:337
  1110.1 15.9 copy-start
  1299.3 11.4 copy-start.21
  1383.1 8.2 copy-start.32
  1383.1 8.2 copy-start.41
  1567.5 11.4 copy-start.21
  1653.7 8.2 copy-start.32
  1653.7 8.2 copy-start.41
  1683.9 13.9 copy-start.58
  1683.9 13.9 copy-start.69
  1686.7 11.1 copy-start.9
  1686.7 11.1 copy-start.65
  1686.7 59.1 %all-gather.47.cloned.1.call-start = ((), (), s32[]{:S(2)}) async-start(), calls=%async_computation.38 | async-start | bytes 3145728 | tf_op jit(solution)/shard_map/all_gather | solution.py:333
  1702.7 110.6 %reduce-scatter.47.cloned.1.call-start = ((), (), s32[]{:S(2)}) async-start(), calls=%async_computation.48 | async-start | bytes 4456448 | tf_op jit(solution)/shard_map/reduce_scatter | solution.py:434
  1712.1 198.2 %reduce-scatter.45.cloned.1.call-start = ((), (), s32[]{:S(2)}) async-start(), calls=%async_computation.47 | async-start | bytes 4456448 | tf_op jit(solution)/shard_map/reduce_scatter | solution.py:431
  1722.4 268.2 %reduce-scatter.43.cloned.1.call-start = ((), (), s32[]{:S(2)}) async-start(), calls=%async_computation.46 | async-start | bytes 1114112 | tf_op jit(solution)/shard_map/reduce_scatter | solution.py:428
  1727.0 343.7 %reduce-scatter.41.cloned.1.call-start = ((), (), s32[]{:S(2)}) async-start(), calls=%async_computation.44 | async-start | bytes 2228224 | tf_op jit(solution)/shard_map/reduce_scatter | solution.py:425
  1732.5 415.9 %reduce-scatter.39.cloned.1.call-start = ((), (), s32[]{:S(2)}) async-start(), calls=%async_computation.43 | async-start | bytes 1114112 | tf_op jit(solution)/shard_map/reduce_scatter | solution.py:422
  1737.6 494.1 %reduce-scatter.37.cloned.1.call-start = ((), (), s32[]{:S(2)}) async-start(), calls=%async_computation.42 | async-start | bytes 3342336 | tf_op jit(solution)/shard_map/reduce_scatter | solution.py:419
  1745.5 495.9 %reduce-scatter.31.cloned.1.call-start = ((), (), s32[]{:S(2)}) async-start(), calls=%async_computation.39 | async-start | bytes 3145728 | tf_op jit(solution)/shard_map/reduce_scatter | solution.py:337
  1745.8 13.4 copy-start.88
  1765.1 576.0 %reduce-scatter.35.cloned.1.call-start = ((), (), s32[]{:S(2)}) async-start(), calls=%async_computation.41 | async-start | bytes 4456448 | tf_op jit(solution)/shard_map/reduce_scatter | solution.py:416
  1775.0 663.2 %reduce-scatter.33.cloned.1.call-start = ((), (), s32[]{:S(2)}) async-start(), calls=%async_computation.40 | async-start | bytes 4456448 | tf_op jit(solution)/shard_map/reduce_scatter | solution.py:413
  1785.0 783.2 %all-reduce.10.cloned.1.call-start = ((), (), s32[]{:S(2)}) async-start(), calls=%async_computation.45 | async-start | bytes 262144 | tf_op jit(solution)/shard_map/psum | solution.py:443
  1796.3 445.2 %copy-start.16 = (bf16[512,1024]{1,0:T(8,128)(2,1)S(1)}, bf16[512,1024]{1,0:T(8,128)(2,1)}, u32[]{:S(2)}) copy-start(bf16[512,1024]{1,0:T(8,128)(2,1)} %param.21) | copy-start | bytes 3145732
  1796.3 445.2 %copy-start.63 = (f32[1,1024]{1,0:T(1,128)S(1)}, f32[1,1024]{1,0:T(1,128)}, u32[]{:S(2)}) copy-start(f32[1,1024]{1,0:T(1,128)} %copy-done.62) | copy-start | bytes 12292
  1796.3 445.1 %copy-start.67 = (f32[512]{0:T(512)S(1)}, f32[512]{0:T(512)}, u32[]{:S(2)}) copy-start(f32[512]{0:T(512)} %copy-done.66) | copy-start | bytes 6148
  1796.3 445.1 %copy-start.71 = (f32[512]{0:T(512)S(1)}, f32[512]{0:T(512)}, u32[]{:S(2)}) copy-start(f32[512]{0:T(512)} %copy-done.70) | copy-start | bytes 6148
  1815.0 428.7 %copy-start.75 = (f32[1024]{0:T(1024)S(1)}, f32[1024]{0:T(1024)}, u32[]{:S(2)}) copy-start(f32[1024]{0:T(1024)} %get-tuple-element.453) | copy-start | bytes 12292
  1815.0 428.7 %copy-start.77 = (f32[1024]{0:T(1024)S(1)}, f32[1024]{0:T(1024)}, u32[]{:S(2)}) copy-start(f32[1024]{0:T(1024)} %get-tuple-element.455) | copy-start | bytes 12292
  1815.0 428.7 %copy-start.79 = (f32[1024]{0:T(1024)S(1)}, f32[1024]{0:T(1024)}, u32[]{:S(2)}) copy-start(f32[1024]{0:T(1024)} %get-tuple-element.457) | copy-start | bytes 12292
  1815.0 428.8 %copy-start.74 = (f32[1024]{0:T(1024)S(1)}, f32[1024]{0:T(1024)}, u32[]{:S(2)}) copy-start(f32[1024]{0:T(1024)} %get-tuple-element.471) | copy-start | bytes 12292
  1815.0 428.8 %copy-start.76 = (f32[1024]{0:T(1024)S(1)}, f32[1024]{0:T(1024)}, u32[]{:S(2)}) copy-start(f32[1024]{0:T(1024)} %get-tuple-element.472) | copy-start | bytes 12292
  1815.0 428.8 %copy-start.78 = (f32[1024]{0:T(1024)S(1)}, f32[1024]{0:T(1024)}, u32[]{:S(2)}) copy-start(f32[1024]{0:T(1024)} %get-tuple-element.473) | copy-start | bytes 12292
  1815.0 428.8 %copy-start.44 = (f32[73,64]{0,1:T(8,128)S(1)}, f32[73,64]{0,1:T(8,128)}, u32[]{:S(2)}) copy-start(f32[73,64]{0,1:T(8,128)} %get-tuple-element.375) | copy-start | bytes 56068
  1912.1 382.0 %copy-start.26 = (f32[512,1024]{1,0:T(8,128)S(1)}, f32[512,1024]{1,0:T(8,128)}, u32[]{:S(2)}) copy-start(f32[512,1024]{1,0:T(8,128)} %get-tuple-element.537) | copy-start | bytes 6291460
  (85 other events, 226.0 us)
Sparse Core Ops, SparseCore 0:
  13.3 13.2 all-gather.16
  29.4 76.7 all-gather.18
  109.0 74.1 all-gather.20
  193.2 10.6 reduce-scatter.16
  206.5 69.1 all-gather.24
  277.7 9.1 all-gather.22
  289.7 56.2 all-gather.26
  639.2 13.2 reduce-scatter.18
  655.2 61.6 all-gather.30
  718.8 9.2 all-gather.28
  731.0 56.2 all-gather.32
  792.1 10.8 reduce-scatter.20
  805.8 76.8 all-gather.36
  884.7 9.1 all-gather.34
  896.5 76.7 all-gather.38
  983.4 10.6 reduce-scatter.22
  1003.3 11.8 all-gather.40
  1034.5 10.8 reduce-scatter.24
  1053.6 11.8 all-gather.42
  1092.4 10.9 reduce-scatter.26
  1108.8 11.8 all-gather.44
  1686.8 10.9 reduce-scatter.28
  1702.8 11.8 all-gather.46
  1716.8 96.3 reduce-scatter.46
  1815.5 94.7 reduce-scatter.44
  1912.4 78.1 reduce-scatter.42
  1992.7 77.9 reduce-scatter.40
  2073.0 75.3 reduce-scatter.38
  2150.7 80.9 reduce-scatter.36
  2233.8 7.5 reduce-scatter.30
  2243.7 97.3 reduce-scatter.34
  2343.4 94.7 reduce-scatter.32
  2444.2 123.9 all-reduce.9
where the time goes:
time: 2590 us; the launch traced here: 2580 us
  waiting for transfers between devices  1300 us (50%)
  local copies, waits for them, and re-layouts  652 us (25%)
  matrix products  310 us (12%)
  other arithmetic  216 us (8%)
  blocking collectives  52 us (2%)
    while x78, local copies, waits for them, and re-layouts  209 us
    reshape x4, local copies, waits for them, and re-layouts, block_scores(): sliced.reshape(local_heads, block_rows, width - 1)[:, :, :key_count]  156 us
    psum x1, waiting for transfers between devices, on_device(): lax.psum((gains_stack, shifts_stack, taps_wide, table_grad), ('dp', 'tens...  128 us
    select_n x4, local copies, waits for them, and re-layouts, block_scores(): jnp.take(toward, bucket_picks(first_row, block_rows, key_count), axis=2)  99.3 us
    reduce_scatter x1, waiting for transfers between devices, on_device(): lax.psum_scatter(grad_up_one.astype(jnp.bfloat16), 'dp', scatter_dimensio...  95.4 us
    reduce_scatter x1, waiting for transfers between devices, on_device(): lax.psum_scatter(grad_up_two.astype(jnp.bfloat16), 'dp', scatter_dimensio...  95.2 us
    reduce_scatter x1, waiting for transfers between devices, on_device(): lax.psum_scatter(grad_proj.astype(jnp.bfloat16), 'dp', scatter_dimension=...  81.8 us
    all_gather x1, waiting for transfers between devices, on_device(): lax.all_gather(first_up, 'dp', axis=0, tiled=True)  79.6 us
  transfers between devices with their start and end apart: 33, of which 31 were waited for; matrix products, arithmetic and copies ran while one was open for 19% of the time, Pallas kernels for 0%

commit v1 on v0

v1 whole, which is shorter than its diff:
```python
import functools

import jax
import jax.numpy as jnp
from jax import lax
from jax.experimental import pallas as pl
from jax.experimental.pallas import tpu as pltpu
from jax.sharding import PartitionSpec as P

HEAD = 64
KERNEL = 31
LEFT = 64
RIGHT = 8
EPSILON = 1e-05
MASKED = -1e30
BLK = 128
SPAN = 512
NT = (((1,), (1,)), ((), ()))
TN = (((0,), (0,)), ((), ()))


def dot_nt(a, b):
    return lax.dot_general(a, b, NT, preferred_element_type=jnp.float32)


def dot_tn(a, b):
    return lax.dot_general(a, b, TN, preferred_element_type=jnp.float32)


def dot_nn(a, b):
    return jnp.dot(a, b, preferred_element_type=jnp.float32)


def rel_blocks(tin, b, own_blocks, key_blocks, rank):
    t_left, t_right = tin[:, 0:1], tin[:, SPAN - 1 : SPAN]
    band = pltpu.roll(tin, SPAN - BLK, 1, stride=1, stride_axis=0)
    out = []
    for kb in range(key_blocks):
        wraps = rank * own_blocks + kb >= key_blocks
        if kb in (b - 1, b) or (kb == b + 1 and kb < own_blocks):
            out.append(band[:, (kb - b + 1) * BLK : (kb - b + 2) * BLK])
        elif kb == b + 1:
            out.append(jnp.where(wraps, t_left, band[:, 2 * BLK : 3 * BLK]))
        elif b == 0 and kb == key_blocks - 1:
            out.append(jnp.where(wraps, band[:, :BLK], t_right))
        elif kb < b - 1:
            out.append(t_left)
        elif kb < own_blocks:
            out.append(t_right)
        else:
            out.append(jnp.where(wraps, t_left, t_right))
    return out


def halves(x):
    low = lax.broadcasted_iota(jnp.int32, x.shape, 1) < HEAD
    zero = jnp.zeros_like(x)
    return jnp.where(low, x, zero), jnp.where(low, zero, x)


def flip_rows(x):
    tiles = []
    back = 7 - lax.broadcasted_iota(jnp.int32, (8, BLK), 0)
    for first in range(x.shape[0] - 8, -1, -8):
        cols = [
            jnp.take_along_axis(x[first : first + 8, c : c + BLK], back, axis=0, mode="promise_in_bounds")
            for c in range(0, x.shape[1], BLK)
        ]
        tiles.append(jnp.concatenate(cols, axis=1) if len(cols) > 1 else cols[0])
    return jnp.concatenate(tiles, axis=0)


def attn_fwd_kernel(rank_ref, q_ref, k_ref, v_ref, tab_ref, mask_ref, o_ref, lse_ref):
    rank = rank_ref[0]
    rows, keys = q_ref.shape[0], k_ref.shape[0]
    own_blocks, key_blocks = rows // BLK, keys // BLK
    low = lax.broadcasted_iota(jnp.int32, (BLK, 2 * HEAD), 1) < HEAD
    for b in range(own_blocks):
        q_blk = q_ref[b * BLK : (b + 1) * BLK, :] * jnp.asarray(HEAD**-0.5, jnp.bfloat16)
        results = []
        for hh, q_one in enumerate(halves(q_blk)):
            tin = dot_nt(q_one, tab_ref[...])
            rel = rel_blocks(tin, b, own_blocks, key_blocks, rank)
            raw = dot_nt(q_one, k_ref[...])
            s = [
                raw[:, kb * BLK : (kb + 1) * BLK] + rel[kb] + mask_ref[:, kb * BLK : (kb + 1) * BLK]
                for kb in range(key_blocks)
            ]
            s = jnp.concatenate(s, axis=1)
            peak = jnp.max(s, axis=-1, keepdims=True)
            e = jnp.exp(s - peak)
            total = jnp.sum(e, axis=-1, keepdims=True)
            o = dot_nn(e.astype(jnp.bfloat16), v_ref[...])
            results.append(o / total)
            first = (hh * own_blocks + b) * BLK
            lse_ref[0, first : first + BLK, :] = peak + jnp.log(total)
        o_ref[b * BLK : (b + 1) * BLK, :] = jnp.where(low, results[0], results[1]).astype(jnp.bfloat16)


def attn_fwd(rank, q, k, v, tab2, mask):
    rows, width = q.shape
    keys = k.shape[0]
    pairs = width // (2 * HEAD)
    col = lambda n: pl.BlockSpec((n, 2 * HEAD), lambda p, r: (0, p))
    return pl.pallas_call(
        attn_fwd_kernel,
        grid_spec=pltpu.PrefetchScalarGridSpec(
            num_scalar_prefetch=1,
            grid=(pairs,),
            in_specs=[
                col(rows),
                col(keys),
                col(keys),
                pl.BlockSpec((SPAN, 2 * HEAD), lambda p, r: (0, 0)),
                pl.BlockSpec((1, keys), lambda p, r: (0, 0)),
            ],
            out_specs=[col(rows), pl.BlockSpec((1, 2 * rows, 1), lambda p, r: (p, 0, 0))],
        ),
        out_shape=[
            jax.ShapeDtypeStruct((rows, width), jnp.bfloat16),
            jax.ShapeDtypeStruct((pairs, 2 * rows, 1), jnp.float32),
        ],
        name="attn_fwd",
    )(rank, q, k, v, tab2, mask)


def attn_bwd_kernel(
    rank_ref, q_ref, k_ref, v_ref, do_ref, o_ref, lse_ref, tab_ref, mask_ref,
    dq_ref, dk_ref, dv_ref, dtab_ref, p_sc, ds_sc, q_sc, do_sc,
):
    rank = rank_ref[0]
    rows, keys = q_ref.shape[0], k_ref.shape[0]
    own_blocks, key_blocks = rows // BLK, keys // BLK
    low = lax.broadcasted_iota(jnp.int32, (BLK, 2 * HEAD), 1) < HEAD
    lane = lax.broadcasted_iota(jnp.int32, (BLK, BLK), 1)
    scale = jnp.asarray(HEAD**-0.5, jnp.bfloat16)

    @pl.when(pl.program_id(0) == 0)
    def _():
        dtab_ref[...] = jnp.zeros_like(dtab_ref)

    for b in range(own_blocks):
        at = slice(b * BLK, (b + 1) * BLK)
        q_blk = q_ref[at, :] * scale
        do_blk = do_ref[at, :]
        prod = do_blk.astype(jnp.float32) * o_ref[at, :].astype(jnp.float32)
        q_back = halves(flip_rows(q_blk.astype(jnp.float32)).astype(jnp.bfloat16))
        results = []
        for hh, (q_one, do_one, pr_one) in enumerate(zip(halves(q_blk), halves(do_blk), halves(prod))):
            first = (hh * own_blocks + b) * BLK
            here = slice(first, first + BLK)
            inner = jnp.sum(pr_one, axis=-1, keepdims=True)
            lse = lse_ref[0, here, :]
            tin = dot_nt(q_one, tab_ref[...])
            rel = rel_blocks(tin - lse, b, own_blocks, key_blocks, rank)
            raw = dot_nt(q_one, k_ref[...])
            dp = dot_nt(do_one, v_ref[...])
            left = jnp.zeros((BLK, BLK), jnp.float32)
            right = jnp.zeros((BLK, BLK), jnp.float32)
            window = [None, None, None]
            for kb in range(key_blocks):
                ks = slice(kb * BLK, (kb + 1) * BLK)
                p = jnp.exp(raw[:, ks] + rel[kb] + mask_ref[:, ks])
                ds = (p * (dp[:, ks] - inner)).astype(jnp.bfloat16)
                p_sc[here, ks] = p.astype(jnp.bfloat16)
                ds_sc[here, ks] = ds
                ds = ds.astype(jnp.float32)
                wraps = rank * own_blocks + kb >= key_blocks
                zero = jnp.zeros_like(ds)
                if kb in (b - 1, b) or (kb == b + 1 and kb < own_blocks):
                    window[kb - b + 1] = ds
                elif kb == b + 1:
                    window[2] = jnp.where(wraps, zero, ds)
                    left = left + jnp.where(wraps, ds, zero)
                elif b == 0 and kb == key_blocks - 1:
                    window[0] = jnp.where(wraps, ds, zero)
                    right = right + jnp.where(wraps, zero, ds)
                elif kb < b - 1:
                    left = left + ds
                elif kb < own_blocks:
                    right = right + ds
                else:
                    left = left + jnp.where(wraps, ds, zero)
                    right = right + jnp.where(wraps, zero, ds)
            none = jnp.zeros((BLK, BLK), jnp.float32)
            window = jnp.concatenate([none if w is None else flip_rows(w) for w in window] + [none], axis=1)
            back = pltpu.roll(window, 1, 1, stride=1, stride_axis=0)
            s_left = flip_rows(jnp.broadcast_to(jnp.sum(left, axis=-1, keepdims=True), (BLK, BLK)))
            s_right = flip_rows(jnp.broadcast_to(jnp.sum(right, axis=-1, keepdims=True), (BLK, BLK)))
            u = jnp.concatenate(
                [
                    back[:, :BLK] + jnp.where(lane == 0, s_left, 0.0),
                    back[:, BLK : 3 * BLK],
                    back[:, 3 * BLK :] + jnp.where(lane == BLK - 1, s_right, 0.0),
                ],
                axis=1,
            ).astype(jnp.bfloat16)
            q_sc[here, :] = q_one
            do_sc[here, :] = do_one
            dtab_ref[...] += dot_tn(u, q_back[hh])
            results.append(dot_nn(ds_sc[here, :], k_ref[...]) + flip_rows(dot_nn(u, tab_ref[...])))
        dq_ref[at, :] = (jnp.where(low, results[0], results[1]) * HEAD**-0.5).astype(jnp.bfloat16)
    dk_ref[...] = dot_tn(ds_sc[...], q_sc[...]).astype(dk_ref.dtype)
    dv_ref[...] = dot_tn(p_sc[...], do_sc[...]).astype(dv_ref.dtype)


def attn_bwd(rank, q, k, v, do, o, lse, tab2, mask):
    rows, width = q.shape
    keys = k.shape[0]
    pairs = width // (2 * HEAD)
    col = lambda n: pl.BlockSpec((n, 2 * HEAD), lambda p, r: (0, p))
    return pl.pallas_call(
        attn_bwd_kernel,
        grid_spec=pltpu.PrefetchScalarGridSpec(
            num_scalar_prefetch=1,
            grid=(pairs,),
            in_specs=[
                col(rows),
                col(keys),
                col(keys),
                col(rows),
                col(rows),
                pl.BlockSpec((1, 2 * rows, 1), lambda p, r: (p, 0, 0)),
                pl.BlockSpec((SPAN, 2 * HEAD), lambda p, r: (0, 0)),
                pl.BlockSpec((1, keys), lambda p, r: (0, 0)),
            ],
            out_specs=[col(rows), col(keys), col(keys), pl.BlockSpec((SPAN, 2 * HEAD), lambda p, r: (0, 0))],
            scratch_shapes=[
                pltpu.VMEM((2 * rows, keys), jnp.bfloat16),
                pltpu.VMEM((2 * rows, keys), jnp.bfloat16),
                pltpu.VMEM((2 * rows, 2 * HEAD), jnp.bfloat16),
                pltpu.VMEM((2 * rows, 2 * HEAD), jnp.bfloat16),
            ],
        ),
        out_shape=[
            jax.ShapeDtypeStruct((rows, width), jnp.bfloat16),
            jax.ShapeDtypeStruct((keys, width), jnp.bfloat16),
            jax.ShapeDtypeStruct((keys, width), jnp.bfloat16),
            jax.ShapeDtypeStruct((SPAN, 2 * HEAD), jnp.float32),
        ],
        name="attn_bwd",
    )(rank, q, k, v, do, o, lse, tab2, mask)


def span_table(rel_table):
    rows = jnp.clip(jnp.arange(SPAN) - SPAN // 2, -LEFT, RIGHT) + LEFT
    table = jnp.take(rel_table, rows, axis=0)
    return jnp.concatenate([table, table], axis=1)


def fold_table(dtab):
    one = dtab[:, :HEAD] + dtab[:, HEAD:]
    rows = jnp.clip(jnp.arange(SPAN) - SPAN // 2, -LEFT, RIGHT) + LEFT
    pick = (rows[None, :] == jnp.arange(LEFT + RIGHT + 1)[:, None]).astype(jnp.float32)
    return jnp.dot(pick, one, precision=lax.Precision.HIGHEST)


MESH = pl.DeviceIdType.MESH
ANY = pl.BlockSpec(memory_space=pl.ANY)
VMEM = pl.BlockSpec(memory_space=pltpu.VMEM)
FACTORS = {16: (4, 2, 2), 32: (4, 2, 4)}


class Place:
    def __init__(self, dims, n_tensor):
        self.dims, self.n_tensor = dims, n_tensor
        n_a, n_b, n_c = dims
        d = lax.axis_index("dp")
        self.t = lax.axis_index("tensor")
        self.at = (lax.div(d, n_b * n_c), lax.rem(lax.div(d, n_c), n_b), lax.rem(d, n_c))

    def peer(self, axis, step):
        at, t = list(self.at), self.t
        if axis == 3:
            t = lax.rem(t + step, self.n_tensor)
            index = t
        else:
            at[axis] = index = lax.rem(at[axis] + step, self.dims[axis])
        n_a, n_b, n_c = self.dims
        return ((at[0] * n_b + at[1]) * n_c + at[2], t), index

    def size(self, axis):
        return self.n_tensor if axis == 3 else self.dims[axis]

    def barrier(self, axes=(0, 1, 2, 3)):
        sem = pltpu.get_barrier_semaphore()
        count = 0
        for axis in axes:
            for step in range(1, self.size(axis)):
                pl.semaphore_signal(sem, inc=1, device_id=self.peer(axis, step)[0], device_id_type=MESH)
                count += 1
        pl.semaphore_wait(sem, count)


def remote(src, dst, send_sem, recv_sem, device):
    return pltpu.make_async_remote_copy(
        src_ref=src, dst_ref=dst, send_sem=send_sem, recv_sem=recv_sem, device_id=device, device_id_type=MESH
    )


class Gather:
    ORDERS = ((0, 1, 2), (0, 2, 1))

    def __init__(self, place, shard, whole, send, recv, local):
        self.place, self.shard, self.whole = place, shard, whole
        self.send, self.recv, self.local = send, recv, local
        self.half = shard.shape[1] // 2
        self.width = shard.shape[2]

    @staticmethod
    def slots(dims, n_tensor):
        return sum(d - 1 for d in dims) + 2 * (n_tensor - 1)

    def slot(self, color, stage, step):
        dims = self.place.dims
        base = [0]
        for axis in self.ORDERS[color]:
            base.append(base[-1] + dims[axis] - 1)
        base.append(base[-1] + self.place.n_tensor - 1)
        return (color, base[stage] + step - 1)

    def region(self, color, index, t):
        cols = pl.ds(pl.multiple_of(t * self.width, 128), self.width)
        return self.whole.at[(slice(None),) + tuple(index) + (pl.ds(color * self.half, self.half), cols)]

    def index(self, color, stage, moved=None):
        order, out = self.ORDERS[color], list(self.place.at)
        for axis in order[:stage]:
            out[axis] = slice(None)
        if moved is not None:
            out[order[stage]] = moved
        return out

    def own(self):
        cols = pl.ds(pl.multiple_of(self.place.t * self.width, 128), self.width)
        there = self.whole.at[(slice(None),) + self.place.at + (slice(None), cols)]
        return pltpu.make_async_copy(self.shard, there, self.local)

    def copies(self, stage, arriving=False):
        place = self.place
        for color in (0, 1):
            order = self.ORDERS[color]
            axis = order[stage] if stage < 3 else 3
            for step in range(1, place.size(axis)):
                device, peer = place.peer(axis, step)
                _, source = place.peer(axis, place.size(axis) - step)
                slot = self.slot(color, stage, step)
                sems = (self.send.at[slot], self.recv.at[slot])
                t = place.t
                if stage < 3:
                    mine = self.region(color, self.index(color, stage), t)
                    theirs = self.region(color, self.index(color, stage, source), t)
                elif stage == 3:
                    mine = self.region(color, self.index(color, 2), t)
                    theirs = self.region(color, self.index(color, 2), source)
                elif self.skip(3):
                    mine = self.region(color, self.index(color, 3), t)
                    theirs = self.region(color, self.index(color, 3), source)
                else:
                    index = self.index(color, 2, place.peer(order[2], 1)[1])
                    mine = self.region(color, index, t)
                    theirs = self.region(color, index, source)
                if stage == 0:
                    mine_src = self.shard.at[:, pl.ds(color * self.half, self.half), :]
                else:
                    mine_src = mine
                if arriving:
                    yield remote(theirs, theirs, *sems, device)
                else:
                    yield remote(mine_src, mine, *sems, device)

    def start(self, stage):
        if self.skip(stage):
            return
        for copy in self.copies(stage):
            copy.start()

    def skip(self, stage):
        return stage == 3 and max(self.place.dims[1:]) > 2

    def arrived(self, stage):
        if self.skip(stage):
            return
        for copy in self.copies(stage, arriving=True):
            copy.wait_recv()

    def sent(self, stage):
        if self.skip(stage):
            return
        for copy in self.copies(stage):
            copy.wait_send()


def gather_kernel(dims, n_tensor, n, *refs):
    shards, wholes = refs[:n], refs[n : 2 * n]
    send, recv, local = refs[2 * n :]
    place = Place(dims, n_tensor)
    gathers = [
        Gather(place, s, w, send.at[i], recv.at[i], local.at[i]) for i, (s, w) in enumerate(zip(shards, wholes))
    ]
    for g in gathers:
        g.own().start()
    place.barrier()
    for g in gathers:
        g.start(0)
    for g in gathers:
        g.own().wait()
    for step in range(n + 2):
        if step < n:
            gathers[step].arrived(0)
            gathers[step].start(1)
        if 0 <= step - 1 < n:
            gathers[step - 1].arrived(1)
            gathers[step - 1].start(2)
            gathers[step - 1].start(3)
        if 0 <= step - 2 < n:
            gathers[step - 2].arrived(2)
            gathers[step - 2].start(4)
    for g in gathers:
        for stage in (3, 4):
            g.arrived(stage)
        for stage in range(5):
            g.sent(stage)


def gather_weights(shards, dims, n_tensor, collective_id):
    n = len(shards)
    n_a, n_b, n_c = dims
    slots = Gather.slots(dims, n_tensor)
    outs = pl.pallas_call(
        functools.partial(gather_kernel, dims, n_tensor, n),
        out_shape=[
            jax.ShapeDtypeStruct((s.shape[0], n_a, n_b, n_c, s.shape[1], n_tensor * s.shape[2]), s.dtype) for s in shards
        ],
        in_specs=[VMEM] * n,
        out_specs=[ANY] * n,
        scratch_shapes=[
            pltpu.SemaphoreType.DMA((n, 2, slots)),
            pltpu.SemaphoreType.DMA((n, 2, slots)),
            pltpu.SemaphoreType.DMA((n,)),
        ],
        compiler_params=pltpu.CompilerParams(collective_id=collective_id, has_side_effects=True),
        name="gather_weights",
    )(*shards)
    return [o.reshape(o.shape[0], -1, o.shape[-1]) for o in outs]


class Piece:
    def __init__(self, source, lead, first, width):
        self.source, self.lead, self.first, self.width = source, lead, first, width


def pieces_of(shapes, n_tensor, chunk):
    chunks, room = [], 0
    for source, (n, _, cols) in enumerate(shapes):
        cols //= n_tensor
        for lead in range(n):
            first = 0
            while first < cols:
                width = min(cols - first, chunk if room == 0 else room)
                if room == 0:
                    chunks.append([])
                    room = chunk
                chunks[-1].append(Piece(source, lead, first, width))
                room -= width
                first += width
    return chunks


class Scatter:
    ORDERS = ((2, 1, 0), (1, 2, 0))

    def __init__(self, place, pieces, grads, outs, bufs, sems):
        self.place, self.pieces, self.grads, self.outs = place, pieces, grads, outs
        self.held, self.far, self.near, self.first, self.second, self.third = bufs
        self.send, self.recv, self.local = sems
        self.width = sum(p.width for p in pieces)
        self.half = self.held.shape[3] // 2

    def rows(self, color):
        return pl.ds(color * self.half, self.half)

    def slab(self, piece, t):
        cols = pl.ds(pl.multiple_of(t * (self.grads[piece.source].shape[-1] // self.place.n_tensor) + piece.first, 128), piece.width)
        return self.grads[piece.source].at[piece.lead, :, :, :, :, cols]

    def columns(self):
        at = 0
        for number, piece in enumerate(self.pieces):
            yield number, piece, pl.ds(at, piece.width)
            at += piece.width

    def loads(self):
        for number, piece, cols in self.columns():
            yield pltpu.make_async_copy(self.slab(piece, self.place.t), self.held.at[:, :, :, :, cols], self.local.at[number])

    def tensor_copies(self):
        for step in range(1, self.place.n_tensor):
            device, peer = self.place.peer(3, step)
            for number, piece, cols in self.columns():
                slot = (step - 1) * 2 + number
                yield remote(
                    self.slab(piece, peer), self.far.at[step - 1, :, :, :, :, cols], self.send.at[slot], self.recv.at[slot], device
                )

    def near_loads(self, slot):
        for step in range(1, self.place.n_tensor):
            yield pltpu.make_async_copy(
                self.far.at[step - 1, :, :, :, :, pl.ds(0, self.width)],
                self.near.at[slot, step - 1, :, :, :, :, pl.ds(0, self.width)],
                self.local.at[1 + step],
            )

    def copies(self, stage):
        place = self.place
        base = 2 * (place.n_tensor - 1)
        cols = pl.ds(0, self.width)
        for color in (0, 1):
            order = self.ORDERS[color]
            axis = order[stage - 1]
            for step in range(1, place.size(axis)):
                device, there = place.peer(axis, step)
                index = [slice(None)] * 3
                for done in order[: stage - 1]:
                    index[done] = place.at[done]
                index[axis] = there
                buf = (self.first, self.second, self.third)[stage - 1][color]
                slot = base + sum(place.size(x) - 1 for x in order[: stage - 1]) + step - 1 + color * sum(d - 1 for d in place.dims)
                whole = (slice(None),) * (len(buf.shape) - 2)
                yield remote(
                    self.held.at[tuple(index) + (self.rows(color), cols)],
                    buf.at[(step - 1,) + whole[1:] + (slice(None), cols)],
                    self.send.at[slot],
                    self.recv.at[slot],
                    device,
                )

    @staticmethod
    def slots(dims, n_tensor):
        return 2 * (n_tensor - 1) + 2 * sum(d - 1 for d in dims)

    def add_tensor(self, slot):
        n_a, n_b, n_c = self.place.dims
        cols = slice(0, self.width)

        def body(i, _):
            at = (lax.div(i, n_b * n_c), lax.rem(lax.div(i, n_c), n_b), lax.rem(i, n_c))
            total = self.held[at + (slice(None), cols)].astype(jnp.float32)
            for step in range(1, self.place.n_tensor):
                total = total + self.near[(slot, step - 1) + at + (slice(None), cols)].astype(jnp.float32)
            self.held[at + (slice(None), cols)] = total.astype(jnp.bfloat16)
            return 0

        lax.fori_loop(0, n_a * n_b * n_c, body, 0)

    def add(self, stage):
        place = self.place
        cols = slice(0, self.width)
        for color in (0, 1):
            order = self.ORDERS[color]
            rows = slice(color * self.half, (color + 1) * self.half)
            left = [x for x in (0, 1, 2) if x not in order[:stage]]
            buf = (self.first, self.second)[stage - 1][color]
            count = 1
            for x in left:
                count *= place.dims[x]

            def body(i, _):
                at = list(place.at)
                if len(left) == 2:
                    where = (lax.div(i, place.dims[left[1]]), lax.rem(i, place.dims[left[1]]))
                else:
                    where = (i,)
                for x, w in zip(left, where):
                    at[x] = w
                at = tuple(at) + (rows, cols)
                total = self.held[at].astype(jnp.float32)
                for step in range(1, place.size(order[stage - 1])):
                    total = total + buf[(step - 1,) + where + (slice(None), cols)].astype(jnp.float32)
                self.held[at] = total.astype(jnp.bfloat16)
                return 0

            lax.fori_loop(0, count, body, 0)

    def finish(self):
        for _, piece, cols in self.columns():
            cols = slice(cols.start, cols.start + cols.size)
            for color in (0, 1):
                rows = slice(color * self.half, (color + 1) * self.half)
                total = self.held[self.place.at + (rows, cols)].astype(jnp.float32)
                for step in range(1, self.place.dims[0]):
                    total = total + self.third[color][step - 1, :, cols].astype(jnp.float32)
                self.outs[piece.source][piece.lead, rows, piece.first : piece.first + piece.width] = total


class Total:
    AXES = (3, 2, 1, 0)

    def __init__(self, place, value, out, boxes, send, recv):
        self.place, self.value, self.out, self.boxes, self.send, self.recv = place, value, out, boxes, send, recv

    @staticmethod
    def slots(dims, n_tensor):
        return sum(dims) + n_tensor - 4

    def copies(self, stage):
        place, axis = self.place, self.AXES[stage]
        base = sum(place.size(x) - 1 for x in self.AXES[:stage])
        for step in range(1, place.size(axis)):
            device, _ = place.peer(axis, step)
            slot = base + step - 1
            yield remote(self.value.at[stage], self.boxes[stage].at[step - 1], self.send.at[slot], self.recv.at[slot], device)

    def add(self, stage):
        place, axis = self.place, self.AXES[stage]
        size = place.size(axis)
        mine = place.t if axis == 3 else place.at[axis]
        own = self.value[stage]
        if size == 2:
            total = own + self.boxes[stage][0]
        else:
            total = jnp.zeros_like(own)
            for index in range(size):
                step = lax.rem(mine - index + size, size)
                term = self.boxes[stage][jnp.maximum(step - 1, 0)]
                total = total + jnp.where(step == 0, own, term)
        if stage == 3:
            self.out[...] = total
        else:
            self.value[stage + 1] = total


def scatter_kernel(dims, n_tensor, plan, n, has_total, *refs):
    count = len(plan)
    refs = list(refs)
    take = lambda k: [refs.pop(0) for _ in range(k)]
    grads = take(n)
    vec = take(1)[0] if has_total else None
    outs = take(n)
    vec_out = take(1)[0] if has_total else None
    (far,) = take(1)
    held, near, x0, x1, y0, y1, z0, z1, send, recv, local = take(11)
    place = Place(dims, n_tensor)
    chunks = [
        Scatter(
            place, pieces, grads, outs,
            (held.at[i], far.at[i], near, (x0.at[i], x1.at[i]), (y0.at[i], y1.at[i]), (z0.at[i], z1.at[i])),
            (send.at[i], recv.at[i], local.at[i]),
        )
        for i, pieces in enumerate(plan)
    ]
    for c in chunks:
        for copy in c.loads():
            copy.start()
    total = None
    if has_total:
        value, *rest = take(7)
        total = Total(place, value, vec_out, rest[:4], rest[4], rest[5])
        value[0] = vec[...]
    place.barrier()
    if total is not None:
        for copy in total.copies(0):
            copy.start()
    for c in chunks:
        for copy in c.tensor_copies():
            copy.start()

    def fetch(i):
        for copy in chunks[i].tensor_copies():
            copy.wait_recv()
        for copy in chunks[i].near_loads(i % 2):
            copy.start()

    fetch(0)
    for step in range(max(count + 3, 4 if has_total else 0)):
        if step < count:
            c = chunks[step]
            for copy in c.loads():
                copy.wait()
            for copy in c.near_loads(step % 2):
                copy.wait()
            if step + 1 < count:
                fetch(step + 1)
            c.add_tensor(step % 2)
            for copy in c.copies(1):
                copy.start()
        for stage in (1, 2):
            at = step - stage
            if 0 <= at < count:
                for copy in chunks[at].copies(stage):
                    copy.wait_recv()
                chunks[at].add(stage)
                for copy in chunks[at].copies(stage + 1):
                    copy.start()
        if 0 <= step - 3 < count:
            for copy in chunks[step - 3].copies(3):
                copy.wait_recv()
            chunks[step - 3].finish()
        if total is not None and step < 4:
            for copy in total.copies(step):
                copy.wait_recv()
            total.add(step)
            if step < 3:
                for copy in total.copies(step + 1):
                    copy.start()
    for c in chunks:
        for copy in c.tensor_copies():
            copy.wait_send()
        for stage in (1, 2, 3):
            for copy in c.copies(stage):
                copy.wait_send()
    if total is not None:
        for stage in range(4):
            for copy in total.copies(stage):
                copy.wait_send()


def scatter_grads(grads, vec, dims, n_tensor, collective_id, chunk=1024):
    n_a, n_b, n_c = dims
    places = n_a * n_b * n_c
    rows = grads[0].shape[1] // places
    plan = pieces_of([g.shape for g in grads], n_tensor, chunk)
    count = len(plan)
    chunk = max(sum(p.width for p in pieces) for pieces in plan)
    views = [g.reshape(g.shape[0], n_a, n_b, n_c, rows, g.shape[2]) for g in grads]
    n = len(grads)
    half = rows // 2
    bf = jnp.bfloat16
    slots = Scatter.slots(dims, n_tensor)
    out_shape = [jax.ShapeDtypeStruct((g.shape[0], rows, g.shape[2] // n_tensor), jnp.float32) for g in grads]
    out_specs = [VMEM] * n
    scratch = [
        pltpu.VMEM((count, n_a, n_b, n_c, rows, chunk), bf),
        pltpu.VMEM((2, n_tensor - 1, n_a, n_b, n_c, rows, chunk), bf),
        pltpu.VMEM((count, n_c - 1, n_a, n_b, half, chunk), bf),
        pltpu.VMEM((count, n_b - 1, n_a, n_c, half, chunk), bf),
        pltpu.VMEM((count, n_b - 1, n_a, half, chunk), bf),
        pltpu.VMEM((count, n_c - 1, n_a, half, chunk), bf),
        pltpu.VMEM((count, n_a - 1, half, chunk), bf),
        pltpu.VMEM((count, n_a - 1, half, chunk), bf),
        pltpu.SemaphoreType.DMA((count, slots)),
        pltpu.SemaphoreType.DMA((count, slots)),
        pltpu.SemaphoreType.DMA((count, 1 + n_tensor)),
    ]
    args, in_specs = list(views), [ANY] * n
    has_total = vec is not None
    if has_total:
        args.append(vec)
        in_specs.append(VMEM)
        out_shape.append(jax.ShapeDtypeStruct(vec.shape, vec.dtype))
        out_specs.append(VMEM)
        box = lambda k: pltpu.VMEM((k - 1,) + vec.shape, vec.dtype)
        t_slots = Total.slots(dims, n_tensor)
        scratch += [pltpu.VMEM((4,) + vec.shape, vec.dtype), box(n_tensor), box(n_c), box(n_b), box(n_a)]
        scratch += [pltpu.SemaphoreType.DMA((t_slots,)), pltpu.SemaphoreType.DMA((t_slots,))]
    out_shape.append(jax.ShapeDtypeStruct((count, n_tensor - 1, n_a, n_b, n_c, rows, chunk), bf))
    out_specs.append(ANY)
    outs = pl.pallas_call(
        functools.partial(scatter_kernel, dims, n_tensor, plan, n, has_total),
        out_shape=out_shape,
        in_specs=in_specs,
        out_specs=out_specs,
        scratch_shapes=scratch,
        compiler_params=pltpu.CompilerParams(
            collective_id=collective_id, has_side_effects=True, vmem_limit_bytes=66_000_000
        ),
        name="scatter_grads",
    )(*args)
    return outs[:n], (outs[n] if has_total else None)


def exchange_kernel(dims, n_tensor, n, *refs):
    ins, outs = refs[:n], refs[n : 2 * n]
    send, recv, local = refs[2 * n :]
    place = Place(dims, n_tensor)

    def copies(i):
        for step in range(1, n_tensor):
            device, _ = place.peer(3, step)
            sems = (send.at[i, step - 1], recv.at[i, step - 1])
            yield remote(ins[i], outs[i].at[n_tensor - step], *sems, device)

    own = [pltpu.make_async_copy(ins[i], outs[i].at[0], local.at[i]) for i in range(n)]
    for copy in own:
        copy.start()
    place.barrier((3,))
    for i in range(n):
        for copy in copies(i):
            copy.start()
    for i in range(n):
        own[i].wait()
        for copy in copies(i):
            copy.wait()


def exchange_rows(arrays, dims, n_tensor, collective_id):
    n = len(arrays)
    outs = pl.pallas_call(
        functools.partial(exchange_kernel, dims, n_tensor, n),
        out_shape=[jax.ShapeDtypeStruct((n_tensor,) + a.shape, a.dtype) for a in arrays],
        in_specs=[VMEM] * n,
        out_specs=[ANY] * n,
        scratch_shapes=[
            pltpu.SemaphoreType.DMA((n, n_tensor - 1)),
            pltpu.SemaphoreType.DMA((n, n_tensor - 1)),
            pltpu.SemaphoreType.DMA((n,)),
        ],
        compiler_params=pltpu.CompilerParams(collective_id=collective_id, has_side_effects=True),
        name="exchange_rows",
    )(*arrays)
    return [o.reshape(-1, o.shape[-1]) for o in outs]


def return_kernel(dims, n_tensor, n, *refs):
    ins, outs, bufs = refs[:n], refs[n : 2 * n], refs[2 * n : 3 * n]
    send, recv = refs[3 * n :]
    place = Place(dims, n_tensor)
    rows = outs[0].shape[0]

    def copies(i):
        for step in range(1, n_tensor):
            device, _ = place.peer(3, step)
            sems = (send.at[i, step - 1], recv.at[i, step - 1])
            yield remote(ins[i].at[pl.ds(step * rows, rows), :], bufs[i].at[step - 1], *sems, device)

    place.barrier((3,))
    for i in range(n):
        for copy in copies(i):
            copy.start()
    for i in range(n):
        for copy in copies(i):
            copy.wait()
        for first in range(0, rows, 64):
            total = ins[i][first : first + 64, :].astype(jnp.float32)
            for step in range(1, n_tensor):
                total = total + bufs[i][step - 1, first : first + 64, :].astype(jnp.float32)
            outs[i][first : first + 64, :] = total.astype(outs[i].dtype)


def return_rows(arrays, dims, n_tensor, collective_id):
    n = len(arrays)
    rows, width = arrays[0].shape[0] // n_tensor, arrays[0].shape[1]
    return pl.pallas_call(
        functools.partial(return_kernel, dims, n_tensor, n),
        out_shape=[jax.ShapeDtypeStruct((rows, width), a.dtype) for a in arrays],
        in_specs=[VMEM] * n,
        out_specs=[VMEM] * n,
        scratch_shapes=[pltpu.VMEM((n_tensor - 1, rows, width), a.dtype) for a in arrays]
        + [pltpu.SemaphoreType.DMA((n, n_tensor - 1)), pltpu.SemaphoreType.DMA((n, n_tensor - 1))],
        compiler_params=pltpu.CompilerParams(collective_id=collective_id, has_side_effects=True),
        name="return_rows",
    )(*arrays)


def norm_forward(stream, gain_row, shift_row):
    centered = stream - jnp.mean(stream, axis=-1, keepdims=True)
    inv_std = lax.rsqrt(jnp.mean(centered * centered, axis=-1, keepdims=True) + EPSILON)
    normed = centered * inv_std
    return (normed * gain_row + shift_row, normed, inv_std)


def norm_backward(grad_result, normed, inv_std, gain_row):
    grad_normed = grad_result * gain_row
    return inv_std * (
        grad_normed
        - jnp.mean(grad_normed, axis=-1, keepdims=True)
        - normed * jnp.mean(grad_normed * normed, axis=-1, keepdims=True)
    )


def low(value):
    return value.astype(jnp.bfloat16)


def ffn_forward(entered, weight_in, weight_out_t):
    before = dot_nn(entered, weight_in)
    active = low(jax.nn.silu(before))
    return dot_nt(active, weight_out_t), (before, active)


def ffn_backward(entered, saved, grad_low, weight_in, weight_out_t):
    before, active = saved
    sigma = jax.nn.sigmoid(before)
    grad_active = dot_nn(grad_low, weight_out_t)
    grad_before = low(grad_active * sigma * (1.0 + before * (1.0 - sigma)))
    grad_in = low(dot_tn(entered, grad_before))
    grad_out_t = low(dot_tn(grad_low, active))
    return dot_nt(grad_before, weight_in), grad_in, grad_out_t


def taps_forward(signal, before, conv_taps):
    rows = signal.shape[0]
    padded = jnp.concatenate([before, signal], axis=0)
    skip = before.shape[0] - (KERNEL - 1)
    result = jnp.zeros_like(signal)
    for tap in range(KERNEL):
        result = result + conv_taps[tap] * padded[skip + tap : skip + tap + rows]
    return result


def taps_backward(grad, after, signal, before, conv_taps):
    rows = signal.shape[0]
    padded_signal = jnp.concatenate([before, signal], axis=0)
    padded_grad = jnp.concatenate([grad, after], axis=0)
    skip = before.shape[0] - (KERNEL - 1)
    grad_signal = jnp.zeros_like(signal)
    taps = []
    for tap in range(KERNEL):
        back = KERNEL - 1 - tap
        grad_signal = grad_signal + conv_taps[tap] * padded_grad[back : back + rows]
        taps.append(jnp.sum(grad * padded_signal[skip + tap : skip + tap + rows], axis=0))
    return grad_signal, jnp.stack(taps)


HALO = 32


def on_device(
    dims,
    n_tensor,
    stream_in,
    grad_out,
    clip_lengths,
    first_up,
    first_down,
    attn_proj,
    attn_out,
    rel_table,
    glu_weight,
    conv_taps,
    conv_out,
    second_up,
    second_down,
    norm_gains,
    norm_shifts,
):
    rank = lax.axis_index("tensor")
    rows, width = stream_in.shape
    keys = rows * n_tensor
    shards = [
        first_up[None], first_down.T[None], attn_proj, attn_out.T[None],
        glu_weight, conv_out.T[None], second_up[None], second_down.T[None],
    ]
    gathered = gather_weights(shards, dims, n_tensor, 0)
    (up_one,), (down_one,), proj, (out_attn,), glu, (out_conv,), (up_two,), (down_two,) = gathered

    def enter(stream, row):
        result, normed, inv_std = norm_forward(stream, norm_gains[row], norm_shifts[row])
        return low(result), (normed, inv_std)

    def norm_back(grad_result, saved, row):
        normed, inv_std = saved
        grad_input = norm_backward(grad_result, normed, inv_std, norm_gains[row])
        return grad_input, jnp.sum(grad_result * normed, axis=0), jnp.sum(grad_result, axis=0)

    def shift_rank(value, step):
        pairs = [(i, i + step) for i in range(n_tensor) if 0 <= i + step < n_tensor]
        return lax.ppermute(value, "tensor", pairs)

    stream = stream_in.astype(jnp.float32)
    squares = []

    entered_a, norm_a = enter(stream, 0)
    branch, ffn_a = ffn_forward(entered_a, up_one, down_one)
    squares.append(jnp.sum(branch * branch))
    stream = stream + 0.5 * branch

    entered_b, norm_b = enter(stream, 1)
    query, own_keys, own_vals = (low(dot_nn(entered_b, proj[i])) for i in range(3))
    key_rows, val_rows = exchange_rows([own_keys, own_vals], dims, n_tensor, 2)
    place = lax.rem(jnp.arange(keys, dtype=jnp.int32) + rank * rows, keys)
    mask = jnp.where(place < clip_lengths[0], 0.0, MASKED).astype(jnp.float32)[None]
    table = span_table(rel_table)
    rank_list = rank.astype(jnp.int32)[None]
    attended, log_totals = attn_fwd(rank_list, query, key_rows, val_rows, table, mask)
    branch = dot_nt(attended, out_attn)
    squares.append(jnp.sum(branch * branch))
    stream = stream + branch

    entered_c, norm_c = enter(stream, 2)
    glu_first = dot_nn(entered_c, glu[0])
    glu_second = dot_nn(entered_c, glu[1])
    sig_second = jax.nn.sigmoid(glu_second)
    gated = glu_first * sig_second
    gated_before = shift_rank(gated[rows - HALO :], 1)
    mixed = taps_forward(gated, gated_before, conv_taps)
    shaped, normed_mid, scale_mid = norm_forward(mixed, norm_gains[3], norm_shifts[3])
    conv_act = low(jax.nn.silu(shaped))
    branch = dot_nt(conv_act, out_conv)
    squares.append(jnp.sum(branch * branch))
    stream = stream + branch

    entered_d, norm_d = enter(stream, 4)
    branch, ffn_d = ffn_forward(entered_d, up_two, down_two)
    squares.append(jnp.sum(branch * branch))
    stream = stream + 0.5 * branch
    squares.append(jnp.sum(stream * stream))
    result, normed_e, scale_e = norm_forward(stream, norm_gains[5], norm_shifts[5])
    output = low(result)

    grad_stream, gain_e, shift_e = norm_back(grad_out.astype(jnp.float32), (normed_e, scale_e), 5)
    grad_low = low(0.5 * grad_stream)
    grad_entered, grad_up_two, grad_down_two = ffn_backward(entered_d, ffn_d, grad_low, up_two, down_two)
    grad_extra, gain_d, shift_d = norm_back(grad_entered, norm_d, 4)
    grad_stream = grad_stream + grad_extra

    grad_low = low(grad_stream)
    grad_conv_out = low(dot_tn(grad_low, conv_act))
    sigma = jax.nn.sigmoid(shaped)
    grad_shaped = dot_nn(grad_low, out_conv) * sigma * (1.0 + shaped * (1.0 - sigma))
    grad_mixed, gain_mid, shift_mid = norm_back(grad_shaped, (normed_mid, scale_mid), 3)
    grad_after = shift_rank(grad_mixed[:HALO], -1)
    grad_gated, taps_grad = taps_backward(grad_mixed, grad_after, gated, gated_before, conv_taps)
    grad_first = low(grad_gated * sig_second)
    grad_second = low(grad_gated * glu_first * sig_second * (1.0 - sig_second))
    grad_glu = [low(dot_tn(entered_c, g)) for g in (grad_first, grad_second)]
    grad_entered = dot_nt(grad_first, glu[0]) + dot_nt(grad_second, glu[1])
    grad_extra, gain_c, shift_c = norm_back(grad_entered, norm_c, 2)
    grad_stream = grad_stream + grad_extra

    grad_low = low(grad_stream)
    grad_attn_out = low(dot_tn(grad_low, attended))
    grad_attended = low(dot_nn(grad_low, out_attn))
    grad_query, grad_keys, grad_vals, grad_span = attn_bwd(
        rank_list, query, key_rows, val_rows, grad_attended, attended, log_totals, table, mask
    )
    grad_keys, grad_vals = return_rows([grad_keys, grad_vals], dims, n_tensor, 3)
    grad_parts = (grad_query, grad_keys, grad_vals)
    grad_proj = [low(dot_tn(entered_b, g)) for g in grad_parts]
    grad_entered = sum(dot_nt(g, proj[i]) for i, g in enumerate(grad_parts))
    grad_extra, gain_b, shift_b = norm_back(grad_entered, norm_b, 1)
    grad_stream = grad_stream + grad_extra

    grad_low = low(0.5 * grad_stream)
    grad_entered, grad_up_one, grad_down_one = ffn_backward(entered_a, ffn_a, grad_low, up_one, down_one)
    grad_extra, gain_a, shift_a = norm_back(grad_entered, norm_a, 0)
    grad_stream = grad_stream + grad_extra

    span_grad = fold_table(grad_span)
    span_rows = -(-span_grad.size // width)
    table_rows = jnp.pad(span_grad.reshape(-1), (0, span_rows * width - span_grad.size)).reshape(span_rows, width)
    square_row = jnp.pad(jnp.stack(squares), (0, width - len(squares)))[None]
    parts = [
        jnp.stack([gain_a, gain_b, gain_c, gain_mid, gain_d, gain_e]),
        jnp.stack([shift_a, shift_b, shift_c, shift_mid, shift_d, shift_e]),
        taps_grad,
        table_rows,
        square_row,
    ]
    vec = jnp.concatenate(parts, axis=0)
    vec = jnp.pad(vec, ((0, -vec.shape[0] % 8), (0, 0)))
    grads = [
        grad_down_two, grad_up_two, grad_conv_out, *grad_glu, grad_attn_out, *grad_proj, grad_down_one, grad_up_one,
    ]
    summed, vec = scatter_grads([g[None] for g in grads], vec, dims, n_tensor, 1)
    s_down_two, s_up_two, s_conv, s_glu0, s_glu1, s_attn, s_q, s_k, s_v, s_down_one, s_up_one = (s[0] for s in summed)
    at = 0
    pieces = []
    for part in parts:
        pieces.append(vec[at : at + part.shape[0]])
        at += part.shape[0]
    gains_sum, shifts_sum, taps_sum, table_sum, square_sum = pieces
    table_sum = table_sum.reshape(-1)[: span_grad.size].reshape(span_grad.shape)
    count_all = float(lax.axis_size("dp") * keys * width)
    rms_values = jnp.sqrt(square_sum[0, : len(squares)] / count_all)
    return (
        output,
        grad_stream,
        s_up_one,
        s_down_one.T,
        jnp.stack([s_q, s_k, s_v]),
        s_attn.T,
        table_sum,
        jnp.stack([s_glu0, s_glu1]),
        taps_sum,
        s_conv.T,
        s_up_two,
        s_down_two.T,
        gains_sum,
        shifts_sum,
        rms_values,
    )


def solution(mesh):
    n_dp, n_tensor = mesh.shape["dp"], mesh.shape["tensor"]
    dims = FACTORS.get(n_dp, (n_dp, 1, 1))
    return jax.shard_map(
        functools.partial(on_device, dims, n_tensor),
        mesh=mesh,
        in_specs=(
            P(("dp", "tensor"), None),
            P(("dp", "tensor"), None),
            P("dp"),
            P("dp", "tensor"),
            P("tensor", "dp"),
            P(None, "dp", "tensor"),
            P("tensor", "dp"),
            P(),
            P(None, "dp", "tensor"),
            P(),
            P("tensor", "dp"),
            P("dp", "tensor"),
            P("tensor", "dp"),
            P(),
            P(),
        ),
        out_specs=(
            P(("dp", "tensor"), None),
            P(("dp", "tensor"), None),
            P("dp", "tensor"),
            P("tensor", "dp"),
            P(None, "dp", "tensor"),
            P("tensor", "dp"),
            P(),
            P(None, "dp", "tensor"),
            P(),
            P("tensor", "dp"),
            P("dp", "tensor"),
            P("tensor", "dp"),
            P(),
            P(),
            P(),
        ),
        check_vma=False,
    )
```

time: 2590 us -> 897 us (0.35)
  waiting for transfers between devices: 1300 us -> 0.3 us
  Pallas kernels: 0 us -> 637 us
  local copies, waits for them, and re-layouts: 652 us -> 28.9 us
  other arithmetic: 216 us -> 56.1 us
  matrix products: 310 us -> 159 us
  blocking collectives: 52 us -> 0 us
    reduce_scatter x16 -> x0, waiting for transfers between devices: 649 us -> none  [the longest x1 95.4 us: on_device(): lax.psum_scatter(grad_up_one.astype(jnp.bfloat16), 'dp', scatter_dimensio...]
    pallas_call x0 -> x6, Pallas kernels: none -> 637 us  [the longest x1 254 us: gather_weights(): pl.pallas_call(functools.partial(gather_kernel, dims, n_tensor, n), out_s...]
    all_gather x16 -> x0, waiting for transfers between devices: 521 us -> none  [the longest x1 79.6 us: on_device(): lax.all_gather(first_up, 'dp', axis=0, tiled=True)]
    while x78 -> x0, local copies, waits for them, and re-layouts: 209 us -> none
    reshape x6 -> x2, local copies, waits for them, and re-layouts: 202 us -> 0.08 us  [the longest x1 0.07 us: on_device(): span_grad.reshape(-1)]
    dot_general x57 -> x34, matrix products: 310 us -> 159 us  [the longest x11 57.9 us: dot_nn(): return jnp.dot(a, b, preferred_element_type=jnp.float32)]
    psum x1 -> x0, waiting for transfers between devices: 128 us -> none  [on_device(): lax.psum((gains_stack, shifts_stack, taps_wide, table_grad), ('dp', 'tens...]
    select_n x4 -> x0, local copies, waits for them, and re-layouts: 99.3 us -> none  [block_scores(): jnp.take(toward, bucket_picks(first_row, block_rows, key_count), axis=2)]
  transfers between devices with their start and end apart: 33 -> 2, of which waited for: 31 -> 1; matrix products, arithmetic and copies ran while one was open for 19% -> 2% of each run, Pallas kernels for 0% -> 0%
where the time goes in v1:
time: 897 us; the launch traced here: 888 us
  Pallas kernels  637 us (71%)
  matrix products  159 us (18%)
  other arithmetic  56.1 us (6%)
  local copies, waits for them, and re-layouts  28.9 us (3%)
    pallas_call x1, Pallas kernels, gather_weights(): pl.pallas_call(functools.partial(gather_kernel, dims, n_tensor, n), out_s...  254 us
    pallas_call x1, Pallas kernels, scatter_grads(): pl.pallas_call(functools.partial(scatter_kernel, dims, n_tensor, plan, n,...  252 us
    pallas_call x1, Pallas kernels, attn_bwd(): pl.pallas_call(attn_bwd_kernel, grid_spec=pltpu.PrefetchScalarGridSpec(nu...  79.3 us
    dot_general x11, matrix products, dot_nn(): return jnp.dot(a, b, preferred_element_type=jnp.float32)  57.9 us
    dot_general x11, matrix products, dot_tn(): return lax.dot_general(a, b, TN, preferred_element_type=jnp.float32)  52 us
    dot_general x11, matrix products, dot_nt(): return lax.dot_general(a, b, NT, preferred_element_type=jnp.float32)  48.8 us
    pallas_call x1, Pallas kernels, attn_fwd(): pl.pallas_call(attn_fwd_kernel, grid_spec=pltpu.PrefetchScalarGridSpec(nu...  37.5 us
  transfers between devices with their start and end apart: 2, of which 1 were waited for; matrix products, arithmetic and copies ran while one was open for 2% of the time, Pallas kernels for 0%

profile of v1, /device:TPU:0, one launch (start us, length us, event | category | flops | bytes accessed | tf_op | source)
XLA Modules:
  0.0 887.6 jit_solution(1796280311500015294)
XLA Ops:
  1.4 1.4 convert_reduce_fusion.1
  2.8 1.7 fusion.16
  4.8 1.3 gather_fusion
  7.1 253.7 %gather_weights.1 = (bf16[1,4,2,2,64,4096]{5,4,3,2,1,0:T(8,128)(2,1)}, bf16[1,4,2,2,64,4096]{5,4,3,2,1,0:T(8,128)(2,1)}, bf16[3,4,2,2,64,1024]{5,4,3,2,1,0:T(8,1...) custom-call(bf16[1,64,2048]{2,1,0:T(8,128)(2,1)} %bitcast.236, ...), custom_call_target="tpu_custom_call" | custom-call | tf_op jit(solution)/shard_map/gather_weights/pallas_call | solution.py:430
  260.8 11.3 %multiply_convert_fusion.3 = (bf16[512,4096]{1,0:T(8,128)(2,1)}, f32[512,4096]{1,0:T(8,128)}) fusion(bf16[1024,4096]{1,0:T(8,128)(2,1)} %bitcast.382, bf16[512,1024]{1,0:T(8,128)(2,1)S(1)} %copy-done.7, f32[1024]{0:T(1024)S(1)} %bitcast.378, f32[1024]{0:T(1024)S(1)} %bitcast.351, f32[512]{0:T(512)S(1)} %add_rsqrt_fusion.5, f32[512]{0:T(512)S(1)} %broadcast_multiply_fusion.17), kind=kOutput, calls=%fused_computation.63 | convolution fusion | flops 4308598784 | bytes 22032384 | tf_op jit(solution)/shard_map/dot_general | solution.py:31
  272.2 7.4 fusion.165
  280.0 2.6 fusion.166
  283.1 2.8 convolution_convert_fusion.14.q_ref
  286.0 2.4 convolution_convert_fusion.12.refs_1_
  288.3 2.3 convolution_convert_fusion.13.refs_0_
  291.2 5.9 exchange_rows.1
  297.1 37.5 %attn_fwd.1 = (bf16[512,1024]{1,0:T(8,128)(2,1)}, f32[8,1024,1]{2,1,0:T(8,128)}) custom-call(s32[1]{0:T(128)} %bitcast.14.rank_ref, bf16[512,1024]{1,0:T(8,128)(2,1)} %convolution_convert_fusion.14.q_ref, bf16[1024,1024]{1,0:T(8,128)(2,1)} %bitcast.209, bf16[1024,1024]{1,0:T(8,128)(2,1)} %bitcast.211, bf16[512,128]{1,0:T(8,128)(2,1)} %pad_maximum_fusion.4.tab_ref, ...), custom_call_target="tpu_custom_call" | custom-call | tf_op jit(solution)/shard_map/attn_fwd/pallas_call | solution.py:105
  334.6 4.0 fusion.164
  339.4 1.6 copy-done.21
  340.9 1.5 add_divide_fusion.3
  342.5 2.6 fusion.173
  345.1 2.3 collective-permute-start
  348.4 9.3 %fusion.163 = (f32[512]{0:T(512)S(1)}, f32[512,1024]{1,0:T(8,128)S(1)}) fusion(f32[512,1024]{1,0:T(8,128)S(1)} %get-tuple-element.217, f32[1024]{0:T(1024)S(1)} %bitcast.312, f32[32,1024]{1,0:T(8,128)S(1)} %collective-permute-done, f32[1024]{0:T(1024)S(1)} %bitcast.314, f32[1024]{0:T(1024)S(1)} %bitcast.256, f32[1024]{0:T(1024)S(1)} %bitcast.258, ...), kind=kLoop, calls=%fused_computation.381 | loop fusion | flops 48233984 | bytes 4454400 | tf_op jit(solution)/shard_map/reduce_sum | solution.py:856
  359.2 2.1 fusion.162
  361.9 7.9 multiply_convert_fusion.2
  369.8 7.8 fusion.161
  378.8 1.9 fusion.20
  380.7 7.8 convolution_convert_fusion.3
  388.5 12.1 %multiply_convert_fusion.1 = bf16[512,4096]{1,0:T(8,128)(2,1)} fusion(f32[512,4096]{1,0:T(8,128)} %get-tuple-element.220, bf16[1024,4096]{1,0:T(8,128)(2,1)} %bitcast.395, bf16[512,1024]{1,0:T(8,128)(2,1)S(1)} %copy-done.17, f32[512,1024]{1,0:T(8,128)S(1)} %get-tuple-element.150, f32[512]{0:T(512)S(1)} %broadcast_multiply_fusion.10, ...), kind=kOutput, calls=%fused_computation.60 | convolution fusion | flops 4319084544 | bytes 24129536 | tf_op jit(solution)/shard_map/dot_general | solution.py:31
  400.7 9.4 %multiply_reduce_fusion.36 = (f32[1024]{0:T(1024)}, f32[512]{0:T(512)S(1)}, f32[512]{0:T(512)S(1)}, f32[1024]{0:T(1024)}, f32[512,1024]{1,0:T(8,128)S(1)}) fusion(f32[512,1024]{1,0:T(8,128)S(1)} %get-tuple-element.152, f32[512]{0:T(512)S(1)} %add_rsqrt_fusion.1, f32[512]{0:T(512)S(1)} %broadcast_multiply_fusion.13, f32[1024]{0:T(1024)S(1)} %bitcast.358, ...), kind=kOutput, calls=%fused_computation.269 | convolution fusion | flops 4299682816 | bytes 16797696 | tf_op jit(solution)/shard_map/dot_general | solution.py:23
  410.1 9.2 %convolution_convert_fusion.2 = bf16[1024,4096]{1,0:T(8,128)(2,1)} fusion(bf16[512,4096]{1,0:T(8,128)(2,1)} %multiply_convert_fusion.1, f32[512,1024]{1,0:T(8,128)S(1)} %get-tuple-element.152, f32[1024]{0:T(1024)S(1)} %bitcast.381, f32[1024]{0:T(1024)S(1)} %bitcast.359, f32[512]{0:T(512)S(1)} %add_rsqrt_fusion.1, f32[512]{0:T(512)S(1)} %broadcast_multiply_fusion.13), kind=kOutput, calls=%fused_computation.67 | convolution fusion | flops 4301783040 | bytes 14692352 | tf_op jit(solution)/shard_map/dot_general | solution.py:27
  419.3 2.5 multiply_add_fusion.2
  421.8 2.9 multiply_reduce_fusion.37
  424.7 4.3 multiply_reduce_fusion.6
  429.0 1.3 collective-permute-start.1
  430.3 1.7 multiply_reduce_fusion.33
  432.0 3.1 multiply_reduce_fusion.24
  435.1 3.1 multiply_reduce_fusion.15
  438.1 2.6 convolution_convert_fusion.10
  440.8 3.6 stack.201
  444.4 1.2 pad.13
  445.5 11.2 %multiply_convert_fusion.6 = (bf16[512,1024]{1,0:T(8,128)(2,1)S(1)}, f32[512,1024]{1,0:T(8,128)S(1)}) fusion(f32[512,1024]{1,0:T(8,128)} %copy-done.2, f32[512,1024]{1,0:T(8,128)S(1)} %get-tuple-element.146, f32[1024]{0:T(1024)S(1)} %bitcast.313, f32[32,1024]{1,0:T(8,128)S(1)} %collective-permute-done.1, f32[1024]{0:T(1024)S(1)} %bitcast.315, ...), kind=kLoop, calls=%fused_computation.280 | loop fusion | flops 48758784 | bytes 7598080 | tf_op jit(solution)/shard_map/convert_element_type | solution.py:872
  457.5 1.1 copy-done.22
  458.7 1.3 fusion.174
  461.3 1.9 multiply_reduce_fusion.38
  464.8 2.2 convolution_convert_fusion.11.do_ref
  467.0 2.7 convolution_convert_fusion.7
  469.7 79.3 %attn_bwd.1 = (bf16[512,1024]{1,0:T(8,128)(2,1)}, bf16[1024,1024]{1,0:T(8,128)(2,1)}, bf16[1024,1024]{1,0:T(8,128)(2,1)}, f32[512,128]{1,0:T(8,128)}) custom-call(s32[1]{0:T(128)} %bitcast.14.rank_ref, bf16[512,1024]{1,0:T(8,128)(2,1)} %convolution_convert_fusion.14.q_ref, bf16[1024,1024]{1,0:T(8,128)(2,1)} %bitcast.210, bf16[1024,1024]{1,0:T(8,128)(2,1)} %bitcast.212, ...), custom_call_target="tpu_custom_call" | custom-call | tf_op jit(solution)/shard_map/attn_bwd/pallas_call | solution.py:212
  548.9 8.5 return_rows.1
  557.4 3.3 fusion.176
  560.8 2.6 convolution_convert_fusion.5
  563.5 1.3 fusion.175
  564.8 2.6 convolution_convert_fusion.6
  567.4 2.7 convolution_convert_fusion.9
  570.1 2.6 convolution_convert_fusion.8
  572.7 2.7 convolution_convert_fusion.4
  575.4 2.0 multiply_reduce_fusion.39
  578.1 1.5 copy-done.98
  579.6 7.0 convolution_convert_fusion.1
  586.7 9.9 %multiply_convert_fusion = bf16[512,4096]{1,0:T(8,128)(2,1)} fusion(f32[512,4096]{1,0:T(8,128)} %get-tuple-element.216, bf16[1024,4096]{1,0:T(8,128)(2,1)S(1)} %bitcast.389, f32[512,1024]{1,0:T(8,128)S(1)} %multiply_add_fusion), kind=kOutput, calls=%fused_computation.59 | convolution fusion | flops 4314890240 | bytes 23068672 | tf_op jit(solution)/shard_map/dot_general | solution.py:31
  596.6 8.5 fusion.15
  605.4 9.5 %convolution_convert_fusion = bf16[1024,4096]{1,0:T(8,128)(2,1)} fusion(bf16[512,4096]{1,0:T(8,128)(2,1)} %multiply_convert_fusion, bf16[512,1024]{1,0:T(8,128)(2,1)S(1)} %copy-done.8, f32[1024]{0:T(1024)} %bitcast.379, f32[1024]{0:T(1024)S(1)} %bitcast.353, f32[512]{0:T(512)S(1)} %copy-done.89, f32[512]{0:T(512)S(1)} %copy-done.51), kind=kOutput, calls=%fused_computation.65 | convolution fusion | flops 4302307328 | bytes 13643776 | tf_op jit(solution)/shard_map/dot_general | solution.py:27
  615.7 1.7 concatenate.16
  618.1 251.6 %scatter_grads.1 = (f32[1,64,2048]{2,1,0:T(8,128)}, f32[1,64,2048]{2,1,0:T(8,128)}, f32[1,64,512]{2,1,0:T(8,128)}, f32[1,64,512]{2,1,0:T(8,128)}, f32[1,64,512]{...) custom-call(bf16[1,4,2,2,64,4096]{5,4,3,2,1,0:T(8,128)(2,1)} %bitcas, ...), custom_call_target="tpu_custom_call" | custom-call | tf_op jit(solution)/shard_map/scatter_grads/pallas_call | solution.py:758
  869.7 1.2 sqrt_bitcast_fusion
  871.6 1.5 fusion.168
  873.1 1.6 slice.551
  875.5 1.7 pad_maximum_fusion.3
  877.2 4.6 fusion.14
  (281 shorter events, 20.4 us)
Async XLA Ops:
  2.8 258.0 %copy-start.50 = (f32[512]{0:T(512)}, f32[512]{0:T(512)S(1)}, u32[]{:S(2)}) copy-start(f32[512]{0:T(512)S(1)} %broadcast_multiply_fusion.17) | copy-start | bytes 6148
  2.8 258.0 %copy-start.7 = (bf16[512,1024]{1,0:T(8,128)(2,1)S(1)}, bf16[512,1024]{1,0:T(8,128)(2,1)}, u32[]{:S(2)}) copy-start(bf16[512,1024]{1,0:T(8,128)(2,1)} %param.15) | copy-start | bytes 3145732
  4.6 267.6 %copy-start.88 = (f32[512]{0:T(512)}, f32[512]{0:T(512)S(1)}, u32[]{:S(2)}) copy-start(f32[512]{0:T(512)S(1)} %add_rsqrt_fusion.5) | copy-start | bytes 6148
  4.7 267.4 %copy-start.79 = (f32[1,1024]{1,0:T(1,128)}, f32[1,1024]{1,0:T(1,128)S(1)}, u32[]{:S(2)}) copy-start(f32[1,1024]{1,0:T(1,128)S(1)} %get-tuple-element.207) | copy-start | bytes 12292
  4.8 277.9 %copy-start.42 = (f32[1,1024]{1,0:T(1,128)}, f32[1,1024]{1,0:T(1,128)S(1)}, u32[]{:S(2)}) copy-start(f32[1,1024]{1,0:T(1,128)S(1)} %get-tuple-element.206) | copy-start | bytes 12292
  4.8 267.4 %copy-start.92 = (f32[1,1024]{1,0:T(1,128)}, f32[1,1024]{1,0:T(1,128)S(1)}, u32[]{:S(2)}) copy-start(f32[1,1024]{1,0:T(1,128)S(1)} %get-tuple-element.213) | copy-start | bytes 12292
  260.8 11.4 %copy-start.93 = (bf16[1,4,2,2,64,4096]{5,4,3,2,1,0:T(8,128)(2,1)S(1)}, bf16[1,4,2,2,64,4096]{5,4,3,2,1,0:T(8,128)(2,1)}, u32[]{:S(2)}) copy-start(bf16[1,4,2,2,64,4096]{5,4,3,2,1,0:T(8,128)(2,1)} %get-tuple-element.46) | copy-start | bytes 25165828
  272.2 7.8 slice-start
  272.2 7.8 slice-start.1
  272.2 7.8 copy-start.16
  279.6 55.0 %copy-start = (f32[512,1024]{1,0:T(8,128)}, f32[512,1024]{1,0:T(8,128)S(1)}, u32[]{:S(2)}) copy-start(f32[512,1024]{1,0:T(8,128)S(1)} %get-tuple-element.158) | copy-start | bytes 6291460
  282.6 5.7 copy-start.20
  338.6 20.2 %copy-start.4 = (f32[512,1024]{1,0:T(8,128)}, f32[512,1024]{1,0:T(8,128)S(1)}, u32[]{:S(2)}) copy-start(f32[512,1024]{1,0:T(8,128)S(1)} %get-tuple-element.156) | copy-start | bytes 6291460
  345.1 3.3 collective-permute-start
  421.8 16.3 %copy-start.13 = (f32[512,1024]{1,0:T(8,128)}, f32[512,1024]{1,0:T(8,128)S(1)}, u32[]{:S(2)}) copy-start(f32[512,1024]{1,0:T(8,128)S(1)} %get-tuple-element.164) | copy-start | bytes 6291460
  429.0 16.5 %collective-permute-start.1 = (f32[32,1024]{1,0:T(8,128)S(1)}, f32[32,1024]{1,0:T(8,128)S(1)}, u32[]{:S(2)}, u32[]{:S(2)}) collective-permute-start(f32[32,1024]{1,0:T(8,128)S(1)} %slice.616), channel_id=1, source_target_pairs={{1,0},{3,2},{5,4},{7,6},{9,8},{11,10},{13,12},{15,14},{17,16},{19,... | collective-permute-start | bytes 393224 | tf_op jit(solution)/shard_map/ppermute | solution.py:958
  445.5 11.2 %copy-start.3 = (f32[512,1024]{1,0:T(8,128)S(1)}, f32[512,1024]{1,0:T(8,128)}, u32[]{:S(2)}) copy-start(f32[512,1024]{1,0:T(8,128)} %copy-done.2) | copy-start | bytes 6291460
  445.5 11.2 %copy-start.6 = (f32[512,1024]{1,0:T(8,128)S(1)}, f32[512,1024]{1,0:T(8,128)}, u32[]{:S(2)}) copy-start(f32[512,1024]{1,0:T(8,128)} %get-tuple-element.218) | copy-start | bytes 6291460
  577.4 9.2 %slice-start.4 = ((s8[8388608]{0:T(1024)(128)(4,1)}), s8[4194304]{0:T(1024)(128)(4,1)S(1)}, s32[]{:S(2)}) async-start(s8[8388608]{0:T(1024)(128)(4,1)} %bitcast.387), calls=%async_computation.4 | async-start | bytes 8388608
  579.6 7.0 copy-start.15
  579.6 7.0 slice-start.5
  579.6 16.9 %slice-start.2 = ((s8[8388608]{0:T(1024)(128)(4,1)}), s8[4194304]{0:T(1024)(128)(4,1)S(1)}, s32[]{:S(2)}) async-start(s8[8388608]{0:T(1024)(128)(4,1)} %bitcast.383), calls=%async_computation.2 | async-start | bytes 8388608
  586.6 9.9 %copy-start.8 = (bf16[512,1024]{1,0:T(8,128)(2,1)S(1)}, bf16[512,1024]{1,0:T(8,128)(2,1)}, u32[]{:S(2)}) copy-start(bf16[512,1024]{1,0:T(8,128)(2,1)} %param.15) | copy-start | bytes 3145732
  586.6 9.9 %copy-start.51 = (f32[512]{0:T(512)S(1)}, f32[512]{0:T(512)}, u32[]{:S(2)}) copy-start(f32[512]{0:T(512)} %copy-done.50) | copy-start | bytes 6148
  586.7 9.9 %copy-start.80 = (f32[1,1024]{1,0:T(1,128)S(1)}, f32[1,1024]{1,0:T(1,128)}, u32[]{:S(2)}) copy-start(f32[1,1024]{1,0:T(1,128)} %copy-done.79) | copy-start | bytes 12292
  586.7 9.9 %copy-start.89 = (f32[512]{0:T(512)S(1)}, f32[512]{0:T(512)}, u32[]{:S(2)}) copy-start(f32[512]{0:T(512)} %copy-done.88) | copy-start | bytes 6148
  586.7 9.9 %slice-start.3 = ((s8[8388608]{0:T(1024)(128)(4,1)}), s8[4194304]{0:T(1024)(128)(4,1)S(1)}, s32[]{:S(2)}) async-start(s8[8388608]{0:T(1024)(128)(4,1)} %bitcast.383), calls=%async_computation.3 | async-start | bytes 8388608
  605.1 9.8 %copy-start.35 = (f32[512,128]{1,0:T(8,128)S(1)}, f32[512,128]{1,0:T(8,128)}, u32[]{:S(2)}) copy-start(f32[512,128]{1,0:T(8,128)} %get-tuple-element.62) | copy-start | bytes 786436
  605.1 9.8 %copy-start.87 = (s32[512]{0:T(512)S(1)}, s32[512]{0:T(512)}, u32[]{:S(2)}) copy-start(s32[512]{0:T(512)} %fusion.149) | copy-start | bytes 6148
  605.1 10.3 %copy-start.52 = (f32[1024]{0:T(1024)S(1)}, f32[1024]{0:T(1024)}, u32[]{:S(2)}) copy-start(f32[1024]{0:T(1024)} %get-tuple-element.129) | copy-start | bytes 12292
  605.1 10.3 %copy-start.53 = (f32[1024]{0:T(1024)S(1)}, f32[1024]{0:T(1024)}, u32[]{:S(2)}) copy-start(f32[1024]{0:T(1024)} %get-tuple-element.145) | copy-start | bytes 12292
  605.1 10.3 %copy-start.54 = (f32[1024]{0:T(1024)S(1)}, f32[1024]{0:T(1024)}, u32[]{:S(2)}) copy-start(f32[1024]{0:T(1024)} %get-tuple-element.92) | copy-start | bytes 12292
  605.1 10.3 %copy-start.55 = (f32[1024]{0:T(1024)S(1)}, f32[1024]{0:T(1024)}, u32[]{:S(2)}) copy-start(f32[1024]{0:T(1024)} %get-tuple-element.93) | copy-start | bytes 12292
  605.1 10.3 %copy-start.56 = (f32[1024]{0:T(1024)S(1)}, f32[1024]{0:T(1024)}, u32[]{:S(2)}) copy-start(f32[1024]{0:T(1024)} %get-tuple-element.94) | copy-start | bytes 12292
  605.1 10.3 %copy-start.57 = (f32[1024]{0:T(1024)S(1)}, f32[1024]{0:T(1024)}, u32[]{:S(2)}) copy-start(f32[1024]{0:T(1024)} %get-tuple-element.95) | copy-start | bytes 12292
  605.1 10.3 %copy-start.58 = (f32[1024]{0:T(1024)S(1)}, f32[1024]{0:T(1024)}, u32[]{:S(2)}) copy-start(f32[1024]{0:T(1024)} %get-tuple-element.96) | copy-start | bytes 12292
  605.1 10.3 %copy-start.59 = (f32[1024]{0:T(1024)S(1)}, f32[1024]{0:T(1024)}, u32[]{:S(2)}) copy-start(f32[1024]{0:T(1024)} %get-tuple-element.97) | copy-start | bytes 12292
  605.2 10.3 %copy-start.60 = (f32[1024]{0:T(1024)S(1)}, f32[1024]{0:T(1024)}, u32[]{:S(2)}) copy-start(f32[1024]{0:T(1024)} %get-tuple-element.98) | copy-start | bytes 12292
  605.2 10.3 %copy-start.61 = (f32[1024]{0:T(1024)S(1)}, f32[1024]{0:T(1024)}, u32[]{:S(2)}) copy-start(f32[1024]{0:T(1024)} %get-tuple-element.108) | copy-start | bytes 12292
  605.2 10.3 %copy-start.62 = (f32[1024]{0:T(1024)S(1)}, f32[1024]{0:T(1024)}, u32[]{:S(2)}) copy-start(f32[1024]{0:T(1024)} %get-tuple-element.109) | copy-start | bytes 12292
  605.2 10.3 %copy-start.63 = (f32[1024]{0:T(1024)S(1)}, f32[1024]{0:T(1024)}, u32[]{:S(2)}) copy-start(f32[1024]{0:T(1024)} %get-tuple-element.110) | copy-start | bytes 12292
  605.2 10.3 %copy-start.64 = (f32[1024]{0:T(1024)S(1)}, f32[1024]{0:T(1024)}, u32[]{:S(2)}) copy-start(f32[1024]{0:T(1024)} %get-tuple-element.111) | copy-start | bytes 12292
  605.2 10.3 %copy-start.65 = (f32[1024]{0:T(1024)S(1)}, f32[1024]{0:T(1024)}, u32[]{:S(2)}) copy-start(f32[1024]{0:T(1024)} %get-tuple-element.112) | copy-start | bytes 12292
  605.2 10.3 %copy-start.66 = (f32[1024]{0:T(1024)S(1)}, f32[1024]{0:T(1024)}, u32[]{:S(2)}) copy-start(f32[1024]{0:T(1024)} %get-tuple-element.113) | copy-start | bytes 12292
  605.2 10.3 %copy-start.67 = (f32[1024]{0:T(1024)S(1)}, f32[1024]{0:T(1024)}, u32[]{:S(2)}) copy-start(f32[1024]{0:T(1024)} %get-tuple-element.114) | copy-start | bytes 12292
  605.2 10.3 %copy-start.68 = (f32[1024]{0:T(1024)S(1)}, f32[1024]{0:T(1024)}, u32[]{:S(2)}) copy-start(f32[1024]{0:T(1024)} %get-tuple-element.115) | copy-start | bytes 12292
  605.2 10.3 %copy-start.69 = (f32[1024]{0:T(1024)S(1)}, f32[1024]{0:T(1024)}, u32[]{:S(2)}) copy-start(f32[1024]{0:T(1024)} %get-tuple-element.116) | copy-start | bytes 12292
  605.3 10.3 %copy-start.70 = (f32[1024]{0:T(1024)S(1)}, f32[1024]{0:T(1024)}, u32[]{:S(2)}) copy-start(f32[1024]{0:T(1024)} %get-tuple-element.99) | copy-start | bytes 12292
  605.3 10.3 %copy-start.71 = (f32[1024]{0:T(1024)S(1)}, f32[1024]{0:T(1024)}, u32[]{:S(2)}) copy-start(f32[1024]{0:T(1024)} %get-tuple-element.100) | copy-start | bytes 12292
  605.3 10.3 %copy-start.72 = (f32[1024]{0:T(1024)S(1)}, f32[1024]{0:T(1024)}, u32[]{:S(2)}) copy-start(f32[1024]{0:T(1024)} %get-tuple-element.101) | copy-start | bytes 12292
  605.3 10.3 %copy-start.73 = (f32[1024]{0:T(1024)S(1)}, f32[1024]{0:T(1024)}, u32[]{:S(2)}) copy-start(f32[1024]{0:T(1024)} %get-tuple-element.102) | copy-start | bytes 12292
  605.3 10.3 %copy-start.74 = (f32[1024]{0:T(1024)S(1)}, f32[1024]{0:T(1024)}, u32[]{:S(2)}) copy-start(f32[1024]{0:T(1024)} %get-tuple-element.103) | copy-start | bytes 12292
  605.3 10.3 %copy-start.75 = (f32[1024]{0:T(1024)S(1)}, f32[1024]{0:T(1024)}, u32[]{:S(2)}) copy-start(f32[1024]{0:T(1024)} %get-tuple-element.104) | copy-start | bytes 12292
  605.3 10.3 %copy-start.76 = (f32[1024]{0:T(1024)S(1)}, f32[1024]{0:T(1024)}, u32[]{:S(2)}) copy-start(f32[1024]{0:T(1024)} %get-tuple-element.105) | copy-start | bytes 12292
  605.3 10.3 %copy-start.77 = (f32[1024]{0:T(1024)S(1)}, f32[1024]{0:T(1024)}, u32[]{:S(2)}) copy-start(f32[1024]{0:T(1024)} %get-tuple-element.106) | copy-start | bytes 12292
  605.3 10.3 %copy-start.78 = (f32[1024]{0:T(1024)S(1)}, f32[1024]{0:T(1024)}, u32[]{:S(2)}) copy-start(f32[1024]{0:T(1024)} %get-tuple-element.107) | copy-start | bytes 12292
  605.3 10.3 %copy-start.81 = (f32[1024]{0:T(1024)S(1)}, f32[1024]{0:T(1024)}, u32[]{:S(2)}) copy-start(f32[1024]{0:T(1024)} %pad.13) | copy-start | bytes 12292
  605.4 10.3 %copy-start.83 = (f32[1024]{0:T(1024)S(1)}, f32[1024]{0:T(1024)}, u32[]{:S(2)}) copy-start(f32[1024]{0:T(1024)} %get-tuple-element.117) | copy-start | bytes 12292
  605.4 10.3 %copy-start.84 = (f32[1024]{0:T(1024)S(1)}, f32[1024]{0:T(1024)}, u32[]{:S(2)}) copy-start(f32[1024]{0:T(1024)} %get-tuple-element.118) | copy-start | bytes 12292
  605.4 10.3 %copy-start.85 = (f32[1024]{0:T(1024)S(1)}, f32[1024]{0:T(1024)}, u32[]{:S(2)}) copy-start(f32[1024]{0:T(1024)} %get-tuple-element.119) | copy-start | bytes 12292
  605.4 10.3 %copy-start.86 = (f32[1024]{0:T(1024)S(1)}, f32[1024]{0:T(1024)}, u32[]{:S(2)}) copy-start(f32[1024]{0:T(1024)} %get-tuple-element.128) | copy-start | bytes 12292
  605.4 10.3 %copy-start.90 = (f32[1024]{0:T(1024)S(1)}, f32[1024]{0:T(1024)}, u32[]{:S(2)}) copy-start(f32[1024]{0:T(1024)} %get-tuple-element.120) | copy-start | bytes 12292
  605.4 10.2 %copy-start.91 = (f32[1024]{0:T(1024)S(1)}, f32[1024]{0:T(1024)}, u32[]{:S(2)}) copy-start(f32[1024]{0:T(1024)} %get-tuple-element.139) | copy-start | bytes 12292
  877.2 5.5 copy-start.34
  (45 other events, 132.2 us)

commit v2 on v1

--- a/solution.py
+++ b/solution.py
@@ -13,6 +13,9 @@
 RIGHT = 8
 EPSILON = 1e-05
 MASKED = -1e30
+VMEM_LIMIT = 66_000_000
+HOST_G = (512, 6, 5)
+HOST_S = (256, 8, 6)
 BLK = 128
 SPAN = 512
 NT = (((1,), (1,)), ((), ()))
@@ -70,12 +73,41 @@
     return jnp.concatenate(tiles, axis=0)
 
 
-def attn_fwd_kernel(rank_ref, q_ref, k_ref, v_ref, tab_ref, mask_ref, o_ref, lse_ref):
-    rank = rank_ref[0]
+def split_refs(refs, sizes):
+    out, at = [], 0
+    for size in sizes:
+        out.append(refs[at : at + size])
+        at += size
+    return out
+
+
+def ticker(plan, ins, outs, scratch, ticks):
+    if plan is None:
+        return lambda block, blocks: None
+    steps = plan.steps(ins, outs, scratch)
+
+    def tick(block, blocks):
+        for number, step in enumerate(steps):
+            at = min(number * ticks // (len(steps) - 1), ticks - 1) if number < len(steps) - 1 else ticks
+            if at < ticks and at % blocks == block:
+                pl.when(pl.program_id(0) == at // blocks)(step)
+            if at == ticks and block == blocks:
+                pl.when(pl.program_id(0) == ticks // blocks - 1)(step)
+
+    return tick
+
+
+def attn_fwd_kernel(plan, *refs):
+    n_in, n_out = (len(plan.in_specs), len(plan.out_specs)) if plan else (0, 0)
+    own, plan_in, (o_ref, lse_ref), plan_out, plan_scratch = split_refs(refs, (5, n_in, 2, n_out, len(refs)))
+    q_ref, k_ref, v_ref, tab_ref, mask_ref = own
+    rank = lax.axis_index("tensor")
     rows, keys = q_ref.shape[0], k_ref.shape[0]
     own_blocks, key_blocks = rows // BLK, keys // BLK
     low = lax.broadcasted_iota(jnp.int32, (BLK, 2 * HEAD), 1) < HEAD
+    tick = ticker(plan, plan_in, plan_out, plan_scratch, own_blocks * pl.num_programs(0))
     for b in range(own_blocks):
+        tick(b, own_blocks)
         q_blk = q_ref[b * BLK : (b + 1) * BLK, :] * jnp.asarray(HEAD**-0.5, jnp.bfloat16)
         results = []
         for hh, q_one in enumerate(halves(q_blk)):
@@ -95,40 +127,48 @@
             first = (hh * own_blocks + b) * BLK
             lse_ref[0, first : first + BLK, :] = peak + jnp.log(total)
         o_ref[b * BLK : (b + 1) * BLK, :] = jnp.where(low, results[0], results[1]).astype(jnp.bfloat16)
-
-
-def attn_fwd(rank, q, k, v, tab2, mask):
+    tick(own_blocks, own_blocks)
+
+
+def attn_fwd(q, k, v, tab2, mask, plan=None, collective_id=None):
     rows, width = q.shape
     keys = k.shape[0]
     pairs = width // (2 * HEAD)
-    col = lambda n: pl.BlockSpec((n, 2 * HEAD), lambda p, r: (0, p))
-    return pl.pallas_call(
-        attn_fwd_kernel,
-        grid_spec=pltpu.PrefetchScalarGridSpec(
-            num_scalar_prefetch=1,
-            grid=(pairs,),
-            in_specs=[
-                col(rows),
-                col(keys),
-                col(keys),
-                pl.BlockSpec((SPAN, 2 * HEAD), lambda p, r: (0, 0)),
-                pl.BlockSpec((1, keys), lambda p, r: (0, 0)),
-            ],
-            out_specs=[col(rows), pl.BlockSpec((1, 2 * rows, 1), lambda p, r: (p, 0, 0))],
+    col = lambda n: pl.BlockSpec((n, 2 * HEAD), lambda p: (0, p))
+    out_specs = [col(rows), pl.BlockSpec((1, 2 * rows, 1), lambda p: (p, 0, 0))]
+    out_shape = [
+        jax.ShapeDtypeStruct((rows, width), jnp.bfloat16),
+        jax.ShapeDtypeStruct((pairs, 2 * rows, 1), jnp.float32),
+    ]
+    outs = pl.pallas_call(
+        functools.partial(attn_fwd_kernel, plan),
+        grid=(pairs,),
+        in_specs=[
+            col(rows),
+            col(keys),
+            col(keys),
+            pl.BlockSpec((SPAN, 2 * HEAD), lambda p: (0, 0)),
+            pl.BlockSpec((1, keys), lambda p: (0, 0)),
+        ]
+        + (plan.in_specs if plan else []),
+        out_specs=out_specs + (plan.out_specs if plan else []),
+        out_shape=out_shape + (plan.out_shape if plan else []),
+        scratch_shapes=plan.scratch if plan else [],
+        compiler_params=pltpu.CompilerParams(
+            collective_id=collective_id, has_side_effects=plan is not None, vmem_limit_bytes=VMEM_LIMIT
         ),
-        out_shape=[
-            jax.ShapeDtypeStruct((rows, width), jnp.bfloat16),
-            jax.ShapeDtypeStruct((pairs, 2 * rows, 1), jnp.float32),
-        ],
         name="attn_fwd",
-    )(rank, q, k, v, tab2, mask)
-
-
-def attn_bwd_kernel(
-    rank_ref, q_ref, k_ref, v_ref, do_ref, o_ref, lse_ref, tab_ref, mask_ref,
-    dq_ref, dk_ref, dv_ref, dtab_ref, p_sc, ds_sc, q_sc, do_sc,
-):
-    rank = rank_ref[0]
+    )(q, k, v, tab2, mask, *(plan.args if plan else []))
+    return outs[0], outs[1], plan.results(outs[2:]) if plan else []
+
+
+def attn_bwd_kernel(plan, *refs):
+    n_in, n_out = (len(plan.in_specs), len(plan.out_specs)) if plan else (0, 0)
+    own, plan_in, own_out, plan_out, own_scratch, plan_scratch = split_refs(refs, (8, n_in, 4, n_out, 4, len(refs)))
+    q_ref, k_ref, v_ref, do_ref, o_ref, lse_ref, tab_ref, mask_ref = own
+    dq_ref, dk_ref, dv_ref, dtab_ref = own_out
+    p_sc, ds_sc, q_sc, do_sc = own_scratch
+    rank = lax.axis_index("tensor")
     rows, keys = q_ref.shape[0], k_ref.shape[0]
     own_blocks, key_blocks = rows // BLK, keys // BLK
     low = lax.broadcasted_iota(jnp.int32, (BLK, 2 * HEAD), 1) < HEAD
@@ -139,7 +179,9 @@
     def _():
         dtab_ref[...] = jnp.zeros_like(dtab_ref)
 
+    tick = ticker(plan, plan_in, plan_out, plan_scratch, own_blocks * pl.num_programs(0))
     for b in range(own_blocks):
+        tick(b, own_blocks)
         at = slice(b * BLK, (b + 1) * BLK)
         q_blk = q_ref[at, :] * scale
         do_blk = do_ref[at, :]
@@ -202,44 +244,50 @@
         dq_ref[at, :] = (jnp.where(low, results[0], results[1]) * HEAD**-0.5).astype(jnp.bfloat16)
     dk_ref[...] = dot_tn(ds_sc[...], q_sc[...]).astype(dk_ref.dtype)
     dv_ref[...] = dot_tn(p_sc[...], do_sc[...]).astype(dv_ref.dtype)
-
-
-def attn_bwd(rank, q, k, v, do, o, lse, tab2, mask):
+    tick(own_blocks, own_blocks)
+
+
+def attn_bwd(q, k, v, do, o, lse, tab2, mask, plan=None, collective_id=None):
     rows, width = q.shape
     keys = k.shape[0]
     pairs = width // (2 * HEAD)
-    col = lambda n: pl.BlockSpec((n, 2 * HEAD), lambda p, r: (0, p))
-    return pl.pallas_call(
-        attn_bwd_kernel,
-        grid_spec=pltpu.PrefetchScalarGridSpec(
-            num_scalar_prefetch=1,
-            grid=(pairs,),
-            in_specs=[
-                col(rows),
-                col(keys),
-                col(keys),
-                col(rows),
-                col(rows),
-                pl.BlockSpec((1, 2 * rows, 1), lambda p, r: (p, 0, 0)),
-                pl.BlockSpec((SPAN, 2 * HEAD), lambda p, r: (0, 0)),
-                pl.BlockSpec((1, keys), lambda p, r: (0, 0)),
-            ],
-            out_specs=[col(rows), col(keys), col(keys), pl.BlockSpec((SPAN, 2 * HEAD), lambda p, r: (0, 0))],
-            scratch_shapes=[
-                pltpu.VMEM((2 * rows, keys), jnp.bfloat16),
-                pltpu.VMEM((2 * rows, keys), jnp.bfloat16),
-                pltpu.VMEM((2 * rows, 2 * HEAD), jnp.bfloat16),
-                pltpu.VMEM((2 * rows, 2 * HEAD), jnp.bfloat16),
-            ],
+    col = lambda n: pl.BlockSpec((n, 2 * HEAD), lambda p: (0, p))
+    table = pl.BlockSpec((SPAN, 2 * HEAD), lambda p: (0, 0))
+    out_shape = [
+        jax.ShapeDtypeStruct((rows, width), jnp.bfloat16),
+        jax.ShapeDtypeStruct((keys, width), jnp.bfloat16),
+        jax.ShapeDtypeStruct((keys, width), jnp.bfloat16),
+        jax.ShapeDtypeStruct((SPAN, 2 * HEAD), jnp.float32),
+    ]
+    outs = pl.pallas_call(
+        functools.partial(attn_bwd_kernel, plan),
+        grid=(pairs,),
+        in_specs=[
+            col(rows),
+            col(keys),
+            col(keys),
+            col(rows),
+            col(rows),
+            pl.BlockSpec((1, 2 * rows, 1), lambda p: (p, 0, 0)),
+            table,
+            pl.BlockSpec((1, keys), lambda p: (0, 0)),
+        ]
+        + (plan.in_specs if plan else []),
+        out_specs=[col(rows), col(keys), col(keys), table] + (plan.out_specs if plan else []),
+        out_shape=out_shape + (plan.out_shape if plan else []),
+        scratch_shapes=[
+            pltpu.VMEM((2 * rows, keys), jnp.bfloat16),
+            pltpu.VMEM((2 * rows, keys), jnp.bfloat16),
+            pltpu.VMEM((2 * rows, 2 * HEAD), jnp.bfloat16),
+            pltpu.VMEM((2 * rows, 2 * HEAD), jnp.bfloat16),
+        ]
+        + (plan.scratch if plan else []),
+        compiler_params=pltpu.CompilerParams(
+            collective_id=collective_id, has_side_effects=plan is not None, vmem_limit_bytes=VMEM_LIMIT
         ),
-        out_shape=[
-            jax.ShapeDtypeStruct((rows, width), jnp.bfloat16),
-            jax.ShapeDtypeStruct((keys, width), jnp.bfloat16),
-            jax.ShapeDtypeStruct((keys, width), jnp.bfloat16),
-            jax.ShapeDtypeStruct((SPAN, 2 * HEAD), jnp.float32),
-        ],
         name="attn_bwd",
-    )(rank, q, k, v, do, o, lse, tab2, mask)
+    )(q, k, v, do, o, lse, tab2, mask, *(plan.args if plan else []))
+    return (*outs[:4], plan.results(outs[4:]) if plan else [])
 
 
 def span_table(rel_table):
@@ -298,33 +346,58 @@
     )
 
 
+class Piece:
+    def __init__(self, source, lead, first, width):
+        self.source, self.lead, self.first, self.width = source, lead, first, width
+
+
+def pieces_of(parts, chunk):
+    return [
+        Piece(source, lead, first, min(chunk, cols - first))
+        for source, (n, cols) in enumerate(parts)
+        for lead in range(n)
+        for first in range(0, cols, chunk)
+    ]
+
+
+def run_all(copies, action):
+    for copy in copies:
+        getattr(copy, action)()
+
+
 class Gather:
-    ORDERS = ((0, 1, 2), (0, 2, 1))
-
-    def __init__(self, place, shard, whole, send, recv, local):
-        self.place, self.shard, self.whole = place, shard, whole
+    NORMAL = ((0, 1, 2), (0, 2, 1))
+    EARLY = ((2, 1, 0), (1, 2, 0))
+
+    def __init__(self, place, piece, orders, shard, whole, send, recv, local):
+        self.place, self.piece, self.orders = place, piece, orders
+        self.shard, self.whole = shard, whole
         self.send, self.recv, self.local = send, recv, local
         self.half = shard.shape[1] // 2
-        self.width = shard.shape[2]
 
     @staticmethod
     def slots(dims, n_tensor):
-        return sum(d - 1 for d in dims) + 2 * (n_tensor - 1)
+        return 2 * (sum(d - 1 for d in dims) + 2 * (n_tensor - 1))
 
     def slot(self, color, stage, step):
-        dims = self.place.dims
-        base = [0]
-        for axis in self.ORDERS[color]:
-            base.append(base[-1] + dims[axis] - 1)
-        base.append(base[-1] + self.place.n_tensor - 1)
-        return (color, base[stage] + step - 1)
+        place, order = self.place, self.orders[color]
+        sizes = [place.dims[x] - 1 for x in order] + [place.n_tensor - 1] * 2
+        return color * sum(sizes) + sum(sizes[:stage]) + step - 1
+
+    def columns(self, t):
+        piece = self.piece
+        return pl.ds(pl.multiple_of(t * self.shard.shape[2] + piece.first, 128), piece.width)
 
     def region(self, color, index, t):
-        cols = pl.ds(pl.multiple_of(t * self.width, 128), self.width)
-        return self.whole.at[(slice(None),) + tuple(index) + (pl.ds(color * self.half, self.half), cols)]
+        rows = pl.ds(color * self.half, self.half)
+        return self.whole.at[(self.piece.lead,) + tuple(index) + (rows, self.columns(t))]
+
+    def source(self, rows):
+        piece = self.piece
+        return self.shard.at[piece.lead, rows, pl.ds(piece.first, piece.width)]
 
     def index(self, color, stage, moved=None):
-        order, out = self.ORDERS[color], list(self.place.at)
+        order, out = self.orders[color], list(self.place.at)
         for axis in order[:stage]:
             out[axis] = slice(None)
         if moved is not None:
@@ -332,191 +405,149 @@
         return out
 
     def own(self):
-        cols = pl.ds(pl.multiple_of(self.place.t * self.width, 128), self.width)
-        there = self.whole.at[(slice(None),) + self.place.at + (slice(None), cols)]
-        return pltpu.make_async_copy(self.shard, there, self.local)
+        there = self.whole.at[(self.piece.lead,) + self.place.at + (slice(None), self.columns(self.place.t))]
+        return pltpu.make_async_copy(self.source(slice(None)), there, self.local)
 
     def copies(self, stage, arriving=False):
-        place = self.place
-        for color in (0, 1):
-            order = self.ORDERS[color]
+        place, t = self.place, self.place.t
+        for color, order in enumerate(self.orders):
+            in_one = place.dims[order[2]] > 2
+            if stage == 3 and in_one:
+                continue
             axis = order[stage] if stage < 3 else 3
             for step in range(1, place.size(axis)):
-                device, peer = place.peer(axis, step)
-                _, source = place.peer(axis, place.size(axis) - step)
+                device, _ = place.peer(axis, step)
+                _, origin = place.peer(axis, place.size(axis) - step)
                 slot = self.slot(color, stage, step)
-                sems = (self.send.at[slot], self.recv.at[slot])
-                t = place.t
                 if stage < 3:
-                    mine = self.region(color, self.index(color, stage), t)
-                    theirs = self.region(color, self.index(color, stage, source), t)
-                elif stage == 3:
-                    mine = self.region(color, self.index(color, 2), t)
-                    theirs = self.region(color, self.index(color, 2), source)
-                elif self.skip(3):
-                    mine = self.region(color, self.index(color, 3), t)
-                    theirs = self.region(color, self.index(color, 3), source)
+                    index, there, then = self.index(color, stage), self.index(color, stage, origin), t
                 else:
-                    index = self.index(color, 2, place.peer(order[2], 1)[1])
-                    mine = self.region(color, index, t)
-                    theirs = self.region(color, index, source)
-                if stage == 0:
-                    mine_src = self.shard.at[:, pl.ds(color * self.half, self.half), :]
-                else:
-                    mine_src = mine
-                if arriving:
-                    yield remote(theirs, theirs, *sems, device)
-                else:
-                    yield remote(mine_src, mine, *sems, device)
+                    if in_one:
+                        index = self.index(color, 3)
+                    elif stage == 3:
+                        index = self.index(color, 2)
+                    else:
+                        index = self.index(color, 2, place.peer(order[2], 1)[1])
+                    there, then = index, origin
+                mine, theirs = self.region(color, index, t), self.region(color, there, then)
+                origin_ref = self.source(pl.ds(color * self.half, self.half)) if stage == 0 else mine
+                sems = (self.send.at[slot], self.recv.at[slot], device)
+                yield remote(theirs, theirs, *sems) if arriving else remote(origin_ref, mine, *sems)
 
     def start(self, stage):
-        if self.skip(stage):
-            return
-        for copy in self.copies(stage):
-            copy.start()
-
-    def skip(self, stage):
-        return stage == 3 and max(self.place.dims[1:]) > 2
+        run_all(self.copies(stage), "start")
 
     def arrived(self, stage):
-        if self.skip(stage):
-            return
-        for copy in self.copies(stage, arriving=True):
-            copy.wait_recv()
+        run_all(self.copies(stage, arriving=True), "wait_recv")
 
     def sent(self, stage):
-        if self.skip(stage):
-            return
-        for copy in self.copies(stage):
-            copy.wait_send()
-
-
-def gather_kernel(dims, n_tensor, n, *refs):
-    shards, wholes = refs[:n], refs[n : 2 * n]
-    send, recv, local = refs[2 * n :]
-    place = Place(dims, n_tensor)
-    gathers = [
-        Gather(place, s, w, send.at[i], recv.at[i], local.at[i]) for i, (s, w) in enumerate(zip(shards, wholes))
-    ]
-    for g in gathers:
-        g.own().start()
-    place.barrier()
-    for g in gathers:
-        g.start(0)
-    for g in gathers:
-        g.own().wait()
-    for step in range(n + 2):
-        if step < n:
-            gathers[step].arrived(0)
-            gathers[step].start(1)
-        if 0 <= step - 1 < n:
-            gathers[step - 1].arrived(1)
-            gathers[step - 1].start(2)
-            gathers[step - 1].start(3)
-        if 0 <= step - 2 < n:
-            gathers[step - 2].arrived(2)
-            gathers[step - 2].start(4)
-    for g in gathers:
-        for stage in (3, 4):
-            g.arrived(stage)
-        for stage in range(5):
-            g.sent(stage)
-
-
-def gather_weights(shards, dims, n_tensor, collective_id):
-    n = len(shards)
-    n_a, n_b, n_c = dims
-    slots = Gather.slots(dims, n_tensor)
-    outs = pl.pallas_call(
-        functools.partial(gather_kernel, dims, n_tensor, n),
-        out_shape=[
-            jax.ShapeDtypeStruct((s.shape[0], n_a, n_b, n_c, s.shape[1], n_tensor * s.shape[2]), s.dtype) for s in shards
-        ],
-        in_specs=[VMEM] * n,
-        out_specs=[ANY] * n,
-        scratch_shapes=[
-            pltpu.SemaphoreType.DMA((n, 2, slots)),
-            pltpu.SemaphoreType.DMA((n, 2, slots)),
-            pltpu.SemaphoreType.DMA((n,)),
-        ],
-        compiler_params=pltpu.CompilerParams(collective_id=collective_id, has_side_effects=True),
-        name="gather_weights",
-    )(*shards)
-    return [o.reshape(o.shape[0], -1, o.shape[-1]) for o in outs]
-
-
-class Piece:
-    def __init__(self, source, lead, first, width):
-        self.source, self.lead, self.first, self.width = source, lead, first, width
-
-
-def pieces_of(shapes, n_tensor, chunk):
-    chunks, room = [], 0
-    for source, (n, _, cols) in enumerate(shapes):
-        cols //= n_tensor
-        for lead in range(n):
-            first = 0
-            while first < cols:
-                width = min(cols - first, chunk if room == 0 else room)
-                if room == 0:
-                    chunks.append([])
-                    room = chunk
-                chunks[-1].append(Piece(source, lead, first, width))
-                room -= width
-                first += width
-    return chunks
+        run_all(self.copies(stage), "wait_send")
+
+
+class GatherPlan:
+    def __init__(self, shards, dims, n_tensor, chunk=1024, every=6, depth=3):
+        self.dims, self.n_tensor, self.depth = dims, n_tensor, depth
+        self.args = list(shards)
+        self.pieces = pieces_of([(s.shape[0], s.shape[2]) for s in shards], chunk)
+        self.orders = [Gather.EARLY if i % every == 0 else Gather.NORMAL for i in range(len(self.pieces))]
+        count, slots = len(self.pieces), Gather.slots(dims, n_tensor)
+        self.in_specs = [VMEM] * len(shards)
+        self.out_specs = [ANY] * len(shards)
+        self.out_shape = [
+            jax.ShapeDtypeStruct((s.shape[0], *dims, s.shape[1], n_tensor * s.shape[2]), s.dtype) for s in shards
+        ]
+        self.scratch = [
+            pltpu.SemaphoreType.DMA((count, slots)),
+            pltpu.SemaphoreType.DMA((count, slots)),
+            pltpu.SemaphoreType.DMA((count,)),
+        ]
+
+    def results(self, outs):
+        return [o.reshape(o.shape[0], -1, o.shape[-1]) for o in outs]
+
+    def steps(self, shards, wholes, scratch):
+        send, recv, local = scratch
+        place = Place(self.dims, self.n_tensor)
+        gathers = [
+            Gather(place, p, orders, shards[p.source], wholes[p.source], send.at[i], recv.at[i], local.at[i])
+            for i, (p, orders) in enumerate(zip(self.pieces, self.orders))
+        ]
+        count, depth = len(gathers), self.depth
+
+        def begin():
+            for g in gathers:
+                g.own().start()
+            place.barrier()
+            for g in gathers:
+                g.start(0)
+            for g in gathers:
+                g.own().wait()
+
+        def step(i):
+            if i < count:
+                gathers[i].arrived(0)
+                gathers[i].start(1)
+            at = i - depth
+            if 0 <= at < count:
+                gathers[at].arrived(1)
+                gathers[at].start(2)
+                gathers[at].start(3)
+            at = i - 2 * depth
+            if 0 <= at < count:
+                gathers[at].arrived(2)
+                gathers[at].start(4)
+
+        def end():
+            for g in gathers:
+                g.arrived(3)
+                g.arrived(4)
+                for stage in range(5):
+                    g.sent(stage)
+
+        return [begin] + [functools.partial(step, i) for i in range(count + 2 * depth)] + [end]
 
 
 class Scatter:
-    ORDERS = ((2, 1, 0), (1, 2, 0))
-
-    def __init__(self, place, pieces, grads, outs, bufs, sems):
-        self.place, self.pieces, self.grads, self.outs = place, pieces, grads, outs
-        self.held, self.far, self.near, self.first, self.second, self.third = bufs
+    NORMAL = ((2, 1, 0), (1, 2, 0))
+    EARLY = ((0, 1, 2), (0, 2, 1))
+
+    def __init__(self, place, piece, orders, grad, out, held, far, near, bufs, sems):
+        self.place, self.piece, self.orders = place, piece, orders
+        self.grad, self.out = grad, out
+        self.held, self.far, self.near, self.bufs = held, far, near, bufs
         self.send, self.recv, self.local = sems
-        self.width = sum(p.width for p in pieces)
-        self.half = self.held.shape[3] // 2
-
-    def rows(self, color):
-        return pl.ds(color * self.half, self.half)
-
-    def slab(self, piece, t):
-        cols = pl.ds(pl.multiple_of(t * (self.grads[piece.source].shape[-1] // self.place.n_tensor) + piece.first, 128), piece.width)
-        return self.grads[piece.source].at[piece.lead, :, :, :, :, cols]
-
-    def columns(self):
-        at = 0
-        for number, piece in enumerate(self.pieces):
-            yield number, piece, pl.ds(at, piece.width)
-            at += piece.width
-
-    def loads(self):
-        for number, piece, cols in self.columns():
-            yield pltpu.make_async_copy(self.slab(piece, self.place.t), self.held.at[:, :, :, :, cols], self.local.at[number])
-
-    def tensor_copies(self):
+        self.half = held.shape[3] // 2
+
+    @staticmethod
+    def slots(dims, n_tensor):
+        return n_tensor - 1 + 2 * sum(d - 1 for d in dims)
+
+    @staticmethod
+    def left(order, stage):
+        return [x for x in (0, 1, 2) if x not in order[:stage]]
+
+    def slab(self, t):
+        piece = self.piece
+        first = t * (self.grad.shape[-1] // self.place.n_tensor) + piece.first
+        return self.grad.at[piece.lead, :, :, :, :, pl.ds(pl.multiple_of(first, 128), piece.width)]
+
+    def load(self):
+        return pltpu.make_async_copy(self.slab(self.place.t), self.held, self.local.at[0])
+
+    def near_loads(self):
         for step in range(1, self.place.n_tensor):
-            device, peer = self.place.peer(3, step)
-            for number, piece, cols in self.columns():
-                slot = (step - 1) * 2 + number
-                yield remote(
-                    self.slab(piece, peer), self.far.at[step - 1, :, :, :, :, cols], self.send.at[slot], self.recv.at[slot], device
-                )
-
-    def near_loads(self, slot):
-        for step in range(1, self.place.n_tensor):
-            yield pltpu.make_async_copy(
-                self.far.at[step - 1, :, :, :, :, pl.ds(0, self.width)],
-                self.near.at[slot, step - 1, :, :, :, :, pl.ds(0, self.width)],
-                self.local.at[1 + step],
-            )
+            yield pltpu.make_async_copy(self.far.at[step - 1], self.near.at[step - 1], self.local.at[step])
 
     def copies(self, stage):
         place = self.place
-        base = 2 * (place.n_tensor - 1)
-        cols = pl.ds(0, self.width)
-        for color in (0, 1):
-            order = self.ORDERS[color]
+        if stage == 0:
+            for step in range(1, place.n_tensor):
+                device, peer = place.peer(3, step)
+                sems = (self.send.at[step - 1], self.recv.at[step - 1], device)
+                yield remote(self.slab(peer), self.far.at[step - 1], *sems)
+            return
+        base = place.n_tensor - 1
+        for color, order in enumerate(self.orders):
             axis = order[stage - 1]
             for step in range(1, place.size(axis)):
                 device, there = place.peer(axis, step)
@@ -524,73 +555,59 @@
                 for done in order[: stage - 1]:
                     index[done] = place.at[done]
                 index[axis] = there
-                buf = (self.first, self.second, self.third)[stage - 1][color]
-                slot = base + sum(place.size(x) - 1 for x in order[: stage - 1]) + step - 1 + color * sum(d - 1 for d in place.dims)
-                whole = (slice(None),) * (len(buf.shape) - 2)
-                yield remote(
-                    self.held.at[tuple(index) + (self.rows(color), cols)],
-                    buf.at[(step - 1,) + whole[1:] + (slice(None), cols)],
-                    self.send.at[slot],
-                    self.recv.at[slot],
-                    device,
-                )
-
-    @staticmethod
-    def slots(dims, n_tensor):
-        return 2 * (n_tensor - 1) + 2 * sum(d - 1 for d in dims)
-
-    def add_tensor(self, slot):
+                slot = base + color * sum(d - 1 for d in place.dims)
+                slot += sum(place.size(x) - 1 for x in order[: stage - 1]) + step - 1
+                origin = self.held.at[tuple(index) + (pl.ds(color * self.half, self.half),)]
+                sems = (self.send.at[slot], self.recv.at[slot], device)
+                yield remote(origin, self.bufs[stage - 1][color].at[step - 1], *sems)
+
+    def add_tensor(self):
         n_a, n_b, n_c = self.place.dims
-        cols = slice(0, self.width)
 
         def body(i, _):
             at = (lax.div(i, n_b * n_c), lax.rem(lax.div(i, n_c), n_b), lax.rem(i, n_c))
-            total = self.held[at + (slice(None), cols)].astype(jnp.float32)
+            total = self.held[at].astype(jnp.float32)
             for step in range(1, self.place.n_tensor):
-                total = total + self.near[(slot, step - 1) + at + (slice(None), cols)].astype(jnp.float32)
-            self.held[at + (slice(None), cols)] = total.astype(jnp.bfloat16)
+                total = total + self.near[(step - 1,) + at].astype(jnp.float32)
+            self.held[at] = total.astype(jnp.bfloat16)
             return 0
 
         lax.fori_loop(0, n_a * n_b * n_c, body, 0)
 
     def add(self, stage):
-        place = self.place
-        cols = slice(0, self.width)
-        for color in (0, 1):
-            order = self.ORDERS[color]
+        place, piece = self.place, self.piece
+        for color, order in enumerate(self.orders):
             rows = slice(color * self.half, (color + 1) * self.half)
-            left = [x for x in (0, 1, 2) if x not in order[:stage]]
-            buf = (self.first, self.second)[stage - 1][color]
-            count = 1
-            for x in left:
-                count *= place.dims[x]
-
-            def body(i, _):
+            left = self.left(order, stage)
+            buf = self.bufs[stage - 1][color]
+
+            def total_at(where):
                 at = list(place.at)
-                if len(left) == 2:
-                    where = (lax.div(i, place.dims[left[1]]), lax.rem(i, place.dims[left[1]]))
-                else:
-                    where = (i,)
                 for x, w in zip(left, where):
                     at[x] = w
-                at = tuple(at) + (rows, cols)
+                at = tuple(at) + (rows,)
                 total = self.held[at].astype(jnp.float32)
                 for step in range(1, place.size(order[stage - 1])):
-                    total = total + buf[(step - 1,) + where + (slice(None), cols)].astype(jnp.float32)
+                    total = total + buf[(step - 1,) + where].astype(jnp.float32)
+                return at, total
+
+            def body(i, _):
+                if len(left) == 2:
+                    size = place.dims[left[1]]
+                    at, total = total_at((lax.div(i, size), lax.rem(i, size)))
+                else:
+                    at, total = total_at((i,))
                 self.held[at] = total.astype(jnp.bfloat16)
                 return 0
 
-            lax.fori_loop(0, count, body, 0)
-
-    def finish(self):
-        for _, piece, cols in self.columns():
-            cols = slice(cols.start, cols.start + cols.size)
-            for color in (0, 1):
-                rows = slice(color * self.half, (color + 1) * self.half)
-                total = self.held[self.place.at + (rows, cols)].astype(jnp.float32)
-                for step in range(1, self.place.dims[0]):
-                    total = total + self.third[color][step - 1, :, cols].astype(jnp.float32)
-                self.outs[piece.source][piece.lead, rows, piece.first : piece.first + piece.width] = total
+            if left:
+                count = 1
+                for x in left:
+                    count *= place.dims[x]
+                lax.fori_loop(0, count, body, 0)
+            else:
+                cols = slice(piece.first, piece.first + piece.width)
+                self.out[piece.lead, rows, cols] = total_at(())[1]
 
 
 class Total:
@@ -608,8 +625,8 @@
         base = sum(place.size(x) - 1 for x in self.AXES[:stage])
         for step in range(1, place.size(axis)):
             device, _ = place.peer(axis, step)
-            slot = base + step - 1
-            yield remote(self.value.at[stage], self.boxes[stage].at[step - 1], self.send.at[slot], self.recv.at[slot], device)
+            sems = (self.send.at[base + step - 1], self.recv.at[base + step - 1], device)
+            yield remote(self.value.at[stage], self.boxes[stage].at[step - 1], *sems)
 
     def add(self, stage):
         place, axis = self.place, self.AXES[stage]
@@ -630,143 +647,140 @@
             self.value[stage + 1] = total
 
 
-def scatter_kernel(dims, n_tensor, plan, n, has_total, *refs):
-    count = len(plan)
-    refs = list(refs)
-    take = lambda k: [refs.pop(0) for _ in range(k)]
-    grads = take(n)
-    vec = take(1)[0] if has_total else None
-    outs = take(n)
-    vec_out = take(1)[0] if has_total else None
-    (far,) = take(1)
-    held, near, x0, x1, y0, y1, z0, z1, send, recv, local = take(11)
-    place = Place(dims, n_tensor)
-    chunks = [
-        Scatter(
-            place, pieces, grads, outs,
-            (held.at[i], far.at[i], near, (x0.at[i], x1.at[i]), (y0.at[i], y1.at[i]), (z0.at[i], z1.at[i])),
-            (send.at[i], recv.at[i], local.at[i]),
-        )
-        for i, pieces in enumerate(plan)
-    ]
-    for c in chunks:
-        for copy in c.loads():
-            copy.start()
-    total = None
-    if has_total:
-        value, *rest = take(7)
-        total = Total(place, value, vec_out, rest[:4], rest[4], rest[5])
-        value[0] = vec[...]
-    place.barrier()
-    if total is not None:
-        for copy in total.copies(0):
-            copy.start()
-    for c in chunks:
-        for copy in c.tensor_copies():
-            copy.start()
-
-    def fetch(i):
-        for copy in chunks[i].tensor_copies():
-            copy.wait_recv()
-        for copy in chunks[i].near_loads(i % 2):
-            copy.start()
-
-    fetch(0)
-    for step in range(max(count + 3, 4 if has_total else 0)):
-        if step < count:
-            c = chunks[step]
-            for copy in c.loads():
-                copy.wait()
-            for copy in c.near_loads(step % 2):
-                copy.wait()
-            if step + 1 < count:
-                fetch(step + 1)
-            c.add_tensor(step % 2)
-            for copy in c.copies(1):
-                copy.start()
-        for stage in (1, 2):
-            at = step - stage
-            if 0 <= at < count:
-                for copy in chunks[at].copies(stage):
-                    copy.wait_recv()
-                chunks[at].add(stage)
-                for copy in chunks[at].copies(stage + 1):
-                    copy.start()
-        if 0 <= step - 3 < count:
-            for copy in chunks[step - 3].copies(3):
-                copy.wait_recv()
-            chunks[step - 3].finish()
-        if total is not None and step < 4:
-            for copy in total.copies(step):
-                copy.wait_recv()
-            total.add(step)
-            if step < 3:
-                for copy in total.copies(step + 1):
-                    copy.start()
-    for c in chunks:
-        for copy in c.tensor_copies():
-            copy.wait_send()
-        for stage in (1, 2, 3):
-            for copy in c.copies(stage):
-                copy.wait_send()
-    if total is not None:
-        for stage in range(4):
-            for copy in total.copies(stage):
-                copy.wait_send()
-
-
-def scatter_grads(grads, vec, dims, n_tensor, collective_id, chunk=1024):
-    n_a, n_b, n_c = dims
-    places = n_a * n_b * n_c
-    rows = grads[0].shape[1] // places
-    plan = pieces_of([g.shape for g in grads], n_tensor, chunk)
-    count = len(plan)
-    chunk = max(sum(p.width for p in pieces) for pieces in plan)
-    views = [g.reshape(g.shape[0], n_a, n_b, n_c, rows, g.shape[2]) for g in grads]
-    n = len(grads)
-    half = rows // 2
-    bf = jnp.bfloat16
-    slots = Scatter.slots(dims, n_tensor)
-    out_shape = [jax.ShapeDtypeStruct((g.shape[0], rows, g.shape[2] // n_tensor), jnp.float32) for g in grads]
-    out_specs = [VMEM] * n
-    scratch = [
-        pltpu.VMEM((count, n_a, n_b, n_c, rows, chunk), bf),
-        pltpu.VMEM((2, n_tensor - 1, n_a, n_b, n_c, rows, chunk), bf),
-        pltpu.VMEM((count, n_c - 1, n_a, n_b, half, chunk), bf),
-        pltpu.VMEM((count, n_b - 1, n_a, n_c, half, chunk), bf),
-        pltpu.VMEM((count, n_b - 1, n_a, half, chunk), bf),
-        pltpu.VMEM((count, n_c - 1, n_a, half, chunk), bf),
-        pltpu.VMEM((count, n_a - 1, half, chunk), bf),
-        pltpu.VMEM((count, n_a - 1, half, chunk), bf),
-        pltpu.SemaphoreType.DMA((count, slots)),
-        pltpu.SemaphoreType.DMA((count, slots)),
-        pltpu.SemaphoreType.DMA((count, 1 + n_tensor)),
-    ]
-    args, in_specs = list(views), [ANY] * n
-    has_total = vec is not None
-    if has_total:
-        args.append(vec)
-        in_specs.append(VMEM)
-        out_shape.append(jax.ShapeDtypeStruct(vec.shape, vec.dtype))
-        out_specs.append(VMEM)
-        box = lambda k: pltpu.VMEM((k - 1,) + vec.shape, vec.dtype)
-        t_slots = Total.slots(dims, n_tensor)
-        scratch += [pltpu.VMEM((4,) + vec.shape, vec.dtype), box(n_tensor), box(n_c), box(n_b), box(n_a)]
-        scratch += [pltpu.SemaphoreType.DMA((t_slots,)), pltpu.SemaphoreType.DMA((t_slots,))]
-    out_shape.append(jax.ShapeDtypeStruct((count, n_tensor - 1, n_a, n_b, n_c, rows, chunk), bf))
-    out_specs.append(ANY)
+class ScatterPlan:
+    def __init__(self, grads, vec, dims, n_tensor, chunk=512, every=6, depth=2):
+        self.dims, self.n_tensor, self.has_total = dims, n_tensor, vec is not None
+        self.depth = depth
+        n_a, n_b, n_c = dims
+        rows = grads[0].shape[1] // (n_a * n_b * n_c)
+        parts = [(g.shape[0], g.shape[2] // n_tensor) for g in grads]
+        chunk = min(chunk, *(cols for _, cols in parts))
+        self.pieces = pieces_of(parts, chunk)
+        count, slots = len(self.pieces), Scatter.slots(dims, n_tensor)
+        kinds = [0 if i % every else 1 for i in range(count)]
+        self.places = [(k, kinds[:i].count(k)) for i, k in enumerate(kinds)]
+        self.args = [g.reshape(g.shape[0], n_a, n_b, n_c, rows, g.shape[2]) for g in grads]
+        self.in_specs = [ANY] * len(grads)
+        self.out_shape = [jax.ShapeDtypeStruct((g.shape[0], rows, g.shape[2] // n_tensor), jnp.float32) for g in grads]
+        self.out_specs = [VMEM] * len(grads)
+        bf, half = jnp.bfloat16, rows // 2
+        self.scratch = [
+            pltpu.VMEM((count, n_a, n_b, n_c, rows, chunk), bf),
+            pltpu.VMEM((2, n_tensor - 1, n_a, n_b, n_c, rows, chunk), bf),
+            pltpu.SemaphoreType.DMA((count, slots)),
+            pltpu.SemaphoreType.DMA((count, slots)),
+            pltpu.SemaphoreType.DMA((count, n_tensor)),
+        ]
+        for kind, orders in enumerate((Scatter.NORMAL, Scatter.EARLY)):
+            for stage in (1, 2, 3):
+                for order in orders:
+                    left = [dims[x] for x in Scatter.left(order, stage)]
+                    shape = (max(kinds.count(kind), 1), dims[order[stage - 1]] - 1, *left, half, chunk)
+                    self.scratch.append(pltpu.VMEM(shape, bf))
+        if self.has_total:
+            self.args.append(vec)
+            self.in_specs.append(VMEM)
+            self.out_shape.append(jax.ShapeDtypeStruct(vec.shape, vec.dtype))
+            self.out_specs.append(VMEM)
+            self.scratch.append(pltpu.VMEM((4,) + vec.shape, vec.dtype))
+            self.scratch += [pltpu.VMEM((k - 1,) + vec.shape, vec.dtype) for k in (n_tensor, n_c, n_b, n_a)]
+            self.scratch += [pltpu.SemaphoreType.DMA((Total.slots(dims, n_tensor),))] * 2
+        self.out_shape.append(jax.ShapeDtypeStruct((count, n_tensor - 1, n_a, n_b, n_c, rows, chunk), bf))
+        self.out_specs.append(ANY)
+
+    def results(self, outs):
+        return list(outs[:-1])
+
+    def steps(self, ins, outs, scratch):
+        place = Place(self.dims, self.n_tensor)
+        far = outs[-1]
+        held, near, send, recv, local = scratch[:5]
+        chunks = []
+        for i, (piece, (kind, at)) in enumerate(zip(self.pieces, self.places)):
+            orders = (Scatter.NORMAL, Scatter.EARLY)[kind]
+            boxes = scratch[5 + 6 * kind : 11 + 6 * kind]
+            bufs = [[boxes[2 * stage + color].at[at] for color in (0, 1)] for stage in range(3)]
+            chunks.append(
+                Scatter(
+                    place, piece, orders, ins[piece.source], outs[piece.source], held.at[i], far.at[i],
+                    near.at[i % 2], bufs, (send.at[i], recv.at[i], local.at[i]),
+                )
+            )
+        count, depth = len(chunks), self.depth
+        total = None
+        if self.has_total:
+            value, *rest = scratch[17:]
+            total = Total(place, value, outs[-2], rest[:4], rest[4], rest[5])
+
+        def fetch(i):
+            run_all(chunks[i].copies(0), "wait_recv")
+            run_all(chunks[i].near_loads(), "start")
+
+        def begin():
+            for c in chunks:
+                c.load().start()
+            if total is not None:
+                value[0] = ins[-1][...]
+            place.barrier()
+            if total is not None:
+                run_all(total.copies(0), "start")
+            for c in chunks:
+                run_all(c.copies(0), "start")
+
+        def step(i):
+            if i == 0:
+                fetch(0)
+            if i < count:
+                chunks[i].load().wait()
+                run_all(chunks[i].near_loads(), "wait")
+                if i + 1 < count:
+                    fetch(i + 1)
+                chunks[i].add_tensor()
+                run_all(chunks[i].copies(1), "start")
+            for stage in (1, 2, 3):
+                if 0 <= i - depth * stage < count:
+                    c = chunks[i - depth * stage]
+                    run_all(c.copies(stage), "wait_recv")
+                    c.add(stage)
+                    if stage < 3:
+                        run_all(c.copies(stage + 1), "start")
+            if total is not None and i < 4:
+                run_all(total.copies(i), "wait_recv")
+                total.add(i)
+                if i < 3:
+                    run_all(total.copies(i + 1), "start")
+
+        def end():
+            for c in chunks:
+                for stage in range(4):
+                    run_all(c.copies(stage), "wait_send")
+            if total is not None:
+                for stage in range(4):
+                    run_all(total.copies(stage), "wait_send")
+
+        last = max(count + 3 * depth, 4 if self.has_total else 0)
+        return [begin] + [functools.partial(step, i) for i in range(last)] + [end]
+
+
+def plan_kernel(plan, *refs):
+    n_in, n_out = len(plan.in_specs), len(plan.out_specs)
+    for step in plan.steps(refs[:n_in], refs[n_in : n_in + n_out], refs[n_in + n_out :]):
+        step()
+
+
+def run_plan(plan, collective_id, name):
     outs = pl.pallas_call(
-        functools.partial(scatter_kernel, dims, n_tensor, plan, n, has_total),
-        out_shape=out_shape,
-        in_specs=in_specs,
-        out_specs=out_specs,
-        scratch_shapes=scratch,
+        functools.partial(plan_kernel, plan),
+        out_shape=plan.out_shape,
+        in_specs=plan.in_specs,
+        out_specs=plan.out_specs,
+        scratch_shapes=plan.scratch,
         compiler_params=pltpu.CompilerParams(
-            collective_id=collective_id, has_side_effects=True, vmem_limit_bytes=66_000_000
+            collective_id=collective_id, has_side_effects=True, vmem_limit_bytes=VMEM_LIMIT
         ),
-        name="scatter_grads",
-    )(*args)
-    return outs[:n], (outs[n] if has_total else None)
+        name=name,
+    )(*plan.args)
+    return plan.results(outs)
 
 
 def exchange_kernel(dims, n_tensor, n, *refs):
@@ -937,12 +951,10 @@
     rank = lax.axis_index("tensor")
     rows, width = stream_in.shape
     keys = rows * n_tensor
-    shards = [
-        first_up[None], first_down.T[None], attn_proj, attn_out.T[None],
-        glu_weight, conv_out.T[None], second_up[None], second_down.T[None],
-    ]
-    gathered = gather_weights(shards, dims, n_tensor, 0)
-    (up_one,), (down_one,), proj, (out_attn,), glu, (out_conv,), (up_two,), (down_two,) = gathered
+    early = [first_up[None], first_down.T[None], attn_proj, attn_out.T[None]]
+    late = [glu_weight, conv_out.T[None], second_up[None], second_down.T[None]]
+    gathered = run_plan(GatherPlan(early, dims, n_tensor), 0, "gather_weights")
+    (up_one,), (down_one,), proj, (out_attn,) = gathered
 
     def enter(stream, row):
         result, normed, inv_std = norm_forward(stream, norm_gains[row], norm_shifts[row])
@@ -971,8 +983,10 @@
     place = lax.rem(jnp.arange(keys, dtype=jnp.int32) + rank * rows, keys)
     mask = jnp.where(place < clip_lengths[0], 0.0, MASKED).astype(jnp.float32)[None]
     table = span_table(rel_table)
-    rank_list = rank.astype(jnp.int32)[None]
-    attended, log_totals = attn_fwd(rank_list, query, key_rows, val_rows, table, mask)
+    attended, log_totals, gathered = attn_fwd(
+        query, key_rows, val_rows, table, mask, GatherPlan(late, dims, n_tensor, *HOST_G), 4
+    )
+    glu, (out_conv,), (up_two,), (down_two,) = gathered
     branch = dot_nt(attended, out_attn)
     squares.append(jnp.sum(branch * branch))
     stream = stream + branch
@@ -1021,9 +1035,12 @@
     grad_low = low(grad_stream)
     grad_attn_out = low(dot_tn(grad_low, attended))
     grad_attended = low(dot_nn(grad_low, out_attn))
-    grad_query, grad_keys, grad_vals, grad_span = attn_bwd(
-        rank_list, query, key_rows, val_rows, grad_attended, attended, log_totals, table, mask
+    grads = [g[None] for g in (grad_down_two, grad_up_two, grad_conv_out, *grad_glu)]
+    grad_query, grad_keys, grad_vals, grad_span, summed = attn_bwd(
+        query, key_rows, val_rows, grad_attended, attended, log_totals, table, mask,
+        ScatterPlan(grads, None, dims, n_tensor, *HOST_S), 5,
     )
+    s_down_two, s_up_two, s_conv, s_glu0, s_glu1 = (s[0] for s in summed)
     grad_keys, grad_vals = return_rows([grad_keys, grad_vals], dims, n_tensor, 3)
     grad_parts = (grad_query, grad_keys, grad_vals)
     grad_proj = [low(dot_tn(entered_b, g)) for g in grad_parts]
@@ -1049,11 +1066,9 @@
     ]
     vec = jnp.concatenate(parts, axis=0)
     vec = jnp.pad(vec, ((0, -vec.shape[0] % 8), (0, 0)))
-    grads = [
-        grad_down_two, grad_up_two, grad_conv_out, *grad_glu, grad_attn_out, *grad_proj, grad_down_one, grad_up_one,
-    ]
-    summed, vec = scatter_grads([g[None] for g in grads], vec, dims, n_tensor, 1)
-    s_down_two, s_up_two, s_conv, s_glu0, s_glu1, s_attn, s_q, s_k, s_v, s_down_one, s_up_one = (s[0] for s in summed)
+    grads = [g[None] for g in (grad_attn_out, *grad_proj, grad_down_one, grad_up_one)]
+    *summed, vec = run_plan(ScatterPlan(grads, vec, dims, n_tensor), 1, "scatter_grads")
+    s_attn, s_q, s_k, s_v, s_down_one, s_up_one = (s[0] for s in summed)
     at = 0
     pieces = []
     for part in parts:

time: 897 us -> 785 us (0.88)
  Pallas kernels: 637 us -> 530 us
    pallas_call x4, Pallas kernels: 622 us -> 516 us  [the longest x2 270 us: run_plan(): pl.pallas_call(functools.partial(plan_kernel, plan), out_shape=plan.out_s...]
where the time goes in v2:
time: 785 us; the launch traced here: 779 us
  Pallas kernels  530 us (68%)
  matrix products  157 us (20%)
  other arithmetic  55.8 us (7%)
  local copies, waits for them, and re-layouts  29.4 us (4%)
    pallas_call x2, Pallas kernels, run_plan(): pl.pallas_call(functools.partial(plan_kernel, plan), out_shape=plan.out_s...  270 us
    pallas_call x1, Pallas kernels, attn_bwd(): pl.pallas_call(functools.partial(attn_bwd_kernel, plan), grid=(pairs,), i...  124 us
    pallas_call x1, Pallas kernels, attn_fwd(): pl.pallas_call(functools.partial(attn_fwd_kernel, plan), grid=(pairs,), i...  122 us
    dot_general x11, matrix products, dot_nn(): return jnp.dot(a, b, preferred_element_type=jnp.float32)  61 us
    dot_general x11, matrix products, dot_tn(): return lax.dot_general(a, b, TN, preferred_element_type=jnp.float32)  51.6 us
    dot_general x11, matrix products, dot_nt(): return lax.dot_general(a, b, NT, preferred_element_type=jnp.float32)  44.5 us
  transfers between devices with their start and end apart: 2, of which 1 were waited for; matrix products, arithmetic and copies ran while one was open for 2% of the time, Pallas kernels for 0%

profile of v2, /device:TPU:0, one launch (start us, length us, event | category | flops | bytes accessed | tf_op | source)
XLA Modules:
  0.0 778.7 jit_solution(14232242613159326478)
XLA Ops:
  0.7 1.0 fusion.171
  1.7 1.4 convert_reduce_fusion.1
  3.2 1.6 fusion.16
  4.9 127.8 %gather_weights.1 = (bf16[1,4,2,2,64,4096]{5,4,3,2,1,0:T(8,128)(2,1)}, bf16[1,4,2,2,64,4096]{5,4,3,2,1,0:T(8,128)(2,1)}, bf16[3,4,2,2,64,1024]{5,4,3,2,1,0:T(8,128)(2,1)}, bf16[1,4,2,2,64,1024]{5,4,3,2,1,0:T(8,128)(2,1)}) custom-call(bf16[1,64,2048]{2,1,0:T(8,128)(2,1)} %bitcast.235, bf16[1,64,2048]{2,1,0:T(8,128)(2,1)} %bitcast.236, ...), custom_call_target="tpu_custom_call" | custom-call | tf_op jit(solution)/shard_map/gather_weights/pallas_call | solution.py:772
  132.7 13.7 %multiply_convert_fusion.3 = (bf16[512,4096]{1,0:T(8,128)(2,1)}, f32[512,4096]{1,0:T(8,128)}) fusion(bf16[1024,4096]{1,0:T(8,128)(2,1)} %bitcast.381, bf16[512,1024]{1,0:T(8,128)(2,1)} %param.15, f32[1024]{0:T(1024)S(1)} %bitcast.377, f32[1024]{0:T(1024)S(1)} %bitcast.350, f32[512]{0:T(512)S(1)} %add_rsqrt_fusion.5, f32[512]{0:T(512)S(1)} %broadcast_multiply_fusion.17), kind=kOutput, calls=%fused_computation.63 | convolution fusion | flops 4308598784 | bytes 22032384 | tf_op jit(solution)/shard_map/dot_general | solution.py:34
  146.5 7.7 fusion.165
  156.5 2.4 convolution_convert_fusion.12.refs_1_
  158.8 2.2 convolution_convert_fusion.13.refs_0_
  161.1 2.2 convolution_convert_fusion.14.refs_0_
  163.4 1.3 gather_fusion
  166.3 5.9 exchange_rows.1
  172.9 122.1 %attn_fwd.1 = (bf16[512,1024]{1,0:T(8,128)(2,1)}, f32[8,1024,1]{2,1,0:T(8,128)}, bf16[2,4,2,2,64,1024]{5,4,3,2,1,0:T(8,128)(2,1)}, bf16[1,4,2,2,64,1024]{5,4,3,2...) custom-call(bf16[512,1024]{1,0:T(8,128)(2,1)} %convolution_convert_fusion.14.refs_0_,, ...), custom_call_target="tpu_custom_call" | custom-call | tf_op jit(solution)/shard_map/attn_fwd/pallas_call | solution.py:143
  295.0 2.8 fusion.167
  298.8 2.1 fusion.164
  301.7 1.5 add_divide_fusion.3
  303.3 2.6 fusion.173
  305.9 1.5 collective-permute-start
  308.3 9.0 %fusion.163 = (f32[512]{0:T(512)S(1)}, f32[512,1024]{1,0:T(8,128)S(1)}) fusion(f32[512,1024]{1,0:T(8,128)S(1)} %get-tuple-element.217, f32[1024]{0:T(1024)S(1)} %bitcast.315, f32[32,1024]{1,0:T(8,128)S(1)} %collective-permute-done, f32[1024]{0:T(1024)S(1)} %bitcast.317, f32[1024]{0:T(1024)S(1)} %bitcast.259, f32[1024]{0:T(1024)S(1)} %bitcast.261, ...), kind=kLoop, calls=%fused_computation.381 | loop fusion | flops 48233984 | bytes 4454400 | tf_op jit(solution)/shard_map/reduce_sum | solution.py:870
  319.0 2.1 fusion.162
  321.7 8.0 %multiply_convert_fusion.2 = (bf16[512,4096]{1,0:T(8,128)(2,1)S(1)}, f32[512,4096]{1,0:T(8,128)}) fusion(bf16[1024,4096]{1,0:T(8,128)(2,1)S(1)} %bitcast.390, f32[512,1024]{1,0:T(8,128)S(1)} %get-tuple-element.152, f32[1024]{0:T(1024)S(1)} %bitcast.379, f32[1024]{0:T(1024)S(1)} %bitcast.356, f32[512]{0:T(512)S(1)} %add_rsqrt_fusion.1, ...), kind=kOutput, calls=%fused_computation.61 | convolution fusion | flops 4308074496 | bytes 23080960 | tf_op jit(solution)/shard_map/dot_general | solution.py:34
  329.6 2.0 copy-done.102
  331.6 7.8 fusion.161
  340.6 1.9 fusion.20
  342.5 12.4 %multiply_convert_fusion.1 = bf16[512,4096]{1,0:T(8,128)(2,1)} fusion(f32[512,4096]{1,0:T(8,128)} %get-tuple-element.220, bf16[1024,4096]{1,0:T(8,128)(2,1)} %bitcast.392, bf16[512,1024]{1,0:T(8,128)(2,1)S(1)} %copy-done.20, f32[512,1024]{1,0:T(8,128)S(1)} %get-tuple-element.150, f32[512]{0:T(512)S(1)} %get-tuple-element.226, ...), kind=kOutput, calls=%fused_computation.60 | convolution fusion | flops 4319084544 | bytes 24129536 | tf_op jit(solution)/shard_map/dot_general | solution.py:34
  354.9 9.4 %multiply_reduce_fusion.36 = (f32[1024]{0:T(1024)}, f32[512]{0:T(512)S(1)}, f32[512]{0:T(512)S(1)}, f32[1024]{0:T(1024)}, f32[512,1024]{1,0:T(8,128)S(1)}) fusion(f32[512,1024]{1,0:T(8,128)S(1)} %get-tuple-element.152, f32[512]{0:T(512)S(1)} %add_rsqrt_fusion.1, f32[512]{0:T(512)S(1)} %broadcast_multiply_fusion.13, f32[1024]{0:T(1024)S(1)} %bitcast.357, ...), kind=kOutput, calls=%fused_computation.269 | convolution fusion | flops 4299682816 | bytes 16797696 | tf_op jit(solution)/shard_map/dot_general | solution.py:26
  364.3 9.2 %convolution_convert_fusion.2 = bf16[1024,4096]{1,0:T(8,128)(2,1)} fusion(bf16[512,4096]{1,0:T(8,128)(2,1)} %multiply_convert_fusion.1, f32[512,1024]{1,0:T(8,128)S(1)} %get-tuple-element.152, f32[1024]{0:T(1024)S(1)} %bitcast.380, f32[1024]{0:T(1024)S(1)} %bitcast.358, f32[512]{0:T(512)S(1)} %add_rsqrt_fusion.1, f32[512]{0:T(512)S(1)} %broadcast_multiply_fusion.13), kind=kOutput, calls=%fused_computation.67 | convolution fusion | flops 4301783040 | bytes 14692352 | tf_op jit(solution)/shard_map/dot_general | solution.py:30
  373.5 9.5 %convolution_convert_fusion.3 = bf16[1024,4096]{1,0:T(8,128)(2,1)} fusion(bf16[512,4096]{1,0:T(8,128)(2,1)} %copy-done.102, bf16[512,1024]{1,0:T(8,128)(2,1)S(1)} %copy-done.20, f32[512,1024]{1,0:T(8,128)S(1)} %get-tuple-element.150, f32[512]{0:T(512)S(1)} %get-tuple-element.226, f32[512]{0:T(512)S(1)} %get-tuple-element.227, f32[1024]{0:T(1024)S(1)} %bitcast.255, ...), kind=kOutput, calls=%fused_computation.68 | convolution fusion | flops 4304404480 | bytes 15740928 | tf_op jit(solution)/shard_map/dot_general | solution.py:30
  383.0 2.4 multiply_add_fusion.2
  385.3 2.9 multiply_reduce_fusion.37
  388.2 4.3 multiply_reduce_fusion.6
  392.5 1.3 collective-permute-start.1
  393.8 3.6 multiply_reduce_fusion.15
  397.4 3.1 multiply_reduce_fusion.24
  400.5 1.6 multiply_reduce_fusion.33
  402.1 2.6 convolution_convert_fusion.10
  404.7 3.8 stack.201
  408.5 1.2 pad.13
  409.7 11.2 %multiply_convert_fusion.6 = (bf16[512,1024]{1,0:T(8,128)(2,1)S(1)}, f32[512,1024]{1,0:T(8,128)S(1)}) fusion(f32[512,1024]{1,0:T(8,128)} %copy-done.3, f32[512,1024]{1,0:T(8,128)S(1)} %get-tuple-element.146, f32[1024]{0:T(1024)S(1)} %bitcast.316, f32[32,1024]{1,0:T(8,128)S(1)} %collective-permute-done.1, f32[1024]{0:T(1024)S(1)} %bitcast.318, ...), kind=kLoop, calls=%fused_computation.280 | loop fusion | flops 48758784 | bytes 7598080 | tf_op jit(solution)/shard_map/convert_element_type | solution.py:886
  421.7 2.6 convolution_convert_fusion.8
  424.3 1.3 fusion.174
  425.7 2.7 convolution_convert_fusion.9
  428.4 1.9 multiply_reduce_fusion.38
  431.0 0.9 copy-done.97
  431.8 2.3 convolution_convert_fusion.11.refs_3_
  434.1 124.0 %attn_bwd.1 = (bf16[512,1024]{1,0:T(8,128)(2,1)}, bf16[1024,1024]{1,0:T(8,128)(2,1)}, bf16[1024,1024]{1,0:T(8,128)(2,1)}, f32[512,128]{1,0:T(8,128)}, f32[1,64,2...) custom-call(bf16[512,1024]{1,0:T(8,128)(2,1)} %convolution_convert_f, ...), custom_call_target="tpu_custom_call" | custom-call | tf_op jit(solution)/shard_map/attn_bwd/pallas_call | solution.py:262
  558.1 7.9 %return_rows.1 = (bf16[512,1024]{1,0:T(8,128)(2,1)}, bf16[512,1024]{1,0:T(8,128)(2,1)}) custom-call(bf16[1024,1024]{1,0:T(8,128)(2,1)} %get-tuple-element.58.refs_0_, bf16[1024,1024]{1,0:T(8,128)(2,1)} %get-tuple-element.59.refs_1_), custom_call_target="tpu_custom_call" | custom-call | tf_op jit(solution)/shard_map/return_rows/pallas_call | solution.py:857
  566.0 2.7 fusion.176
  568.7 2.7 convolution_convert_fusion.5
  571.4 1.3 fusion.175
  572.8 2.6 convolution_convert_fusion.4
  575.4 2.0 multiply_reduce_fusion.39
  578.1 1.5 copy-done.101
  579.6 6.9 convolution_convert_fusion.1
  586.5 10.8 %multiply_convert_fusion = bf16[512,4096]{1,0:T(8,128)(2,1)S(1)} fusion(f32[512,4096]{1,0:T(8,128)} %get-tuple-element.216, bf16[1024,4096]{1,0:T(8,128)(2,1)} %bitcast.385, f32[512,1024]{1,0:T(8,128)S(1)} %multiply_add_fusion), kind=kOutput, calls=%fused_computation.59 | convolution fusion | flops 4314890240 | bytes 23068672 | tf_op jit(solution)/shard_map/dot_general | solution.py:34
  597.5 6.3 fusion.15
  603.7 7.4 convolution_convert_fusion
  611.2 2.6 convolution_convert_fusion.6
  614.2 2.7 convolution_convert_fusion.7
  618.8 142.5 %scatter_grads.1 = (f32[1,64,512]{2,1,0:T(8,128)}, f32[1,64,512]{2,1,0:T(8,128)}, f32[1,64,512]{2,1,0:T(8,128)}, f32[1,64,512]{2,1,0:T(8,128)}, f32[1,64,2048]{2...) custom-call(bf16[1,4,2,2,64,1024]{5,4,3,2,1,0:T(8,128)(2,1)} %bitcast.222, ...), custom_call_target="tpu_custom_call" | custom-call | tf_op jit(solution)/shard_map/scatter_grads/pallas_call | solution.py:772
  761.3 1.7 slice.551
  763.7 1.5 fusion.168
  765.2 1.2 sqrt_bitcast_fusion
  767.9 1.8 pad_maximum_fusion.2
  769.7 4.3 fusion.14
  (284 shorter events, 20.8 us)
Async XLA Ops:
  0.6 4.2 copy-start.48
  1.7 144.7 %copy-start.78 = (f32[1,1024]{1,0:T(1,128)}, f32[1,1024]{1,0:T(1,128)S(1)}, u32[]{:S(2)}) copy-start(f32[1,1024]{1,0:T(1,128)S(1)} %get-tuple-element.207) | copy-start | bytes 12292
  1.7 153.7 %copy-start.42 = (f32[1,1024]{1,0:T(1,128)}, f32[1,1024]{1,0:T(1,128)S(1)}, u32[]{:S(2)}) copy-start(f32[1,1024]{1,0:T(1,128)S(1)} %get-tuple-element.206) | copy-start | bytes 12292
  3.2 143.2 %copy-start.49 = (f32[512]{0:T(512)}, f32[512]{0:T(512)S(1)}, u32[]{:S(2)}) copy-start(f32[512]{0:T(512)S(1)} %broadcast_multiply_fusion.17) | copy-start | bytes 6148
  4.8 141.6 %copy-start.87 = (f32[512]{0:T(512)}, f32[512]{0:T(512)S(1)}, u32[]{:S(2)}) copy-start(f32[512]{0:T(512)S(1)} %add_rsqrt_fusion.5) | copy-start | bytes 6148
  4.9 141.6 %copy-start.93 = (f32[1,1024]{1,0:T(1,128)}, f32[1,1024]{1,0:T(1,128)S(1)}, u32[]{:S(2)}) copy-start(f32[1,1024]{1,0:T(1,128)S(1)} %get-tuple-element.213) | copy-start | bytes 12292
  132.7 13.8 %copy-start.8 = (bf16[512,1024]{1,0:T(8,128)(2,1)S(1)}, bf16[512,1024]{1,0:T(8,128)(2,1)}, u32[]{:S(2)}) copy-start(bf16[512,1024]{1,0:T(8,128)(2,1)} %param.15) | copy-start | bytes 3145732
  132.7 13.8 %copy-start.95 = (bf16[1,4,2,2,64,4096]{5,4,3,2,1,0:T(8,128)(2,1)S(1)}, bf16[1,4,2,2,64,4096]{5,4,3,2,1,0:T(8,128)(2,1)}, u32[]{:S(2)}) copy-start(bf16[1,4,2,2,64,4096]{5,4,3,2,1,0:T(8,128)(2,1)} %get-tuple-element.46) | copy-start | bytes 25165828
  146.4 8.1 %slice-start = ((s8[6291456]{0:T(1024)(128)(4,1)}), s8[4194304]{0:T(1024)(128)(4,1)S(1)}, s32[]{:S(2)}) async-start(s8[6291456]{0:T(1024)(128)(4,1)} %bitcast.216), calls=%async_computation | async-start | bytes 8388608
  146.5 8.1 %slice-start.1 = ((s8[6291456]{0:T(1024)(128)(4,1)}), s8[2097152]{0:T(1024)(128)(4,1)S(1)}, s32[]{:S(2)}) async-start(s8[6291456]{0:T(1024)(128)(4,1)} %bitcast.216), calls=%async_computation.1 | async-start | bytes 4194304
  155.4 5.6 copy-start.21
  156.4 4.6 copy-start.29
  295.0 3.8 copy-start.96
  297.9 3.8 copy-start.25
  297.9 5.4 copy-start.13
  300.9 17.6 %copy-start.5 = (f32[512,1024]{1,0:T(8,128)}, f32[512,1024]{1,0:T(8,128)S(1)}, u32[]{:S(2)}) copy-start(f32[512,1024]{1,0:T(8,128)S(1)} %get-tuple-element.156) | copy-start | bytes 6291460
  303.2 4.1 copy-start.41
  305.9 2.4 collective-permute-start
  317.4 4.0 slice-start.4
  385.3 16.7 %copy-start.15 = (f32[512,1024]{1,0:T(8,128)}, f32[512,1024]{1,0:T(8,128)S(1)}, u32[]{:S(2)}) copy-start(f32[512,1024]{1,0:T(8,128)S(1)} %get-tuple-element.164) | copy-start | bytes 6291460
  392.5 17.2 %collective-permute-start.1 = (f32[32,1024]{1,0:T(8,128)S(1)}, f32[32,1024]{1,0:T(8,128)S(1)}, u32[]{:S(2)}, u32[]{:S(2)}) collective-permute-start(f32[32,1024]{1,0:T(8,128)S(1)} %slice.616), channel_id=1, source_target_pairs={{1,0},{3,2},{5,4},{7,6},{9,8},{11,10},{13,12},{15,14},{17,16},{19,... | collective-permute-start | bytes 393224 | tf_op jit(solution)/shard_map/ppermute | solution.py:970
  409.7 11.2 %copy-start.4 = (f32[512,1024]{1,0:T(8,128)S(1)}, f32[512,1024]{1,0:T(8,128)}, u32[]{:S(2)}) copy-start(f32[512,1024]{1,0:T(8,128)} %copy-done.3) | copy-start | bytes 6291460
  409.7 11.2 %copy-start.7 = (f32[512,1024]{1,0:T(8,128)S(1)}, f32[512,1024]{1,0:T(8,128)}, u32[]{:S(2)}) copy-start(f32[512,1024]{1,0:T(8,128)} %get-tuple-element.218) | copy-start | bytes 6291460
  558.1 7.9 %copy-start.24 = (bf16[1,4,2,2,64,1024]{5,4,3,2,1,0:T(8,128)(2,1)S(1)}, bf16[1,4,2,2,64,1024]{5,4,3,2,1,0:T(8,128)(2,1)}, u32[]{:S(2)}) copy-start(bf16[1,4,2,2,64,1024]{5,4,3,2,1,0:T(8,128)(2,1)} %copy-done.23) | copy-start | bytes 6291460
  579.6 6.9 copy-start.17
  579.6 17.8 %slice-start.2 = ((s8[8388608]{0:T(1024)(128)(4,1)}), s8[4194304]{0:T(1024)(128)(4,1)S(1)}, s32[]{:S(2)}) async-start(s8[8388608]{0:T(1024)(128)(4,1)} %bitcast.382), calls=%async_computation.2 | async-start | bytes 8388608
  586.5 10.9 %copy-start.9 = (bf16[512,1024]{1,0:T(8,128)(2,1)S(1)}, bf16[512,1024]{1,0:T(8,128)(2,1)}, u32[]{:S(2)}) copy-start(bf16[512,1024]{1,0:T(8,128)(2,1)} %param.15) | copy-start | bytes 3145732
  586.5 10.9 %copy-start.50 = (f32[512]{0:T(512)S(1)}, f32[512]{0:T(512)}, u32[]{:S(2)}) copy-start(f32[512]{0:T(512)} %copy-done.49) | copy-start | bytes 6148
  586.5 10.9 %copy-start.79 = (f32[1,1024]{1,0:T(1,128)S(1)}, f32[1,1024]{1,0:T(1,128)}, u32[]{:S(2)}) copy-start(f32[1,1024]{1,0:T(1,128)} %copy-done.78) | copy-start | bytes 12292
  586.5 10.9 %copy-start.88 = (f32[512]{0:T(512)S(1)}, f32[512]{0:T(512)}, u32[]{:S(2)}) copy-start(f32[512]{0:T(512)} %copy-done.87) | copy-start | bytes 6148
  586.5 10.9 %slice-start.3 = ((s8[8388608]{0:T(1024)(128)(4,1)}), s8[4194304]{0:T(1024)(128)(4,1)S(1)}, s32[]{:S(2)}) async-start(s8[8388608]{0:T(1024)(128)(4,1)} %bitcast.382), calls=%async_computation.3 | async-start | bytes 8388608
  597.4 6.3 copy-start.94
  613.8 3.5 copy-start.51
  613.8 3.5 copy-start.52
  613.9 3.5 copy-start.53
  613.9 3.5 copy-start.54
  613.9 3.5 copy-start.55
  613.9 3.5 copy-start.56
  613.9 3.5 copy-start.57
  613.9 3.5 copy-start.58
  613.9 3.5 copy-start.59
  613.9 3.5 copy-start.60
  613.9 3.5 copy-start.61
  614.0 3.5 copy-start.62
  614.0 3.5 copy-start.63
  614.0 3.5 copy-start.64
  614.0 3.5 copy-start.65
  614.0 3.5 copy-start.66
  614.0 3.5 copy-start.67
  614.0 3.5 copy-start.68
  614.0 3.5 copy-start.69
  614.0 3.5 copy-start.70
  614.0 3.5 copy-start.71
  614.1 3.5 copy-start.72
  614.1 3.5 copy-start.73
  614.1 3.5 copy-start.74
  614.1 3.5 copy-start.75
  614.1 3.5 copy-start.76
  618.8 148.4 %copy-start.39 = (f32[1,64,512]{2,1,0:T(8,128)S(1)}, f32[1,64,512]{2,1,0:T(8,128)}, u32[]{:S(2)}) copy-start(f32[1,64,512]{2,1,0:T(8,128)} %get-tuple-element.70) | copy-start | bytes 393220
  618.8 148.4 %copy-start.40 = (f32[1,64,512]{2,1,0:T(8,128)S(1)}, f32[1,64,512]{2,1,0:T(8,128)}, u32[]{:S(2)}) copy-start(f32[1,64,512]{2,1,0:T(8,128)} %get-tuple-element.71) | copy-start | bytes 393220
  761.3 8.4 %copy-start.10 = (bf16[512,1024]{1,0:T(8,128)(2,1)S(1)}, bf16[512,1024]{1,0:T(8,128)(2,1)}, u32[]{:S(2)}) copy-start(bf16[512,1024]{1,0:T(8,128)(2,1)} %param.15) | copy-start | bytes 3145732
  769.7 4.3 copy-start.35
  769.7 5.1 copy-start.34
  774.0 3.7 copy-start.32
  (47 other events, 124.6 us)

commit v3 on v2

--- a/solution.py
+++ b/solution.py
@@ -15,7 +15,7 @@
 MASKED = -1e30
 VMEM_LIMIT = 66_000_000
 HOST_G = (512, 6, 5)
-HOST_S = (256, 8, 6)
+HOST_S = (256, 8, 4)
 BLK = 128
 SPAN = 512
 NT = (((1,), (1,)), ((), ()))
@@ -511,11 +511,11 @@
     NORMAL = ((2, 1, 0), (1, 2, 0))
     EARLY = ((0, 1, 2), (0, 2, 1))
 
-    def __init__(self, place, piece, orders, grad, out, held, far, near, bufs, sems):
+    def __init__(self, place, piece, orders, left_op, slabs, out, held, near, sent, bufs, sems):
         self.place, self.piece, self.orders = place, piece, orders
-        self.grad, self.out = grad, out
-        self.held, self.far, self.near, self.bufs = held, far, near, bufs
-        self.send, self.recv, self.local = sems
+        self.left_op, self.slabs, self.out = left_op, slabs, out
+        self.held, self.near, self.sent, self.bufs = held, near, sent, bufs
+        self.send, self.recv = sems
         self.half = held.shape[3] // 2
 
     @staticmethod
@@ -526,25 +526,31 @@
     def left(order, stage):
         return [x for x in (0, 1, 2) if x not in order[:stage]]
 
-    def slab(self, t):
-        piece = self.piece
-        first = t * (self.grad.shape[-1] // self.place.n_tensor) + piece.first
-        return self.grad.at[piece.lead, :, :, :, :, pl.ds(pl.multiple_of(first, 128), piece.width)]
-
-    def load(self):
-        return pltpu.make_async_copy(self.slab(self.place.t), self.held, self.local.at[0])
-
-    def near_loads(self):
-        for step in range(1, self.place.n_tensor):
-            yield pltpu.make_async_copy(self.far.at[step - 1], self.near.at[step - 1], self.local.at[step])
+    def product(self, t, target):
+        n_a, n_b, n_c = self.place.dims
+        rows = self.held.shape[3]
+        block = n_b * n_c * rows
+
+        def body(a, _):
+            lhs = self.left_op[pl.ds(pl.multiple_of(a * block, block), block), :]
+            value = dot_nn(lhs, self.slabs[t]).astype(jnp.bfloat16)
+            target[a] = value.reshape(n_b, n_c, rows, value.shape[-1])
+            return 0
+
+        lax.fori_loop(0, n_a, body, 0)
+
+    def compute(self):
+        for step, copy in enumerate(self.copies(0)):
+            self.product(self.place.peer(3, step + 1)[1], self.sent.at[step])
+            copy.start()
+        self.product(self.place.t, self.held)
 
     def copies(self, stage):
         place = self.place
         if stage == 0:
             for step in range(1, place.n_tensor):
-                device, peer = place.peer(3, step)
-                sems = (self.send.at[step - 1], self.recv.at[step - 1], device)
-                yield remote(self.slab(peer), self.far.at[step - 1], *sems)
+                sems = (self.send.at[step - 1], self.recv.at[step - 1], place.peer(3, step)[0])
+                yield remote(self.sent.at[step - 1], self.near.at[step - 1], *sems)
             return
         base = place.n_tensor - 1
         for color, order in enumerate(self.orders):
@@ -607,7 +613,7 @@
                 lax.fori_loop(0, count, body, 0)
             else:
                 cols = slice(piece.first, piece.first + piece.width)
-                self.out[piece.lead, rows, cols] = total_at(())[1]
+                self.out[rows, cols] = total_at(())[1]
 
 
 class Total:
@@ -648,28 +654,40 @@
 
 
 class ScatterPlan:
-    def __init__(self, grads, vec, dims, n_tensor, chunk=512, every=6, depth=2):
-        self.dims, self.n_tensor, self.has_total = dims, n_tensor, vec is not None
-        self.depth = depth
+    def __init__(self, terms, vec, dims, n_tensor, chunk=256, every=8, depth=4):
+        self.dims, self.n_tensor, self.has_total, self.depth = dims, n_tensor, vec is not None, depth
         n_a, n_b, n_c = dims
-        rows = grads[0].shape[1] // (n_a * n_b * n_c)
-        parts = [(g.shape[0], g.shape[2] // n_tensor) for g in grads]
+        tokens, width = terms[0][0].shape
+        rows = width // (n_a * n_b * n_c)
+        parts = [(1, right.shape[1] // n_tensor) for _, right in terms]
         chunk = min(chunk, *(cols for _, cols in parts))
         self.pieces = pieces_of(parts, chunk)
+        self.part_cols = [cols for _, cols in parts]
         count, slots = len(self.pieces), Scatter.slots(dims, n_tensor)
         kinds = [0 if i % every else 1 for i in range(count)]
         self.places = [(k, kinds[:i].count(k)) for i, k in enumerate(kinds)]
-        self.args = [g.reshape(g.shape[0], n_a, n_b, n_c, rows, g.shape[2]) for g in grads]
-        self.in_specs = [ANY] * len(grads)
-        self.out_shape = [jax.ShapeDtypeStruct((g.shape[0], rows, g.shape[2] // n_tensor), jnp.float32) for g in grads]
-        self.out_specs = [VMEM] * len(grads)
+        lefts = []
+        self.left_at = []
+        for left, _ in terms:
+            known = [i for i, other in enumerate(lefts) if other is left]
+            if not known:
+                lefts.append(left)
+            self.left_at.append(known[0] if known else len(lefts) - 1)
+        self.n_left = len(lefts)
+        self.args = lefts + [right for _, right in terms]
+        self.in_specs = [VMEM] * len(lefts) + [ANY] * len(terms)
+        self.out_shape = [jax.ShapeDtypeStruct((rows, cols), jnp.float32) for _, cols in parts]
+        self.out_specs = [VMEM] * len(terms)
         bf, half = jnp.bfloat16, rows // 2
         self.scratch = [
             pltpu.VMEM((count, n_a, n_b, n_c, rows, chunk), bf),
-            pltpu.VMEM((2, n_tensor - 1, n_a, n_b, n_c, rows, chunk), bf),
+            pltpu.VMEM((count, n_tensor - 1, n_a, n_b, n_c, rows, chunk), bf),
+            pltpu.VMEM((self.SENDS, n_tensor - 1, n_a, n_b, n_c, rows, chunk), bf),
+            pltpu.VMEM((2, n_tensor, tokens, chunk), bf),
+            pltpu.VMEM((len(lefts), width, tokens), bf),
             pltpu.SemaphoreType.DMA((count, slots)),
             pltpu.SemaphoreType.DMA((count, slots)),
-            pltpu.SemaphoreType.DMA((count, n_tensor)),
+            pltpu.SemaphoreType.DMA((2, n_tensor)),
         ]
         for kind, orders in enumerate((Scatter.NORMAL, Scatter.EARLY)):
             for stage in (1, 2, 3):
@@ -685,65 +703,82 @@
             self.scratch.append(pltpu.VMEM((4,) + vec.shape, vec.dtype))
             self.scratch += [pltpu.VMEM((k - 1,) + vec.shape, vec.dtype) for k in (n_tensor, n_c, n_b, n_a)]
             self.scratch += [pltpu.SemaphoreType.DMA((Total.slots(dims, n_tensor),))] * 2
-        self.out_shape.append(jax.ShapeDtypeStruct((count, n_tensor - 1, n_a, n_b, n_c, rows, chunk), bf))
-        self.out_specs.append(ANY)
+
+    SENDS = 3
 
     def results(self, outs):
-        return list(outs[:-1])
+        return list(outs)
 
     def steps(self, ins, outs, scratch):
         place = Place(self.dims, self.n_tensor)
-        far = outs[-1]
-        held, near, send, recv, local = scratch[:5]
+        held, near, sent, slabs, turned, send, recv, local = scratch[:8]
         chunks = []
         for i, (piece, (kind, at)) in enumerate(zip(self.pieces, self.places)):
             orders = (Scatter.NORMAL, Scatter.EARLY)[kind]
-            boxes = scratch[5 + 6 * kind : 11 + 6 * kind]
+            boxes = scratch[8 + 6 * kind : 14 + 6 * kind]
             bufs = [[boxes[2 * stage + color].at[at] for color in (0, 1)] for stage in range(3)]
             chunks.append(
                 Scatter(
-                    place, piece, orders, ins[piece.source], outs[piece.source], held.at[i], far.at[i],
-                    near.at[i % 2], bufs, (send.at[i], recv.at[i], local.at[i]),
+                    place, piece, orders, turned.at[self.left_at[piece.source]], slabs.at[i % 2], outs[piece.source],
+                    held.at[i], near.at[i], sent.at[i % self.SENDS], bufs, (send.at[i], recv.at[i]),
                 )
             )
         count, depth = len(chunks), self.depth
         total = None
         if self.has_total:
-            value, *rest = scratch[17:]
-            total = Total(place, value, outs[-2], rest[:4], rest[4], rest[5])
-
-        def fetch(i):
-            run_all(chunks[i].copies(0), "wait_recv")
-            run_all(chunks[i].near_loads(), "start")
+            value, *rest = scratch[20:]
+            total = Total(place, value, outs[-1], rest[:4], rest[4], rest[5])
+
+        def loads(i):
+            piece = self.pieces[i]
+            right = ins[self.n_left + piece.source]
+            for t in range(self.n_tensor):
+                cols = pl.ds(t * self.part_cols[piece.source] + piece.first, piece.width)
+                yield pltpu.make_async_copy(right.at[:, cols], slabs.at[i % 2, t], local.at[i % 2, t])
+
+        def turn(number):
+            block = 256
+
+            def body(a, _):
+                cols = pl.ds(pl.multiple_of(a * block, block), block)
+                turned[number, cols, :] = ins[number][:, cols].T
+                return 0
+
+            lax.fori_loop(0, turned.shape[1] // block, body, 0)
+
+        firsts = [next(i for i, p in enumerate(self.pieces) if self.left_at[p.source] == n) for n in range(self.n_left)]
 
         def begin():
-            for c in chunks:
-                c.load().start()
+            run_all(loads(0), "start")
             if total is not None:
                 value[0] = ins[-1][...]
             place.barrier()
             if total is not None:
                 run_all(total.copies(0), "start")
-            for c in chunks:
-                run_all(c.copies(0), "start")
 
         def step(i):
-            if i == 0:
-                fetch(0)
             if i < count:
-                chunks[i].load().wait()
-                run_all(chunks[i].near_loads(), "wait")
+                run_all(loads(i), "wait")
                 if i + 1 < count:
-                    fetch(i + 1)
-                chunks[i].add_tensor()
-                run_all(chunks[i].copies(1), "start")
+                    run_all(loads(i + 1), "start")
+                if i >= self.SENDS:
+                    run_all(chunks[i - self.SENDS].copies(0), "wait_send")
+                for number, first in enumerate(firsts):
+                    if first == i:
+                        turn(number)
+                chunks[i].compute()
+            if 0 <= i - 1 < count:
+                c = chunks[i - 1]
+                run_all(c.copies(0), "wait_recv")
+                c.add_tensor()
+                run_all(c.copies(1), "start")
             for stage in (1, 2, 3):
-                if 0 <= i - depth * stage < count:
-                    c = chunks[i - depth * stage]
-                    run_all(c.copies(stage), "wait_recv")
-                    c.add(stage)
+                at = i - 1 - depth * stage
+                if 0 <= at < count:
+                    run_all(chunks[at].copies(stage), "wait_recv")
+                    chunks[at].add(stage)
                     if stage < 3:
-                        run_all(c.copies(stage + 1), "start")
+                        run_all(chunks[at].copies(stage + 1), "start")
             if total is not None and i < 4:
                 run_all(total.copies(i), "wait_recv")
                 total.add(i)
@@ -751,14 +786,14 @@
                     run_all(total.copies(i + 1), "start")
 
         def end():
-            for c in chunks:
-                for stage in range(4):
+            for i, c in enumerate(chunks):
+                for stage in range(0 if i >= count - self.SENDS else 1, 4):
                     run_all(c.copies(stage), "wait_send")
             if total is not None:
                 for stage in range(4):
                     run_all(total.copies(stage), "wait_send")
 
-        last = max(count + 3 * depth, 4 if self.has_total else 0)
+        last = max(count + 1 + 3 * depth, 4 if self.has_total else 0)
         return [begin] + [functools.partial(step, i) for i in range(last)] + [end]
 
 
@@ -897,9 +932,7 @@
     sigma = jax.nn.sigmoid(before)
     grad_active = dot_nn(grad_low, weight_out_t)
     grad_before = low(grad_active * sigma * (1.0 + before * (1.0 - sigma)))
-    grad_in = low(dot_tn(entered, grad_before))
-    grad_out_t = low(dot_tn(grad_low, active))
-    return dot_nt(grad_before, weight_in), grad_in, grad_out_t
+    return dot_nt(grad_before, weight_in), [(grad_low, active), (entered, grad_before)]
 
 
 def taps_forward(signal, before, conv_taps):
@@ -1014,12 +1047,12 @@
 
     grad_stream, gain_e, shift_e = norm_back(grad_out.astype(jnp.float32), (normed_e, scale_e), 5)
     grad_low = low(0.5 * grad_stream)
-    grad_entered, grad_up_two, grad_down_two = ffn_backward(entered_d, ffn_d, grad_low, up_two, down_two)
+    grad_entered, terms_two = ffn_backward(entered_d, ffn_d, grad_low, up_two, down_two)
     grad_extra, gain_d, shift_d = norm_back(grad_entered, norm_d, 4)
     grad_stream = grad_stream + grad_extra
 
     grad_low = low(grad_stream)
-    grad_conv_out = low(dot_tn(grad_low, conv_act))
+    terms_mid = [(grad_low, conv_act)]
     sigma = jax.nn.sigmoid(shaped)
     grad_shaped = dot_nn(grad_low, out_conv) * sigma * (1.0 + shaped * (1.0 - sigma))
     grad_mixed, gain_mid, shift_mid = norm_back(grad_shaped, (normed_mid, scale_mid), 3)
@@ -1027,29 +1060,28 @@
     grad_gated, taps_grad = taps_backward(grad_mixed, grad_after, gated, gated_before, conv_taps)
     grad_first = low(grad_gated * sig_second)
     grad_second = low(grad_gated * glu_first * sig_second * (1.0 - sig_second))
-    grad_glu = [low(dot_tn(entered_c, g)) for g in (grad_first, grad_second)]
+    terms_mid += [(entered_c, g) for g in (grad_first, grad_second)]
     grad_entered = dot_nt(grad_first, glu[0]) + dot_nt(grad_second, glu[1])
     grad_extra, gain_c, shift_c = norm_back(grad_entered, norm_c, 2)
     grad_stream = grad_stream + grad_extra
 
     grad_low = low(grad_stream)
-    grad_attn_out = low(dot_tn(grad_low, attended))
+    terms_attn = [(grad_low, attended)]
     grad_attended = low(dot_nn(grad_low, out_attn))
-    grads = [g[None] for g in (grad_down_two, grad_up_two, grad_conv_out, *grad_glu)]
     grad_query, grad_keys, grad_vals, grad_span, summed = attn_bwd(
         query, key_rows, val_rows, grad_attended, attended, log_totals, table, mask,
-        ScatterPlan(grads, None, dims, n_tensor, *HOST_S), 5,
+        ScatterPlan(terms_two + terms_mid, None, dims, n_tensor, *HOST_S), 5,
     )
-    s_down_two, s_up_two, s_conv, s_glu0, s_glu1 = (s[0] for s in summed)
+    s_down_two, s_up_two, s_conv, s_glu0, s_glu1 = summed
     grad_keys, grad_vals = return_rows([grad_keys, grad_vals], dims, n_tensor, 3)
     grad_parts = (grad_query, grad_keys, grad_vals)
-    grad_proj = [low(dot_tn(entered_b, g)) for g in grad_parts]
+    terms_attn += [(entered_b, g) for g in grad_parts]
     grad_entered = sum(dot_nt(g, proj[i]) for i, g in enumerate(grad_parts))
     grad_extra, gain_b, shift_b = norm_back(grad_entered, norm_b, 1)
     grad_stream = grad_stream + grad_extra
 
     grad_low = low(0.5 * grad_stream)
-    grad_entered, grad_up_one, grad_down_one = ffn_backward(entered_a, ffn_a, grad_low, up_one, down_one)
+    grad_entered, terms_one = ffn_backward(entered_a, ffn_a, grad_low, up_one, down_one)
     grad_extra, gain_a, shift_a = norm_back(grad_entered, norm_a, 0)
     grad_stream = grad_stream + grad_extra
 
@@ -1066,9 +1098,8 @@
     ]
     vec = jnp.concatenate(parts, axis=0)
     vec = jnp.pad(vec, ((0, -vec.shape[0] % 8), (0, 0)))
-    grads = [g[None] for g in (grad_attn_out, *grad_proj, grad_down_one, grad_up_one)]
-    *summed, vec = run_plan(ScatterPlan(grads, vec, dims, n_tensor), 1, "scatter_grads")
-    s_attn, s_q, s_k, s_v, s_down_one, s_up_one = (s[0] for s in summed)
+    *summed, vec = run_plan(ScatterPlan(terms_attn + terms_one, vec, dims, n_tensor), 1, "scatter_grads")
+    s_attn, s_q, s_k, s_v, s_down_one, s_up_one = summed
     at = 0
     pieces = []
     for part in parts:

time: 785 us -> 763 us (0.972)
  matrix products: 157 us -> 103 us
  Pallas kernels: 530 us -> 558 us
    dot_general x11 -> x0, matrix products: 51.6 us -> none  [dot_tn(): return lax.dot_general(a, b, TN, preferred_element_type=jnp.float32)]
    pallas_call x1, Pallas kernels: 124 us -> 147 us  [attn_bwd(): pl.pallas_call(functools.partial(attn_bwd_kernel, plan), grid=(pairs,), i...]
    convert_element_type x5 -> x11, other arithmetic: 13.5 us -> 23.2 us  [low(): return value.astype(jnp.bfloat16)]
    unnamed x226 -> x146, local copies, waits for them, and re-layouts: 13.1 us -> 16.3 us
  transfers between devices with their start and end apart: 2 -> 2, of which waited for: 1 -> 1; matrix products, arithmetic and copies ran while one was open for 2% -> 1% of each run, Pallas kernels for 0% -> 0%
where the time goes in v3:
time: 763 us; the launch traced here: 757 us
  Pallas kernels  558 us (73%)
  matrix products  103 us (13%)
  other arithmetic  59.1 us (8%)
  local copies, waits for them, and re-layouts  31.9 us (4%)
    pallas_call x2, Pallas kernels, run_plan(): pl.pallas_call(functools.partial(plan_kernel, plan), out_shape=plan.out_s...  274 us
    pallas_call x1, Pallas kernels, attn_bwd(): pl.pallas_call(functools.partial(attn_bwd_kernel, plan), grid=(pairs,), i...  147 us
    pallas_call x1, Pallas kernels, attn_fwd(): pl.pallas_call(functools.partial(attn_fwd_kernel, plan), grid=(pairs,), i...  122 us
    dot_general x11, matrix products, dot_nn(): return jnp.dot(a, b, preferred_element_type=jnp.float32)  56.3 us
    dot_general x11, matrix products, dot_nt(): return lax.dot_general(a, b, NT, preferred_element_type=jnp.float32)  46.4 us
    convert_element_type x11, other arithmetic, low(): return value.astype(jnp.bfloat16)  23.2 us
    unnamed x146, local copies, waits for them, and re-layouts  16.3 us
  transfers between devices with their start and end apart: 2, of which 1 were waited for; matrix products, arithmetic and copies ran while one was open for 1% of the time, Pallas kernels for 0%

profile of v3, /device:TPU:0, one launch (start us, length us, event | category | flops | bytes accessed | tf_op | source)
XLA Modules:
  0.0 757.3 jit_solution(11968424710323952150)
XLA Ops:
  0.7 1.0 fusion.159
  1.7 1.0 fusion.160
  2.7 1.4 convert_reduce_fusion.1
  4.2 1.6 fusion.16
  5.8 1.5 fusion.10.refs_3_
  7.3 127.8 %gather_weights.1 = (bf16[1,4,2,2,64,4096]{5,4,3,2,1,0:T(8,128)(2,1)}, bf16[1,4,2,2,64,4096]{5,4,3,2,1,0:T(8,128)(2,1)}, bf16[3,4,2,2,64,1024]{5,4,3,2,1,0:T(8,128)(2,1)}, bf16[1,4,2,2,64,1024]{5,4,3,2,1,0:T(8,128)(2,1)}) custom-call(bf16[1,64,2048]{2,1,0:T(8,128)(2,1)} %bitcast.196, bf16[1,64,2048]{2,1,0:T(8,128)(2,1)} %bitcast.197, ...), custom_call_target="tpu_custom_call" | custom-call | tf_op jit(solution)/shard_map/gather_weights/pallas_call | solution.py:807
  135.1 12.2 %multiply_convert_fusion.3 = (bf16[512,4096]{1,0:T(8,128)(2,1)S(1)}, f32[512,4096]{1,0:T(8,128)}) fusion(bf16[512,1024]{1,0:T(8,128)(2,1)} %fusion.10.refs_3_, bf16[1024,4096]{1,0:T(8,128)(2,1)} %bitcast.342), kind=kOutput, calls=%fused_computation.63 | convolution fusion | flops 4305453056 | bytes 22020096 | tf_op jit(solution)/shard_map/dot_general | solution.py:34
  147.4 9.9 %fusion.153 = (f32[512]{0:T(512)S(1)}, f32[512,1024]{1,0:T(8,128)S(1)}, f32[]{:T(128)}) fusion(bf16[512,1024]{1,0:T(8,128)(2,1)S(1)} %copy-done.8, bf16[512,4096]{1,0:T(8,128)(2,1)S(1)} %get-tuple-element.220.refs_8_, bf16[1024,4096]{1,0:T(8,128)(2,1)} %bitcast.346), kind=kOutput, calls=%fused_computation.364 | convolution fusion | flops 4298112512 | bytes 15730692 | tf_op jit(solution)/shard_map/dot_general | solution.py:26
  157.7 0.8 fusion.154
  159.6 2.3 convolution_convert_fusion.1.refs_1_
  161.8 2.2 convolution_convert_fusion.2.refs_0_
  164.1 2.3 convolution_convert_fusion.3.refs_0_
  166.5 1.3 gather_fusion
  169.4 5.9 exchange_rows.1
  176.0 121.8 %attn_fwd.1 = (bf16[512,1024]{1,0:T(8,128)(2,1)}, f32[8,1024,1]{2,1,0:T(8,128)}, bf16[2,4,2,2,64,1024]{5,4,3,2,1,0:T(8,128)(2,1)}, bf16[1,4,2,2,64,1024]{5,4,3,2...) custom-call(bf16[512,1024]{1,0:T(8,128)(2,1)} %convolution_convert_fusion.3.refs_0_, ...), custom_call_target="tpu_custom_call" | custom-call | tf_op jit(solution)/shard_map/attn_fwd/pallas_call | solution.py:143
  297.8 2.9 fusion.155
  301.6 2.0 fusion.152
  304.4 1.5 add_divide_fusion.3
  306.0 2.6 fusion.161
  308.6 1.5 collective-permute-start
  311.0 9.3 %fusion.151 = (f32[512]{0:T(512)S(1)}, f32[512,1024]{1,0:T(8,128)S(1)}) fusion(f32[512,1024]{1,0:T(8,128)S(1)} %get-tuple-element.222, f32[1024]{0:T(1024)S(1)} %bitcast.286, f32[32,1024]{1,0:T(8,128)S(1)} %collective-permute-done, f32[1024]{0:T(1024)S(1)} %bitcast.288, f32[1024]{0:T(1024)S(1)} %bitcast.230, f32[1024]{0:T(1024)S(1)} %bitcast.232, ...), kind=kLoop, calls=%fused_computation.362 | loop fusion | flops 48233984 | bytes 4454400 | tf_op jit(solution)/shard_map/reduce_sum | solution.py:905
  322.3 2.0 fusion.150
  325.2 7.6 %multiply_convert_fusion.2 = (bf16[512,4096]{1,0:T(8,128)(2,1)S(1)}, f32[512,4096]{1,0:T(8,128)}) fusion(bf16[512,1024]{1,0:T(8,128)(2,1)S(1)} %add_convert_fusion.1.refs_9_, bf16[1024,4096]{1,0:T(8,128)(2,1)S(1)} %bitcast.351), kind=kOutput, calls=%fused_computation.61 | convolution fusion | flops 4305453056 | bytes 22020096 | tf_op jit(solution)/shard_map/dot_general | solution.py:34
  332.8 1.9 copy-done.31
  334.8 7.8 %fusion.149 = (f32[512]{0:T(512)S(1)}, f32[512,1024]{1,0:T(8,128)S(1)}, f32[]{:T(128)}) fusion(f32[512,1024]{1,0:T(8,128)S(1)} %get-tuple-element.158, bf16[512,4096]{1,0:T(8,128)(2,1)S(1)} %get-tuple-element.224.refs_12_, bf16[1024,4096]{1,0:T(8,128)(2,1)} %bitcast.352), kind=kOutput, calls=%fused_computation.360 | convolution fusion | flops 4297588224 | bytes 16779268 | tf_op jit(solution)/shard_map/dot_general | solution.py:26
  342.9 0.9 copy-done.13
  343.8 1.8 fusion.20
  346.3 1.0 copy-done.21
  347.3 10.4 %multiply_convert_fusion.1.refs_13_ = bf16[512,4096]{1,0:T(8,128)(2,1)S(1)} fusion(f32[512,4096]{1,0:T(8,128)} %get-tuple-element.225, bf16[512,1024]{1,0:T(8,128)(2,1)S(1)} %multiply_convert_fusion.7.refs_8_, bf16[1024,4096]{1,0:T(8,128)(2,1)} %bitcast.353), kind=kOutput, calls=%fused_computation.60 | convolution fusion | flops 4313841664 | bytes 22020096 | tf_op jit(solution)/shard_map/dot_general | solution.py:34
  357.7 9.0 %multiply_reduce_fusion.36 = (f32[1024]{0:T(1024)S(1)}, f32[512]{0:T(512)S(1)}, f32[512]{0:T(512)S(1)}, f32[1024]{0:T(1024)S(1)}, f32[512,1024]{1,0:T(8,128)S(1)}) fusion(f32[512,1024]{1,0:T(8,128)S(1)} %get-tuple-element.158, f32[512]{0:T(512)S(1)} %add_rsqrt_fusion.1, f32[512]{0:T(512)S(1)} %broadcast_multiply_fusion.13, f32[1024]{0:T(1024)S(1)} %bitcast.226, ...), kind=kOutput, calls=%fused_computation.265 | convolution fusion | flops 4299682816 | bytes 16797696 | tf_op jit(solution)/shard_map/dot_general | solution.py:26
  366.8 2.8 fusion.148
  369.6 2.4 multiply_reduce_fusion.37
  372.0 3.7 multiply_reduce_fusion.6
  375.7 1.3 collective-permute-start.1
  377.0 2.5 multiply_reduce_fusion.15
  379.5 2.5 multiply_reduce_fusion.24
  382.0 1.1 multiply_reduce_fusion.33
  383.1 3.3 stack.216
  386.4 11.2 %multiply_convert_fusion.6 = (bf16[512,1024]{1,0:T(8,128)(2,1)S(1)}, f32[512,1024]{1,0:T(8,128)S(1)}) fusion(f32[512,1024]{1,0:T(8,128)} %copy-done.3, f32[512,1024]{1,0:T(8,128)S(1)} %get-tuple-element.146, f32[1024]{0:T(1024)S(1)} %bitcast.287, f32[32,1024]{1,0:T(8,128)S(1)} %collective-permute-done.1, f32[1024]{0:T(1024)S(1)} %bitcast.289, ...), kind=kLoop, calls=%fused_computation.276 | loop fusion | flops 48758784 | bytes 7598080 | tf_op jit(solution)/shard_map/convert_element_type | solution.py:921
  397.6 0.8 multiply_convert_fusion.5.refs_16_
  398.4 1.1 copy-done.40
  399.6 1.3 fusion.162
  402.2 2.0 multiply_reduce_fusion.38
  404.2 2.1 fusion.146
  406.3 2.3 convolution_convert_fusion.refs_3_
  408.6 147.3 %attn_bwd.1 = (bf16[512,1024]{1,0:T(8,128)(2,1)}, bf16[1024,1024]{1,0:T(8,128)(2,1)}, bf16[1024,1024]{1,0:T(8,128)(2,1)}, f32[512,128]{1,0:T(8,128)}, f32[64,204...) custom-call(bf16[512,1024]{1,0:T(8,128)(2,1)} %convolution_convert_fusion.3.ref, ...), custom_call_target="tpu_custom_call" | custom-call | tf_op jit(solution)/shard_map/attn_bwd/pallas_call | solution.py:262
  555.9 8.4 %return_rows.1 = (bf16[512,1024]{1,0:T(8,128)(2,1)}, bf16[512,1024]{1,0:T(8,128)(2,1)}) custom-call(bf16[1024,1024]{1,0:T(8,128)(2,1)} %get-tuple-element.58.refs_0_, bf16[1024,1024]{1,0:T(8,128)(2,1)} %get-tuple-element.59.refs_1_), custom_call_target="tpu_custom_call" | custom-call | tf_op jit(solution)/shard_map/return_rows/pallas_call | solution.py:892
  564.3 2.7 fusion.163
  567.0 1.3 fusion.164
  569.5 2.1 multiply_reduce_fusion.39
  571.6 2.1 multiply_convert_fusion.4
  573.7 1.1 copy-done.24
  574.8 10.6 %multiply_convert_fusion.refs_9_ = bf16[512,4096]{1,0:T(8,128)(2,1)S(1)} fusion(f32[512,4096]{1,0:T(8,128)} %get-tuple-element.221, bf16[512,1024]{1,0:T(8,128)(2,1)S(1)} %get-tuple-element.147.refs_2_, bf16[1024,4096]{1,0:T(8,128)(2,1)} %bitcast.347), kind=kOutput, calls=%fused_computation.59 | convolution fusion | flops 4313841664 | bytes 22020096 | tf_op jit(solution)/shard_map/dot_general | solution.py:34
  585.4 6.3 fusion.15
  593.2 146.5 %scatter_grads.1 = (f32[64,512]{1,0:T(8,128)}, f32[64,512]{1,0:T(8,128)}, f32[64,512]{1,0:T(8,128)}, f32[64,512]{1,0:T(8,128)}, f32[64,2048]{1,0:T(8,128)}, /*index=5*/f32[64,2048]{1,0:T(8,128)}, f32[56,1024]{1,0:T(8,128)}) custom-call(bf16[512,1024]{1,0:T(8,128)(2,1)} %copy-done.23, bf16[512,1024]{1,0:T(8,128)(2,1)} %copy-done.26, ...), custom_call_target="tpu_custom_call" | custom-call | tf_op jit(solution)/shard_map/scatter_grads/pallas_call | solution.py:807
  739.8 1.7 slice.551
  742.2 1.5 fusion.156
  743.7 1.2 sqrt_bitcast_fusion
  746.4 1.8 pad_maximum_fusion.2
  748.2 4.3 fusion.14
  752.5 0.8 copy.43
  753.3 0.8 copy.44
  755.4 0.8 copy.47
  756.2 0.8 copy.48
  (196 shorter events, 17.3 us)
Async XLA Ops:
  0.6 5.2 copy-start.7
  1.7 5.6 copy-start.52
  4.2 3.1 copy-start.54
  135.1 12.3 %copy-start.8 = (bf16[512,1024]{1,0:T(8,128)(2,1)S(1)}, bf16[512,1024]{1,0:T(8,128)(2,1)}, u32[]{:S(2)}) copy-start(bf16[512,1024]{1,0:T(8,128)(2,1)} %param.15) | copy-start | bytes 3145732
  147.4 9.9 %copy-start.30 = (bf16[512,4096]{1,0:T(8,128)(2,1)}, bf16[512,4096]{1,0:T(8,128)(2,1)S(1)}, u32[]{:S(2)}) copy-start(bf16[512,4096]{1,0:T(8,128)(2,1)S(1)} %get-tuple-element.220.refs_8_) | copy-start | bytes 12582916
  147.4 10.3 %slice-start = ((s8[6291456]{0:T(1024)(128)(4,1)}), s8[4194304]{0:T(1024)(128)(4,1)S(1)}, s32[]{:S(2)}) async-start(s8[6291456]{0:T(1024)(128)(4,1)} %bitcast.186), calls=%async_computation | async-start | bytes 8388608
  147.4 10.3 %slice-start.1 = ((s8[6291456]{0:T(1024)(128)(4,1)}), s8[2097152]{0:T(1024)(128)(4,1)S(1)}, s32[]{:S(2)}) async-start(s8[6291456]{0:T(1024)(128)(4,1)} %bitcast.186), calls=%async_computation.1 | async-start | bytes 4194304
  157.3 1.9 copy-start
  158.5 3.3 copy-start.35
  158.5 3.3 copy-start.37
  158.5 5.5 copy-start.18
  159.6 4.5 copy-start.26
  164.1 2.3 copy-start.58
  297.8 3.0 copy-start.1
  297.8 3.1 copy-start.20
  297.8 3.8 copy-start.60
  300.7 3.7 copy-start.39
  300.7 5.2 copy-start.15
  303.6 17.9 %copy-start.5 = (f32[512,1024]{1,0:T(8,128)}, f32[512,1024]{1,0:T(8,128)S(1)}, u32[]{:S(2)}) copy-start(f32[512,1024]{1,0:T(8,128)S(1)} %get-tuple-element.162) | copy-start | bytes 6291460
  305.9 2.6 copy-start.3
  306.0 4.1 copy-start.51
  308.6 2.4 collective-permute-start
  320.7 1.6 copy-start.62
  320.7 4.4 slice-start.4
  321.5 2.8 copy-start.27
  322.3 3.0 slice-start.5
  325.1 7.7 %copy-start.28 = (bf16[512,1024]{1,0:T(8,128)(2,1)}, bf16[512,1024]{1,0:T(8,128)(2,1)S(1)}, u32[]{:S(2)}) copy-start(bf16[512,1024]{1,0:T(8,128)(2,1)S(1)} %add_convert_fusion.1.refs_9_) | copy-start | bytes 3145732
  332.8 1.9 copy-start.31
  357.7 9.1 %copy-start.32 = (bf16[512,4096]{1,0:T(8,128)(2,1)}, bf16[512,4096]{1,0:T(8,128)(2,1)S(1)}, u32[]{:S(2)}) copy-start(bf16[512,4096]{1,0:T(8,128)(2,1)S(1)} %multiply_convert_fusion.1.refs_13_) | copy-start | bytes 12582916
  369.6 2.4 copy-start.22
  375.7 10.7 %collective-permute-start.1 = (f32[32,1024]{1,0:T(8,128)S(1)}, f32[32,1024]{1,0:T(8,128)S(1)}, u32[]{:S(2)}, u32[]{:S(2)}) collective-permute-start(f32[32,1024]{1,0:T(8,128)S(1)} %slice.616), channel_id=1, source_target_pairs={{1,0},{3,2},{5,4},{7,6},{9,8},{11,10},{13,12},{15,14},{17,16},{19,... | collective-permute-start | bytes 393224 | tf_op jit(solution)/shard_map/ppermute | solution.py:1003
  386.4 11.2 %copy-start.4 = (f32[512,1024]{1,0:T(8,128)S(1)}, f32[512,1024]{1,0:T(8,128)}, u32[]{:S(2)}) copy-start(f32[512,1024]{1,0:T(8,128)} %copy-done.3) | copy-start | bytes 6291460
  386.4 11.2 %copy-start.11 = (f32[512,1024]{1,0:T(8,128)S(1)}, f32[512,1024]{1,0:T(8,128)}, u32[]{:S(2)}) copy-start(f32[512,1024]{1,0:T(8,128)} %get-tuple-element.223) | copy-start | bytes 6291460
  397.6 3.3 copy-start.29
  397.6 2.0 copy-start.40
  399.6 2.0 copy-start.6
  399.6 2.6 copy-start.16
  402.2 2.0 copy-start.17
  404.2 2.1 copy-start.61
  406.3 2.3 copy-start.23
  555.9 8.4 %copy-start.38 = (bf16[1,4,2,2,64,1024]{5,4,3,2,1,0:T(8,128)(2,1)S(1)}, bf16[1,4,2,2,64,1024]{5,4,3,2,1,0:T(8,128)(2,1)}, u32[]{:S(2)}) copy-start(bf16[1,4,2,2,64,1024]{5,4,3,2,1,0:T(8,128)(2,1)} %copy-done.37) | copy-start | bytes 6291460
  564.3 2.7 copy-start.36
  564.3 2.7 copy-start.41
  567.0 2.2 copy-start.19
  567.0 2.5 copy-start.34
  569.5 2.1 copy-start.14
  571.6 13.8 %slice-start.2 = ((s8[8388608]{0:T(1024)(128)(4,1)}), s8[4194304]{0:T(1024)(128)(4,1)S(1)}, s32[]{:S(2)}) async-start(s8[8388608]{0:T(1024)(128)(4,1)} %bitcast.343), calls=%async_computation.2 | async-start | bytes 8388608
  574.8 10.6 %copy-start.9 = (bf16[512,1024]{1,0:T(8,128)(2,1)S(1)}, bf16[512,1024]{1,0:T(8,128)(2,1)}, u32[]{:S(2)}) copy-start(bf16[512,1024]{1,0:T(8,128)(2,1)} %param.15) | copy-start | bytes 3145732
  574.8 10.6 %copy-start.53 = (f32[1,1024]{1,0:T(1,128)S(1)}, f32[1,1024]{1,0:T(1,128)}, u32[]{:S(2)}) copy-start(f32[1,1024]{1,0:T(1,128)} %copy-done.52) | copy-start | bytes 12292
  574.8 10.6 %copy-start.55 = (f32[512]{0:T(512)S(1)}, f32[512]{0:T(512)}, u32[]{:S(2)}) copy-start(f32[512]{0:T(512)} %copy-done.54) | copy-start | bytes 6148
  574.8 10.6 %copy-start.57 = (f32[512]{0:T(512)S(1)}, f32[512]{0:T(512)}, u32[]{:S(2)}) copy-start(f32[512]{0:T(512)} %copy-done.56) | copy-start | bytes 6148
  574.8 10.6 %slice-start.3 = ((s8[8388608]{0:T(1024)(128)(4,1)}), s8[4194304]{0:T(1024)(128)(4,1)S(1)}, s32[]{:S(2)}) async-start(s8[8388608]{0:T(1024)(128)(4,1)} %bitcast.343), calls=%async_computation.3 | async-start | bytes 8388608
  585.4 6.3 copy-start.33
  585.4 6.3 copy-start.46
  585.4 6.3 copy-start.59
  593.2 152.4 %copy-start.49 = (f32[64,512]{1,0:T(8,128)S(1)}, f32[64,512]{1,0:T(8,128)}, u32[]{:S(2)}) copy-start(f32[64,512]{1,0:T(8,128)} %get-tuple-element.70) | copy-start | bytes 393220
  593.2 152.4 %copy-start.50 = (f32[64,512]{1,0:T(8,128)S(1)}, f32[64,512]{1,0:T(8,128)}, u32[]{:S(2)}) copy-start(f32[64,512]{1,0:T(8,128)} %get-tuple-element.71) | copy-start | bytes 393220
  739.8 8.4 %copy-start.10 = (bf16[512,1024]{1,0:T(8,128)(2,1)S(1)}, bf16[512,1024]{1,0:T(8,128)(2,1)}, u32[]{:S(2)}) copy-start(bf16[512,1024]{1,0:T(8,128)(2,1)} %param.15) | copy-start | bytes 3145732
  748.2 4.3 copy-start.45
  748.2 5.1 copy-start.44
  752.5 1.6 copy-start.48
  752.5 2.3 copy-start.47
  752.5 2.9 copy-start.43
  752.5 3.7 copy-start.42
  (7 other events, 9.2 us)

commit v4 on v3

--- a/solution.py
+++ b/solution.py
@@ -472,6 +472,9 @@
             Gather(place, p, orders, shards[p.source], wholes[p.source], send.at[i], recv.at[i], local.at[i])
             for i, (p, orders) in enumerate(zip(self.pieces, self.orders))
         ]
+        return self.steps_of(place, gathers)
+
+    def steps_of(self, place, gathers, read=()):
         count, depth = len(gathers), self.depth
 
         def begin():
@@ -498,13 +501,112 @@
                 gathers[at].start(4)
 
         def end():
-            for g in gathers:
-                g.arrived(3)
-                g.arrived(4)
+            for i, g in enumerate(gathers):
+                if i not in read:
+                    g.arrived(3)
+                    g.arrived(4)
                 for stage in range(5):
                     g.sent(stage)
 
         return [begin] + [functools.partial(step, i) for i in range(count + 2 * depth)] + [end]
+
+
+class FeedPlan(GatherPlan):
+    TILE = 512
+
+    def __init__(self, shards, entered, dims, n_tensor):
+        super().__init__(shards, dims, n_tensor)
+        tokens, width = entered.shape
+        cols = shards[0].shape[2]
+        hidden = cols * n_tensor
+        fed = sorted((p for p in self.pieces if p.source < 2), key=lambda p: (p.first, p.source))
+        self.pieces = fed + [p for p in self.pieces if p.source >= 2]
+        self.pairs = len(fed) // 2
+        self.tile = tile = min(self.TILE, fed[0].width)
+        self.args = self.args + [entered]
+        self.in_specs = self.in_specs + [VMEM]
+        self.out_specs = self.out_specs + [ANY, ANY, VMEM]
+        self.out_shape = self.out_shape + [
+            jax.ShapeDtypeStruct((tokens, hidden), jnp.float32),
+            jax.ShapeDtypeStruct((tokens, hidden), jnp.bfloat16),
+            jax.ShapeDtypeStruct((tokens, width), jnp.float32),
+        ]
+        rows = shards[0].shape[1]
+        self.scratch = self.scratch + [
+            pltpu.VMEM((2, 2, *dims, rows, tile), jnp.bfloat16),
+            pltpu.VMEM((2, tokens, tile), jnp.float32),
+            pltpu.VMEM((2, tokens, tile), jnp.bfloat16),
+            pltpu.SemaphoreType.DMA((2, 2)),
+            pltpu.SemaphoreType.DMA((2, 2)),
+        ]
+
+    def results(self, outs):
+        return super().results(outs[:-3]) + list(outs[-3:])
+
+    def steps(self, ins, outs, scratch):
+        send, recv, local, weights, pre_st, act_st, load_sem, store_sem = scratch
+        place = Place(self.dims, self.n_tensor)
+        shards, entered = ins[:-1], ins[-1]
+        wholes, (before, active, branch) = outs[:-3], outs[-3:]
+        gathers = [
+            Gather(place, p, orders, shards[p.source], wholes[p.source], send.at[i], recv.at[i], local.at[i])
+            for i, (p, orders) in enumerate(zip(self.pieces, self.orders))
+        ]
+        steps = self.steps_of(place, gathers, range(2 * self.pairs))
+        tile, tokens, width = self.tile, entered.shape[0], entered.shape[1]
+        tiles = [
+            (pair, t * shards[0].shape[2] + self.pieces[2 * pair].first + sub * tile)
+            for pair in range(self.pairs)
+            for t in range(self.n_tensor)
+            for sub in range(self.pieces[2 * pair].width // tile)
+        ]
+
+        def loads(number):
+            cols = pl.ds(tiles[number][1], tile)
+            for k in (0, 1):
+                origin = wholes[k].at[0, :, :, :, :, cols]
+                yield pltpu.make_async_copy(origin, weights.at[number % 2, k], load_sem.at[number % 2, k])
+
+        def stores(number):
+            cols, slot = pl.ds(tiles[number][1], tile), number % 2
+            yield pltpu.make_async_copy(pre_st.at[slot], before.at[:, cols], store_sem.at[slot, 0])
+            yield pltpu.make_async_copy(act_st.at[slot], active.at[:, cols], store_sem.at[slot, 1])
+
+        def feed(number):
+            slot, pair = number % 2, tiles[number][0]
+            if number == 0 or tiles[number - 1][0] != pair:
+                for g in gathers[2 * pair : 2 * pair + 2]:
+                    g.arrived(3)
+                    g.arrived(4)
+                run_all(loads(number), "start")
+            run_all(loads(number), "wait")
+            if number + 1 < len(tiles) and tiles[number + 1][0] == pair:
+                run_all(loads(number + 1), "start")
+            if number >= 2:
+                run_all(stores(number - 2), "wait")
+            up = weights[slot, 0].reshape(width, tile)
+            pre = dot_nn(entered[...], up)
+            pre_st[slot] = pre
+            act = low(jax.nn.silu(pre))
+            act_st[slot] = act
+            run_all(stores(number), "start")
+            added = dot_nt(act, weights[slot, 1].reshape(width, tile))
+            branch[...] = added if number == 0 else branch[...] + added
+            if number == len(tiles) - 1:
+                for last in range(max(number - 1, 0), number + 1):
+                    run_all(stores(last), "wait")
+
+        first = [2 * pair + 2 + 2 * self.depth + 1 for pair in range(self.pairs)]
+        out, at = [], 0
+        for number, step in enumerate(steps[:-1]):
+            out.append(step)
+            rest = len(steps) - 2 - number
+            room = -(-(len(tiles) - at) // max(rest + 1, 1)) if number > first[0] else 0
+            while room and at < len(tiles) and number > first[tiles[at][0]]:
+                out.append(functools.partial(feed, at))
+                at, room = at + 1, room - 1
+        out += [functools.partial(feed, k) for k in range(at, len(tiles))]
+        return out + steps[-1:]
 
 
 class Scatter:
@@ -986,9 +1088,6 @@
     keys = rows * n_tensor
     early = [first_up[None], first_down.T[None], attn_proj, attn_out.T[None]]
     late = [glu_weight, conv_out.T[None], second_up[None], second_down.T[None]]
-    gathered = run_plan(GatherPlan(early, dims, n_tensor), 0, "gather_weights")
-    (up_one,), (down_one,), proj, (out_attn,) = gathered
-
     def enter(stream, row):
         result, normed, inv_std = norm_forward(stream, norm_gains[row], norm_shifts[row])
         return low(result), (normed, inv_std)
@@ -1003,10 +1102,11 @@
         return lax.ppermute(value, "tensor", pairs)
 
     stream = stream_in.astype(jnp.float32)
+    entered_a, norm_a = enter(stream, 0)
+    gathered = run_plan(FeedPlan(early, entered_a, dims, n_tensor), 0, "gather_weights")
+    (up_one,), (down_one,), proj, (out_attn,), before_a, active_a, branch = gathered
     squares = []
-
-    entered_a, norm_a = enter(stream, 0)
-    branch, ffn_a = ffn_forward(entered_a, up_one, down_one)
+    ffn_a = (before_a, active_a)
     squares.append(jnp.sum(branch * branch))
     stream = stream + 0.5 * branch
 

time: 763 us -> 757 us (level)
  matrix products: 103 us -> 82.8 us
    dot_general x11 -> x10, matrix products: 56.3 us -> 44.9 us  [dot_nn(): return jnp.dot(a, b, preferred_element_type=jnp.float32)]
    dot_general x11 -> x10, matrix products: 46.4 us -> 37.6 us  [dot_nt(): return lax.dot_general(a, b, NT, preferred_element_type=jnp.float32)]
    unnamed x146 -> x136, local copies, waits for them, and re-layouts: 16.3 us -> 15.2 us
where the time goes in v4:
time: 757 us; the launch traced here: 747 us
  Pallas kernels  563 us (74%)
  matrix products  82.8 us (11%)
  other arithmetic  63.9 us (8%)
  local copies, waits for them, and re-layouts  31.3 us (4%)
    pallas_call x2, Pallas kernels, run_plan(): pl.pallas_call(functools.partial(plan_kernel, plan), out_shape=plan.out_s...  275 us
    pallas_call x1, Pallas kernels, attn_bwd(): pl.pallas_call(functools.partial(attn_bwd_kernel, plan), grid=(pairs,), i...  146 us
    pallas_call x1, Pallas kernels, attn_fwd(): pl.pallas_call(functools.partial(attn_fwd_kernel, plan), grid=(pairs,), i...  127 us
    dot_general x10, matrix products, dot_nn(): return jnp.dot(a, b, preferred_element_type=jnp.float32)  44.9 us
    dot_general x10, matrix products, dot_nt(): return lax.dot_general(a, b, NT, preferred_element_type=jnp.float32)  37.6 us
    convert_element_type x11, other arithmetic, low(): return value.astype(jnp.bfloat16)  25.6 us
    unnamed x136, local copies, waits for them, and re-layouts  15.2 us
  transfers between devices with their start and end apart: 2, of which 1 were waited for; matrix products, arithmetic and copies ran while one was open for 1% of the time, Pallas kernels for 0%

profile of v4, /device:TPU:0, one launch (start us, length us, event | category | flops | bytes accessed | tf_op | source)
XLA Modules:
  0.0 747.4 jit_solution(53754578646694207)
XLA Ops:
  0.7 1.0 fusion.159
  1.7 1.0 fusion.160
  2.7 1.4 convert_reduce_fusion.1
  4.2 1.6 fusion.16
  5.9 1.5 fusion.10.refs_4_.refs_3_
  7.3 129.9 %gather_weights.1 = (bf16[1,4,2,2,64,4096]{5,4,3,2,1,0:T(8,128)(2,1)}, bf16[1,4,2,2,64,4096]{5,4,3,2,1,0:T(8,128)(2,1)}, bf16[3,4,2,2,64,1024]{5,4,3,2,1,0:T(8,1...) custom-call(bf16[1,64,2048]{2,1,0:T(8,128)(2,1)} %bitcast.190, ...), custom_call_target="tpu_custom_call" | custom-call | tf_op jit(solution)/shard_map/gather_weights/pallas_call | solution.py:909
  137.2 3.3 fusion.153
  140.9 1.2 fusion.154
  143.2 2.3 convolution_convert_fusion.1.refs_1_
  145.5 2.6 convolution_convert_fusion.2.refs_0_
  148.1 2.3 convolution_convert_fusion.3.refs_0_
  150.5 1.3 gather_fusion
  153.4 5.9 exchange_rows.1
  159.9 127.0 %attn_fwd.1 = (bf16[512,1024]{1,0:T(8,128)(2,1)}, f32[8,1024,1]{2,1,0:T(8,128)}, bf16[2,4,2,2,64,1024]{5,4,3,2,1,0:T(8,128)(2,1)}, bf16[1,4,2,2,64,1024]{5,4,3,2...) custom-call(bf16[512,1024]{1,0:T(8,128)(2,1)} %convolution_convert_fusion.3.refs_0_, ...), custom_call_target="tpu_custom_call" | custom-call | tf_op jit(solution)/shard_map/attn_fwd/pallas_call | solution.py:143
  287.0 2.9 fusion.155
  290.8 2.0 fusion.152
  293.6 1.5 add_divide_fusion.2
  295.2 2.6 fusion.161
  297.8 1.7 collective-permute-start
  299.6 0.8 collective-permute-done
  300.4 9.0 %fusion.151 = (f32[512]{0:T(512)S(1)}, f32[512,1024]{1,0:T(8,128)S(1)}) fusion(f32[512,1024]{1,0:T(8,128)S(1)} %get-tuple-element.226, f32[1024]{0:T(1024)S(1)} %bitcast.280, f32[32,1024]{1,0:T(8,128)S(1)} %collective-permute-done, f32[1024]{0:T(1024)S(1)} %bitcast.282, f32[1024]{0:T(1024)S(1)} %bitcast.224, f32[1024]{0:T(1024)S(1)} %bitcast.226, ...), kind=kLoop, calls=%fused_computation.360 | loop fusion | flops 48233984 | bytes 4454400 | tf_op jit(solution)/shard_map/reduce_sum | solution.py:1007
  309.8 0.8 multiply_convert_fusion.7.refs_14_
  311.4 2.0 fusion.150
  314.4 7.6 %multiply_convert_fusion.2 = (bf16[512,4096]{1,0:T(8,128)(2,1)S(1)}, f32[512,4096]{1,0:T(8,128)}) fusion(bf16[512,1024]{1,0:T(8,128)(2,1)S(1)} %add_convert_fusion.1.refs_9_, bf16[1024,4096]{1,0:T(8,128)(2,1)S(1)} %bitcast.343), kind=kOutput, calls=%fused_computation.61 | convolution fusion | flops 4305453056 | bytes 22020096 | tf_op jit(solution)/shard_map/dot_general | solution.py:34
  322.0 1.9 copy-done.29
  323.9 7.8 %fusion.149 = (f32[512]{0:T(512)S(1)}, f32[512,1024]{1,0:T(8,128)S(1)}, f32[]{:T(128)}) fusion(f32[512,1024]{1,0:T(8,128)S(1)} %get-tuple-element.164, bf16[512,4096]{1,0:T(8,128)(2,1)S(1)} %get-tuple-element.228.refs_12_, bf16[1024,4096]{1,0:T(8,128)(2,1)} %bitcast.344), kind=kOutput, calls=%fused_computation.358 | convolution fusion | flops 4297588224 | bytes 16779268 | tf_op jit(solution)/shard_map/dot_general | solution.py:26
  332.1 0.9 copy-done.12
  332.9 1.8 fusion.20
  335.5 1.0 copy-done.20
  336.4 10.6 %multiply_convert_fusion.1.refs_13_ = bf16[512,4096]{1,0:T(8,128)(2,1)S(1)} fusion(f32[512,4096]{1,0:T(8,128)} %get-tuple-element.229, bf16[512,1024]{1,0:T(8,128)(2,1)S(1)} %multiply_convert_fusion.6.refs_8_, bf16[1024,4096]{1,0:T(8,128)(2,1)} %bitcast.345), kind=kOutput, calls=%fused_computation.60 | convolution fusion | flops 4313841664 | bytes 22020096 | tf_op jit(solution)/shard_map/dot_general | solution.py:34
  347.1 9.1 %multiply_reduce_fusion.36 = (f32[1024]{0:T(1024)S(1)}, f32[512]{0:T(512)S(1)}, f32[512]{0:T(512)S(1)}, f32[1024]{0:T(1024)S(1)}, f32[512,1024]{1,0:T(8,128)S(1)}) fusion(f32[512,1024]{1,0:T(8,128)S(1)} %get-tuple-element.164, f32[512]{0:T(512)S(1)} %add_rsqrt_fusion.1, f32[512]{0:T(512)S(1)} %broadcast_multiply_fusion.13, f32[1024]{0:T(1024)S(1)} %bitcast.220, ...), kind=kOutput, calls=%fused_computation.263 | convolution fusion | flops 4299682816 | bytes 16797696 | tf_op jit(solution)/shard_map/dot_general | solution.py:26
  356.1 2.8 fusion.148
  359.0 2.4 multiply_reduce_fusion.37
  361.4 3.7 multiply_reduce_fusion.6
  365.1 1.3 collective-permute-start.1
  366.4 2.5 multiply_reduce_fusion.15
  368.9 2.5 multiply_reduce_fusion.24
  371.4 1.1 multiply_reduce_fusion.33
  372.4 3.3 stack.216
  375.8 11.2 %multiply_convert_fusion.5 = (bf16[512,1024]{1,0:T(8,128)(2,1)S(1)}, f32[512,1024]{1,0:T(8,128)S(1)}) fusion(f32[512,1024]{1,0:T(8,128)} %copy-done.6, f32[512,1024]{1,0:T(8,128)S(1)} %get-tuple-element.152, f32[1024]{0:T(1024)S(1)} %bitcast.281, f32[32,1024]{1,0:T(8,128)S(1)} %collective-permute-done.1, f32[1024]{0:T(1024)S(1)} %bitcast.283, ...), kind=kLoop, calls=%fused_computation.274 | loop fusion | flops 48758784 | bytes 7598080 | tf_op jit(solution)/shard_map/convert_element_type | solution.py:1023
  387.0 0.8 multiply_convert_fusion.4.refs_16_
  387.8 1.1 copy-done.38
  388.9 1.3 fusion.162
  391.5 2.0 multiply_reduce_fusion.38
  393.5 2.1 fusion.146
  395.7 2.3 convolution_convert_fusion.refs_3_
  398.0 146.4 %attn_bwd.1 = (bf16[512,1024]{1,0:T(8,128)(2,1)}, bf16[1024,1024]{1,0:T(8,128)(2,1)}, bf16[1024,1024]{1,0:T(8,128)(2,1)}, f32[512,128]{1,0:T(8,128)}, f32[64,204...) custom-call(bf16[512,1024]{1,0:T(8,128)(2,1)} %convolution_convert_fusion.3.ref, ...), custom_call_target="tpu_custom_call" | custom-call | tf_op jit(solution)/shard_map/attn_bwd/pallas_call | solution.py:262
  544.4 8.3 %return_rows.1 = (bf16[512,1024]{1,0:T(8,128)(2,1)}, bf16[512,1024]{1,0:T(8,128)(2,1)}) custom-call(bf16[1024,1024]{1,0:T(8,128)(2,1)} %get-tuple-element.60.refs_0_, bf16[1024,1024]{1,0:T(8,128)(2,1)} %get-tuple-element.61.refs_1_), custom_call_target="tpu_custom_call" | custom-call | tf_op jit(solution)/shard_map/return_rows/pallas_call | solution.py:994
  552.8 2.7 fusion.163
  555.5 1.3 fusion.164
  557.9 3.1 multiply_reduce_fusion.39
  561.5 4.5 multiply_convert_fusion.3
  566.0 10.8 %multiply_convert_fusion.refs_9_ = bf16[512,4096]{1,0:T(8,128)(2,1)S(1)} fusion(f32[512,4096]{1,0:T(8,128)} %get-tuple-element.65, bf16[512,1024]{1,0:T(8,128)(2,1)S(1)} %get-tuple-element.153.refs_2_, bf16[1024,4096]{1,0:T(8,128)(2,1)} %bitcast.339), kind=kOutput, calls=%fused_computation.59 | convolution fusion | flops 4313841664 | bytes 22020096 | tf_op jit(solution)/shard_map/dot_general | solution.py:34
  576.9 6.3 fusion.15
  584.3 145.6 %scatter_grads.1 = (f32[64,512]{1,0:T(8,128)}, f32[64,512]{1,0:T(8,128)}, f32[64,512]{1,0:T(8,128)}, f32[64,512]{1,0:T(8,128)}, f32[64,2048]{1,0:T(8,128)}, /*index=5*/f32[64,2048]{1,0:T(8,128)}, f32[56,1024]{1,0:T(8,128)}) custom-call(bf16[512,1024]{1,0:T(8,128)(2,1)} %copy-done.22, bf16[512,1024]{1,0:T(8,128)(2,1)} %copy-done.25, ...), custom_call_target="tpu_custom_call" | custom-call | tf_op jit(solution)/shard_map/scatter_grads/pallas_call | solution.py:909
  729.9 1.7 slice.551
  732.3 1.5 fusion.156
  733.8 1.2 sqrt_bitcast_fusion
  736.5 1.8 pad_maximum_fusion.2
  738.3 4.3 fusion.14
  742.6 0.8 copy.43
  743.4 0.8 copy.44
  745.5 0.8 copy.47
  746.3 0.8 copy.48
  (184 shorter events, 15.7 us)
Async XLA Ops:
  0.6 5.2 copy-start.3
  1.7 5.6 copy-start.50
  4.2 3.1 copy-start.52
  5.8 1.5 copy-start.54
  137.2 3.7 copy-start.18
  140.5 2.3 copy-start
  142.2 3.3 copy-start.33
  142.2 3.3 copy-start.35
  142.2 5.9 copy-start.16
  143.2 4.9 copy-start.25
  148.1 2.3 copy-start.56
  287.0 3.0 copy-start.1
  287.0 3.1 copy-start.19
  287.0 3.8 copy-start.57
  289.9 3.7 copy-start.37
  289.9 5.2 copy-start.13
  292.8 17.8 %copy-start.8 = (f32[512,1024]{1,0:T(8,128)}, f32[512,1024]{1,0:T(8,128)S(1)}, u32[]{:S(2)}) copy-start(f32[512,1024]{1,0:T(8,128)S(1)} %get-tuple-element.168) | copy-start | bytes 6291460
  293.6 1.6 copy-start.11
  295.1 2.6 copy-start.6
  295.2 4.3 copy-start.49
  297.8 2.6 collective-permute-start
  309.8 1.6 copy-start.59
  309.8 4.4 slice-start.2
  310.6 2.8 copy-start.26
  311.4 3.0 slice-start.3
  314.2 7.7 %copy-start.27 = (bf16[512,1024]{1,0:T(8,128)(2,1)}, bf16[512,1024]{1,0:T(8,128)(2,1)S(1)}, u32[]{:S(2)}) copy-start(bf16[512,1024]{1,0:T(8,128)(2,1)S(1)} %add_convert_fusion.1.refs_9_) | copy-start | bytes 3145732
  322.0 1.9 copy-start.29
  347.0 9.1 %copy-start.30 = (bf16[512,4096]{1,0:T(8,128)(2,1)}, bf16[512,4096]{1,0:T(8,128)(2,1)S(1)}, u32[]{:S(2)}) copy-start(bf16[512,4096]{1,0:T(8,128)(2,1)S(1)} %multiply_convert_fusion.1.refs_13_) | copy-start | bytes 12582916
  359.0 2.4 copy-start.21
  365.1 10.7 %collective-permute-start.1 = (f32[32,1024]{1,0:T(8,128)S(1)}, f32[32,1024]{1,0:T(8,128)S(1)}, u32[]{:S(2)}, u32[]{:S(2)}) collective-permute-start(f32[32,1024]{1,0:T(8,128)S(1)} %slice.616), channel_id=1, source_target_pairs={{1,0},{3,2},{5,4},{7,6},{9,8},{11,10},{13,12},{15,14},{17,16},{19,... | collective-permute-start | bytes 393224 | tf_op jit(solution)/shard_map/ppermute | solution.py:1102
  375.8 11.2 %copy-start.7 = (f32[512,1024]{1,0:T(8,128)S(1)}, f32[512,1024]{1,0:T(8,128)}, u32[]{:S(2)}) copy-start(f32[512,1024]{1,0:T(8,128)} %copy-done.6) | copy-start | bytes 6291460
  375.8 11.2 %copy-start.10 = (f32[512,1024]{1,0:T(8,128)S(1)}, f32[512,1024]{1,0:T(8,128)}, u32[]{:S(2)}) copy-start(f32[512,1024]{1,0:T(8,128)} %get-tuple-element.227) | copy-start | bytes 6291460
  386.9 3.3 copy-start.28
  387.0 2.0 copy-start.38
  388.9 1.3 copy-start.24
  388.9 2.0 copy-start.9
  388.9 2.6 copy-start.14
  391.5 2.0 copy-start.15
  393.5 2.1 copy-start.58
  395.7 2.3 copy-start.22
  544.4 8.4 %copy-start.36 = (bf16[1,4,2,2,64,1024]{5,4,3,2,1,0:T(8,128)(2,1)S(1)}, bf16[1,4,2,2,64,1024]{5,4,3,2,1,0:T(8,128)(2,1)}, u32[]{:S(2)}) copy-start(bf16[1,4,2,2,64,1024]{5,4,3,2,1,0:T(8,128)(2,1)} %copy-done.35) | copy-start | bytes 6291460
  552.8 2.7 copy-start.34
  552.8 2.7 copy-start.39
  555.5 1.6 copy-start.2
  555.5 2.2 copy-start.17
  555.5 2.5 copy-start.32
  557.9 3.1 copy-start.44
  561.5 15.3 %slice-start = ((s8[8388608]{0:T(1024)(128)(4,1)}), s8[4194304]{0:T(1024)(128)(4,1)S(1)}, s32[]{:S(2)}) async-start(s8[8388608]{0:T(1024)(128)(4,1)} %bitcast.336), calls=%async_computation | async-start | bytes 8388608
  566.0 10.8 %copy-start.23 = (bf16[512,1024]{1,0:T(8,128)(2,1)}, bf16[512,1024]{1,0:T(8,128)(2,1)S(1)}, u32[]{:S(2)}) copy-start(bf16[512,1024]{1,0:T(8,128)(2,1)S(1)} %get-tuple-element.153.refs_2_) | copy-start | bytes 3145732
  566.0 10.8 %copy-start.4 = (bf16[512,1024]{1,0:T(8,128)(2,1)S(1)}, bf16[512,1024]{1,0:T(8,128)(2,1)}, u32[]{:S(2)}) copy-start(bf16[512,1024]{1,0:T(8,128)(2,1)} %param.15) | copy-start | bytes 3145732
  566.0 10.8 %copy-start.51 = (f32[1,1024]{1,0:T(1,128)S(1)}, f32[1,1024]{1,0:T(1,128)}, u32[]{:S(2)}) copy-start(f32[1,1024]{1,0:T(1,128)} %copy-done.50) | copy-start | bytes 12292
  566.0 10.8 %copy-start.53 = (f32[512]{0:T(512)S(1)}, f32[512]{0:T(512)}, u32[]{:S(2)}) copy-start(f32[512]{0:T(512)} %copy-done.52) | copy-start | bytes 6148
  566.0 10.8 %copy-start.55 = (f32[512]{0:T(512)S(1)}, f32[512]{0:T(512)}, u32[]{:S(2)}) copy-start(f32[512]{0:T(512)} %copy-done.54) | copy-start | bytes 6148
  566.0 10.8 %slice-start.1 = ((s8[8388608]{0:T(1024)(128)(4,1)}), s8[4194304]{0:T(1024)(128)(4,1)S(1)}, s32[]{:S(2)}) async-start(s8[8388608]{0:T(1024)(128)(4,1)} %bitcast.336), calls=%async_computation.1 | async-start | bytes 8388608
  576.8 6.4 copy-start.31
  584.2 151.5 %copy-start.47 = (f32[64,512]{1,0:T(8,128)S(1)}, f32[64,512]{1,0:T(8,128)}, u32[]{:S(2)}) copy-start(f32[64,512]{1,0:T(8,128)} %get-tuple-element.76) | copy-start | bytes 393220
  584.2 151.5 %copy-start.48 = (f32[64,512]{1,0:T(8,128)S(1)}, f32[64,512]{1,0:T(8,128)}, u32[]{:S(2)}) copy-start(f32[64,512]{1,0:T(8,128)} %get-tuple-element.77) | copy-start | bytes 393220
  729.9 8.4 %copy-start.5 = (bf16[512,1024]{1,0:T(8,128)(2,1)S(1)}, bf16[512,1024]{1,0:T(8,128)(2,1)}, u32[]{:S(2)}) copy-start(bf16[512,1024]{1,0:T(8,128)(2,1)} %param.15) | copy-start | bytes 3145732
  738.3 4.3 copy-start.43
  738.3 5.1 copy-start.42
  742.6 1.6 copy-start.46
  742.6 2.3 copy-start.45
  742.6 2.9 copy-start.41
  742.6 3.7 copy-start.40
  (2 other events, 2.2 us)

commit v5 on v4

--- a/solution.py
+++ b/solution.py
@@ -670,17 +670,14 @@
                 yield remote(origin, self.bufs[stage - 1][color].at[step - 1], *sems)
 
     def add_tensor(self):
-        n_a, n_b, n_c = self.place.dims
-
-        def body(i, _):
-            at = (lax.div(i, n_b * n_c), lax.rem(lax.div(i, n_c), n_b), lax.rem(i, n_c))
-            total = self.held[at].astype(jnp.float32)
+        def body(a, _):
+            total = self.held[a].astype(jnp.float32)
             for step in range(1, self.place.n_tensor):
-                total = total + self.near[(step - 1,) + at].astype(jnp.float32)
-            self.held[at] = total.astype(jnp.bfloat16)
+                total = total + self.near[step - 1, a].astype(jnp.float32)
+            self.held[a] = total.astype(jnp.bfloat16)
             return 0
 
-        lax.fori_loop(0, n_a * n_b * n_c, body, 0)
+        lax.fori_loop(0, self.place.dims[0], body, 0)
 
     def add(self, stage):
         place, piece = self.place, self.piece
@@ -700,19 +697,15 @@
                 return at, total
 
             def body(i, _):
-                if len(left) == 2:
-                    size = place.dims[left[1]]
-                    at, total = total_at((lax.div(i, size), lax.rem(i, size)))
-                else:
-                    at, total = total_at((i,))
+                at, total = total_at((i, slice(None)))
                 self.held[at] = total.astype(jnp.bfloat16)
                 return 0
 
-            if left:
-                count = 1
-                for x in left:
-                    count *= place.dims[x]
-                lax.fori_loop(0, count, body, 0)
+            if len(left) == 2:
+                lax.fori_loop(0, place.dims[left[0]], body, 0)
+            elif left:
+                at, total = total_at((slice(None),))
+                self.held[at] = total.astype(jnp.bfloat16)
             else:
                 cols = slice(piece.first, piece.first + piece.width)
                 self.out[rows, cols] = total_at(())[1]

time: 757 us -> 750 us (level)
  no operation moved by 1% of the time
where the time goes in v5:
time: 750 us; the launch traced here: 741 us
  Pallas kernels  556 us (74%)
  matrix products  82.8 us (11%)
  other arithmetic  63.9 us (9%)
  local copies, waits for them, and re-layouts  31.3 us (4%)
    pallas_call x2, Pallas kernels, run_plan(): pl.pallas_call(functools.partial(plan_kernel, plan), out_shape=plan.out_s...  275 us
    pallas_call x1, Pallas kernels, attn_bwd(): pl.pallas_call(functools.partial(attn_bwd_kernel, plan), grid=(pairs,), i...  141 us
    pallas_call x1, Pallas kernels, attn_fwd(): pl.pallas_call(functools.partial(attn_fwd_kernel, plan), grid=(pairs,), i...  127 us
    dot_general x10, matrix products, dot_nn(): return jnp.dot(a, b, preferred_element_type=jnp.float32)  44.9 us
    dot_general x10, matrix products, dot_nt(): return lax.dot_general(a, b, NT, preferred_element_type=jnp.float32)  37.6 us
    convert_element_type x11, other arithmetic, low(): return value.astype(jnp.bfloat16)  25.6 us
    unnamed x136, local copies, waits for them, and re-layouts  15.2 us
  transfers between devices with their start and end apart: 2, of which 1 were waited for; matrix products, arithmetic and copies ran while one was open for 1% of the time, Pallas kernels for 0%

profile of v5, /device:TPU:0, one launch (start us, length us, event | category | flops | bytes accessed | tf_op | source)
XLA Modules:
  0.0 740.7 jit_solution(12095932304305126933)
XLA Ops:
  0.7 1.0 fusion.159
  1.7 1.0 fusion.160
  2.7 1.4 convert_reduce_fusion.1
  4.2 1.6 fusion.16
  5.9 1.5 fusion.10.refs_4_.refs_3_
  7.3 129.9 %gather_weights.1 = (bf16[1,4,2,2,64,4096]{5,4,3,2,1,0:T(8,128)(2,1)}, bf16[1,4,2,2,64,4096]{5,4,3,2,1,0:T(8,128)(2,1)}, bf16[3,4,2,2,64,1024]{5,4,3,2,1,0:T(8,1...) custom-call(bf16[1,64,2048]{2,1,0:T(8,128)(2,1)} %bitcast.190, ...), custom_call_target="tpu_custom_call" | custom-call | tf_op jit(solution)/shard_map/gather_weights/pallas_call | solution.py:902
  137.2 3.3 fusion.153
  140.9 1.2 fusion.154
  143.2 2.3 convolution_convert_fusion.1.refs_1_
  145.5 2.6 convolution_convert_fusion.2.refs_0_
  148.1 2.3 convolution_convert_fusion.3.refs_0_
  150.5 1.3 gather_fusion
  153.4 5.9 exchange_rows.1
  159.9 127.0 %attn_fwd.1 = (bf16[512,1024]{1,0:T(8,128)(2,1)}, f32[8,1024,1]{2,1,0:T(8,128)}, bf16[2,4,2,2,64,1024]{5,4,3,2,1,0:T(8,128)(2,1)}, bf16[1,4,2,2,64,1024]{5,4,3,2...) custom-call(bf16[512,1024]{1,0:T(8,128)(2,1)} %convolution_convert_fusion.3.refs_0_, ...), custom_call_target="tpu_custom_call" | custom-call | tf_op jit(solution)/shard_map/attn_fwd/pallas_call | solution.py:143
  287.0 2.9 fusion.155
  290.8 2.0 fusion.152
  293.6 1.5 add_divide_fusion.2
  295.2 2.6 fusion.161
  297.8 1.7 collective-permute-start
  299.6 0.8 collective-permute-done
  300.4 9.0 %fusion.151 = (f32[512]{0:T(512)S(1)}, f32[512,1024]{1,0:T(8,128)S(1)}) fusion(f32[512,1024]{1,0:T(8,128)S(1)} %get-tuple-element.226, f32[1024]{0:T(1024)S(1)} %bitcast.280, f32[32,1024]{1,0:T(8,128)S(1)} %collective-permute-done, f32[1024]{0:T(1024)S(1)} %bitcast.282, f32[1024]{0:T(1024)S(1)} %bitcast.224, f32[1024]{0:T(1024)S(1)} %bitcast.226, ...), kind=kLoop, calls=%fused_computation.360 | loop fusion | flops 48233984 | bytes 4454400 | tf_op jit(solution)/shard_map/reduce_sum | solution.py:1000
  309.8 0.8 multiply_convert_fusion.7.refs_14_
  311.4 2.0 fusion.150
  314.4 7.6 %multiply_convert_fusion.2 = (bf16[512,4096]{1,0:T(8,128)(2,1)S(1)}, f32[512,4096]{1,0:T(8,128)}) fusion(bf16[512,1024]{1,0:T(8,128)(2,1)S(1)} %add_convert_fusion.1.refs_9_, bf16[1024,4096]{1,0:T(8,128)(2,1)S(1)} %bitcast.343), kind=kOutput, calls=%fused_computation.61 | convolution fusion | flops 4305453056 | bytes 22020096 | tf_op jit(solution)/shard_map/dot_general | solution.py:34
  322.0 1.9 copy-done.29
  323.9 7.8 %fusion.149 = (f32[512]{0:T(512)S(1)}, f32[512,1024]{1,0:T(8,128)S(1)}, f32[]{:T(128)}) fusion(f32[512,1024]{1,0:T(8,128)S(1)} %get-tuple-element.164, bf16[512,4096]{1,0:T(8,128)(2,1)S(1)} %get-tuple-element.228.refs_12_, bf16[1024,4096]{1,0:T(8,128)(2,1)} %bitcast.344), kind=kOutput, calls=%fused_computation.358 | convolution fusion | flops 4297588224 | bytes 16779268 | tf_op jit(solution)/shard_map/dot_general | solution.py:26
  332.1 0.9 copy-done.12
  332.9 1.8 fusion.20
  335.5 1.0 copy-done.20
  336.4 10.6 %multiply_convert_fusion.1.refs_13_ = bf16[512,4096]{1,0:T(8,128)(2,1)S(1)} fusion(f32[512,4096]{1,0:T(8,128)} %get-tuple-element.229, bf16[512,1024]{1,0:T(8,128)(2,1)S(1)} %multiply_convert_fusion.6.refs_8_, bf16[1024,4096]{1,0:T(8,128)(2,1)} %bitcast.345), kind=kOutput, calls=%fused_computation.60 | convolution fusion | flops 4313841664 | bytes 22020096 | tf_op jit(solution)/shard_map/dot_general | solution.py:34
  347.1 9.1 %multiply_reduce_fusion.36 = (f32[1024]{0:T(1024)S(1)}, f32[512]{0:T(512)S(1)}, f32[512]{0:T(512)S(1)}, f32[1024]{0:T(1024)S(1)}, f32[512,1024]{1,0:T(8,128)S(1)}) fusion(f32[512,1024]{1,0:T(8,128)S(1)} %get-tuple-element.164, f32[512]{0:T(512)S(1)} %add_rsqrt_fusion.1, f32[512]{0:T(512)S(1)} %broadcast_multiply_fusion.13, f32[1024]{0:T(1024)S(1)} %bitcast.220, ...), kind=kOutput, calls=%fused_computation.263 | convolution fusion | flops 4299682816 | bytes 16797696 | tf_op jit(solution)/shard_map/dot_general | solution.py:26
  356.1 2.8 fusion.148
  359.0 2.4 multiply_reduce_fusion.37
  361.4 3.7 multiply_reduce_fusion.6
  365.1 1.3 collective-permute-start.1
  366.4 2.5 multiply_reduce_fusion.15
  368.9 2.5 multiply_reduce_fusion.24
  371.4 1.1 multiply_reduce_fusion.33
  372.4 3.3 stack.216
  375.8 11.2 %multiply_convert_fusion.5 = (bf16[512,1024]{1,0:T(8,128)(2,1)S(1)}, f32[512,1024]{1,0:T(8,128)S(1)}) fusion(f32[512,1024]{1,0:T(8,128)} %copy-done.6, f32[512,1024]{1,0:T(8,128)S(1)} %get-tuple-element.152, f32[1024]{0:T(1024)S(1)} %bitcast.281, f32[32,1024]{1,0:T(8,128)S(1)} %collective-permute-done.1, f32[1024]{0:T(1024)S(1)} %bitcast.283, ...), kind=kLoop, calls=%fused_computation.274 | loop fusion | flops 48758784 | bytes 7598080 | tf_op jit(solution)/shard_map/convert_element_type | solution.py:1016
  387.0 0.8 multiply_convert_fusion.4.refs_16_
  387.8 1.1 copy-done.38
  388.9 1.3 fusion.162
  391.5 2.0 multiply_reduce_fusion.38
  393.5 2.1 fusion.146
  395.7 2.3 convolution_convert_fusion.refs_3_
  398.0 140.9 %attn_bwd.1 = (bf16[512,1024]{1,0:T(8,128)(2,1)}, bf16[1024,1024]{1,0:T(8,128)(2,1)}, bf16[1024,1024]{1,0:T(8,128)(2,1)}, f32[512,128]{1,0:T(8,128)}, f32[64,204...) custom-call(bf16[512,1024]{1,0:T(8,128)(2,1)} %convolution_convert_fusion.3.ref, ...), custom_call_target="tpu_custom_call" | custom-call | tf_op jit(solution)/shard_map/attn_bwd/pallas_call | solution.py:262
  538.9 7.9 %return_rows.1 = (bf16[512,1024]{1,0:T(8,128)(2,1)}, bf16[512,1024]{1,0:T(8,128)(2,1)}) custom-call(bf16[1024,1024]{1,0:T(8,128)(2,1)} %get-tuple-element.60.refs_0_, bf16[1024,1024]{1,0:T(8,128)(2,1)} %get-tuple-element.61.refs_1_), custom_call_target="tpu_custom_call" | custom-call | tf_op jit(solution)/shard_map/return_rows/pallas_call | solution.py:987
  546.8 2.7 fusion.163
  549.5 1.3 fusion.164
  551.9 3.1 multiply_reduce_fusion.39
  555.5 4.5 multiply_convert_fusion.3
  560.0 10.8 %multiply_convert_fusion.refs_9_ = bf16[512,4096]{1,0:T(8,128)(2,1)S(1)} fusion(f32[512,4096]{1,0:T(8,128)} %get-tuple-element.65, bf16[512,1024]{1,0:T(8,128)(2,1)S(1)} %get-tuple-element.153.refs_2_, bf16[1024,4096]{1,0:T(8,128)(2,1)} %bitcast.339), kind=kOutput, calls=%fused_computation.59 | convolution fusion | flops 4313841664 | bytes 22020096 | tf_op jit(solution)/shard_map/dot_general | solution.py:34
  570.9 6.3 fusion.15
  578.2 144.9 %scatter_grads.1 = (f32[64,512]{1,0:T(8,128)}, f32[64,512]{1,0:T(8,128)}, f32[64,512]{1,0:T(8,128)}, f32[64,512]{1,0:T(8,128)}, f32[64,2048]{1,0:T(8,128)}, /*index=5*/f32[64,2048]{1,0:T(8,128)}, f32[56,1024]{1,0:T(8,128)}) custom-call(bf16[512,1024]{1,0:T(8,128)(2,1)} %copy-done.22, bf16[512,1024]{1,0:T(8,128)(2,1)} %copy-done.25, ...), custom_call_target="tpu_custom_call" | custom-call | tf_op jit(solution)/shard_map/scatter_grads/pallas_call | solution.py:902
  723.2 1.7 slice.551
  725.6 1.5 fusion.156
  727.1 1.2 sqrt_bitcast_fusion
  729.8 1.8 pad_maximum_fusion.2
  731.6 4.3 fusion.14
  735.9 0.8 copy.43
  736.7 0.8 copy.44
  738.9 0.8 copy.47
  739.6 0.8 copy.48
  (184 shorter events, 15.7 us)
Async XLA Ops:
  0.6 5.2 copy-start.3
  1.7 5.6 copy-start.50
  4.2 3.1 copy-start.52
  5.8 1.5 copy-start.54
  137.2 3.7 copy-start.18
  140.5 2.3 copy-start
  142.2 3.3 copy-start.33
  142.2 3.3 copy-start.35
  142.2 5.9 copy-start.16
  143.2 4.9 copy-start.25
  148.1 2.3 copy-start.56
  287.0 3.0 copy-start.1
  287.0 3.1 copy-start.19
  287.0 3.8 copy-start.57
  289.9 3.7 copy-start.37
  289.9 5.2 copy-start.13
  292.8 17.8 %copy-start.8 = (f32[512,1024]{1,0:T(8,128)}, f32[512,1024]{1,0:T(8,128)S(1)}, u32[]{:S(2)}) copy-start(f32[512,1024]{1,0:T(8,128)S(1)} %get-tuple-element.168) | copy-start | bytes 6291460
  293.6 1.6 copy-start.11
  295.1 2.6 copy-start.6
  295.2 4.3 copy-start.49
  297.8 2.6 collective-permute-start
  309.8 1.6 copy-start.59
  309.8 4.4 slice-start.2
  310.6 2.8 copy-start.26
  311.4 3.0 slice-start.3
  314.2 7.7 %copy-start.27 = (bf16[512,1024]{1,0:T(8,128)(2,1)}, bf16[512,1024]{1,0:T(8,128)(2,1)S(1)}, u32[]{:S(2)}) copy-start(bf16[512,1024]{1,0:T(8,128)(2,1)S(1)} %add_convert_fusion.1.refs_9_) | copy-start | bytes 3145732
  322.0 1.9 copy-start.29
  347.0 9.1 %copy-start.30 = (bf16[512,4096]{1,0:T(8,128)(2,1)}, bf16[512,4096]{1,0:T(8,128)(2,1)S(1)}, u32[]{:S(2)}) copy-start(bf16[512,4096]{1,0:T(8,128)(2,1)S(1)} %multiply_convert_fusion.1.refs_13_) | copy-start | bytes 12582916
  359.0 2.4 copy-start.21
  365.1 10.7 %collective-permute-start.1 = (f32[32,1024]{1,0:T(8,128)S(1)}, f32[32,1024]{1,0:T(8,128)S(1)}, u32[]{:S(2)}, u32[]{:S(2)}) collective-permute-start(f32[32,1024]{1,0:T(8,128)S(1)} %slice.616), channel_id=1, source_target_pairs={{1,0},{3,2},{5,4},{7,6},{9,8},{11,10},{13,12},{15,14},{17,16},{19,... | collective-permute-start | bytes 393224 | tf_op jit(solution)/shard_map/ppermute | solution.py:1095
  375.8 11.2 %copy-start.7 = (f32[512,1024]{1,0:T(8,128)S(1)}, f32[512,1024]{1,0:T(8,128)}, u32[]{:S(2)}) copy-start(f32[512,1024]{1,0:T(8,128)} %copy-done.6) | copy-start | bytes 6291460
  375.8 11.2 %copy-start.10 = (f32[512,1024]{1,0:T(8,128)S(1)}, f32[512,1024]{1,0:T(8,128)}, u32[]{:S(2)}) copy-start(f32[512,1024]{1,0:T(8,128)} %get-tuple-element.227) | copy-start | bytes 6291460
  386.9 3.3 copy-start.28
  387.0 2.0 copy-start.38
  388.9 1.3 copy-start.24
  388.9 2.0 copy-start.9
  388.9 2.6 copy-start.14
  391.5 2.0 copy-start.15
  393.5 2.1 copy-start.58
  395.7 2.3 copy-start.22
  538.9 7.9 %copy-start.36 = (bf16[1,4,2,2,64,1024]{5,4,3,2,1,0:T(8,128)(2,1)S(1)}, bf16[1,4,2,2,64,1024]{5,4,3,2,1,0:T(8,128)(2,1)}, u32[]{:S(2)}) copy-start(bf16[1,4,2,2,64,1024]{5,4,3,2,1,0:T(8,128)(2,1)} %copy-done.35) | copy-start | bytes 6291460
  546.7 2.7 copy-start.34
  546.8 2.7 copy-start.39
  549.4 1.6 copy-start.2
  549.5 2.2 copy-start.17
  549.5 2.5 copy-start.32
  551.9 3.1 copy-start.44
  555.5 15.3 %slice-start = ((s8[8388608]{0:T(1024)(128)(4,1)}), s8[4194304]{0:T(1024)(128)(4,1)S(1)}, s32[]{:S(2)}) async-start(s8[8388608]{0:T(1024)(128)(4,1)} %bitcast.336), calls=%async_computation | async-start | bytes 8388608
  560.0 10.8 %copy-start.23 = (bf16[512,1024]{1,0:T(8,128)(2,1)}, bf16[512,1024]{1,0:T(8,128)(2,1)S(1)}, u32[]{:S(2)}) copy-start(bf16[512,1024]{1,0:T(8,128)(2,1)S(1)} %get-tuple-element.153.refs_2_) | copy-start | bytes 3145732
  560.0 10.8 %copy-start.4 = (bf16[512,1024]{1,0:T(8,128)(2,1)S(1)}, bf16[512,1024]{1,0:T(8,128)(2,1)}, u32[]{:S(2)}) copy-start(bf16[512,1024]{1,0:T(8,128)(2,1)} %param.15) | copy-start | bytes 3145732
  560.0 10.8 %copy-start.51 = (f32[1,1024]{1,0:T(1,128)S(1)}, f32[1,1024]{1,0:T(1,128)}, u32[]{:S(2)}) copy-start(f32[1,1024]{1,0:T(1,128)} %copy-done.50) | copy-start | bytes 12292
  560.0 10.8 %copy-start.53 = (f32[512]{0:T(512)S(1)}, f32[512]{0:T(512)}, u32[]{:S(2)}) copy-start(f32[512]{0:T(512)} %copy-done.52) | copy-start | bytes 6148
  560.0 10.9 %copy-start.55 = (f32[512]{0:T(512)S(1)}, f32[512]{0:T(512)}, u32[]{:S(2)}) copy-start(f32[512]{0:T(512)} %copy-done.54) | copy-start | bytes 6148
  560.0 10.8 %slice-start.1 = ((s8[8388608]{0:T(1024)(128)(4,1)}), s8[4194304]{0:T(1024)(128)(4,1)S(1)}, s32[]{:S(2)}) async-start(s8[8388608]{0:T(1024)(128)(4,1)} %bitcast.336), calls=%async_computation.1 | async-start | bytes 8388608
  570.8 6.4 copy-start.31
  578.2 150.8 %copy-start.47 = (f32[64,512]{1,0:T(8,128)S(1)}, f32[64,512]{1,0:T(8,128)}, u32[]{:S(2)}) copy-start(f32[64,512]{1,0:T(8,128)} %get-tuple-element.76) | copy-start | bytes 393220
  578.2 150.8 %copy-start.48 = (f32[64,512]{1,0:T(8,128)S(1)}, f32[64,512]{1,0:T(8,128)}, u32[]{:S(2)}) copy-start(f32[64,512]{1,0:T(8,128)} %get-tuple-element.77) | copy-start | bytes 393220
  723.2 8.4 %copy-start.5 = (bf16[512,1024]{1,0:T(8,128)(2,1)S(1)}, bf16[512,1024]{1,0:T(8,128)(2,1)}, u32[]{:S(2)}) copy-start(bf16[512,1024]{1,0:T(8,128)(2,1)} %param.15) | copy-start | bytes 3145732
  731.6 4.3 copy-start.43
  731.6 5.1 copy-start.42
  735.9 1.6 copy-start.46
  735.9 2.3 copy-start.45
  735.9 2.9 copy-start.41
  735.9 3.7 copy-start.40
  (2 other events, 2.2 us)
